TPU v7x, 256 devices: a whole 4x4x8 slice. The times are simulated.
256 devices in a mesh: rows: 64 (over x, z, y_hi), cols: 4 (over y_lo, core).
Axes of the slice: x: 4, y: 4 (y_hi: 2, y_lo: 2; y = y_hi * 2 + y_lo), z: 8, core: 2. Of those that a mesh axis runs over, the one named last changes fastest.
Arguments:
- matrix: float32 [4096, 32, 2, 128], P('rows', 'cols'), may hold values from -54 to 54
- plan: int32 [2, 4, 256], replicated, may hold values from 0 to 255, as said below
Outputs:
- rotated: float32 [4096, 32, 2, 128], P('rows', 'cols')
Inputs may be any that keep to these rules, and one draw needn't show every extreme that they name: Each plan[s, r] pairs the 256 columns: partner of partner of i is i, and no column is its own partner.
All inputs are finite; a program needn't handle non-finite values.
Results may differ from a plain program's by a relative error of at most 0.0003.
Values sent between devices are 32-bit elements; how exact they have to be, the bound alone decides.
No kernel may reach another device: no remote copies, remote signals or barrier semaphores. Data moves between devices by JAX's collectives and lax.ppermute only.
A program may use at most 128 MiB of HBM per device.

v0:
```python
import jax
import jax.numpy as jnp
from jax import lax
from jax.sharding import Mesh
from jax.sharding import PartitionSpec as P

STEPS = 2
ROWS = ("rows_0", "rows_1", "rows_2")


def padded_to(lines, devices):
    spare = -len(lines) % devices
    return jnp.pad(lines, [(0, spare)] + [(0, 0)] * (lines.ndim - 1))


def sent_to_all(value, axis):
    copies = jnp.broadcast_to(value, (lax.axis_size(axis), *value.shape))
    return lax.all_to_all(copies, axis, split_axis=0, concat_axis=0, tiled=True)


def joined_along(blocks, dim):
    lengths = list(blocks.shape[1:])
    lengths[dim] *= blocks.shape[0]
    return jnp.moveaxis(blocks, 0, dim).reshape(lengths)


def whole_of(value, axes, dim):
    far, near = axes
    blocks = sent_to_all(sent_to_all(value, far), near)
    return joined_along(blocks.swapaxes(0, 1).reshape(-1, *value.shape), dim)


def split_up(value, dim, devices):
    lengths = value.shape
    blocks = value.reshape(*lengths[:dim], devices, lengths[dim] // devices, *lengths[dim + 1 :])
    return jnp.moveaxis(blocks, dim, 0)


def summed_on_arrival(value, axis, dim):
    blocks = split_up(value, dim, lax.axis_size(axis))
    arrived = lax.all_to_all(blocks, axis, split_axis=0, concat_axis=0, tiled=True)
    return arrived.sum(axis=0)


def summed_rows(value, axes, dim):
    far, near = axes
    own = summed_on_arrival(split_up(value, dim, lax.axis_size(far)), near, dim + 1)
    return jnp.sum(lax.all_to_all(own, far, 0, 0, tiled=True), axis=0)


def total_of(value, axes):
    lines = value.reshape(-1, value.shape[-1])
    padded = padded_to(lines, lax.axis_size(axes[0]) * lax.axis_size(axes[1]))
    whole = whole_of(summed_rows(padded, axes, 0), axes, 0)
    return lax.slice_in_dim(whole, 0, len(lines)).reshape(value.shape)


def passed_along(block, axis, distance):
    devices = range(lax.axis_size(axis))
    route = [((i - distance) % len(devices), i) for i in devices]
    return lax.ppermute(block, axis, route)


def diagonalize(grams, table):
    width = grams.shape[1]
    indices = jnp.arange(width, dtype=jnp.int32)
    rotation = jnp.broadcast_to(jnp.eye(width, dtype=jnp.float32), grams.shape)
    unit_matrix = jnp.eye(width, dtype=jnp.float32)
    for round_index in range(table.shape[0]):
        partner = table[round_index]
        onehot = (partner[:, None] == indices[None, :]).astype(jnp.float32)
        diagonal_now = jnp.diagonal(grams, axis1=1, axis2=2)
        partner_diag = jnp.einsum(
            "pj,ij->pi", diagonal_now, onehot, precision=lax.Precision.HIGHEST
        )
        partner_gram = jnp.sum(grams * onehot[None], axis=2)
        orient = jnp.where(indices < partner, 1.0, -1.0).astype(jnp.float32)
        spread = orient[None, :] * (partner_diag - diagonal_now)
        sign_part = jnp.where(spread >= 0.0, 1.0, -1.0).astype(jnp.float32)
        tangent = (
            sign_part
            * 2.0
            * partner_gram
            / (jnp.abs(spread) + jnp.sqrt(spread * spread + 4.0 * partner_gram * partner_gram))
        )
        cosine = 1.0 / jnp.sqrt(1.0 + tangent * tangent)
        sine_part = tangent * cosine
        off_part = jnp.swapaxes(onehot[None] * (-orient[None, :] * sine_part)[:, :, None], 1, 2)
        rot_now = cosine[:, :, None] * unit_matrix[None] + off_part
        product = jnp.einsum("pij,pjk->pik", grams, rot_now, precision=lax.Precision.HIGHEST)
        grams = jnp.einsum("pji,pjk->pik", rot_now, product, precision=lax.Precision.HIGHEST)
        rotation = jnp.einsum("pij,pjk->pik", rotation, rot_now, precision=lax.Precision.HIGHEST)
    return (grams, rotation)


def full_grams(columns):
    local_sum = jnp.einsum("mpi,mpj->pij", columns, columns, precision=lax.Precision.HIGHEST)
    return total_of(local_sum, (("rows_0", "rows_1"), "rows_2"))


def body(matrix, plan):
    rows_here, pair_here, halves, width = matrix.shape
    columns = matrix.reshape(rows_here, pair_here, halves * width)
    grams = full_grams(columns)
    for step_index in range(STEPS):
        grams, rotation = diagonalize(grams, plan[step_index])
        columns = jnp.einsum("mpi,pij->mpj", columns, rotation, precision=lax.Precision.HIGHEST)
        quarter = columns.reshape(rows_here, pair_here, halves, width)
        tops = quarter[:, :, 0, :]
        bottoms = quarter[:, :, 1, :]
        bottoms = passed_along(bottoms, "cols", 1)
        columns = jnp.stack([tops, bottoms], axis=2).reshape(rows_here, pair_here, halves * width)
        if step_index + 1 < STEPS:
            grams = full_grams(columns)
    return columns.reshape(matrix.shape)


def solution(mesh):
    split = Mesh(
        mesh.devices.reshape(4, 8, 2, mesh.shape["cols"]), ("rows_0", "rows_1", "rows_2", "cols")
    )
    in_specs = (P(ROWS, "cols", None, None), P())
    out_specs = P(ROWS, "cols", None, None)
    return jax.shard_map(body, mesh=split, in_specs=in_specs, out_specs=out_specs, check_vma=False)
```

profile of v0, /device:TPU:8, one launch (start us, length us, event | category | flops | bytes accessed | tf_op | source)
XLA Modules:
  0.0 514.7 jit_solution(14729319137601983196)
XLA Ops:
  0.0 1.5 reshape.372
  1.5 1.9 fusion.122
  3.6 29.7 %all_to_all.40 = f32[2,32,32,256]{3,2,1,0:T(8,128)S(1)} all-to-all(f32[2,32,32,256]{3,2,1,0:T(8,128)S(1)} %bitcast.132), channel_id=1, replica_groups=mesh['rows_0'=4,'rows_1'=8,'rows_2'=2,'cols'=4] {'rows_2'}, dimensions={0} | all-to-all | bytes 4194304 | tf_op jit(solution)/shard_map/all_to_all | solution.py:41
  33.3 1.3 reduce_sum.112
  34.5 38.9 %all_to_all.41 = f32[32,32,256]{2,1,0:T(8,128)S(1)} all-to-all(f32[32,32,256]{2,1,0:T(8,128)} %reduce_sum.112), channel_id=1, replica_groups=mesh['rows_0'=4,'rows_1'=8,'rows_2'=2,'cols'=4] {'rows_0','rows_1'}, dimensions={0} | all-to-all | bytes 2097152 | tf_op jit(solution)/shard_map/all_to_all | solution.py:48
  74.6 5.0 all-to-all-start.2
  83.5 23.7 %all-to-all-done.2 = f32[32,32,256]{2,1,0:T(8,128)S(1)} async-done(((f32[32,32,256]{2,1,0:T(8,128)}), f32[32,32,256]{2,1,0:T(8,128)S(1)}, u32[]{:S(2)}, u32[]{:S(2)}) %all-to-all-start.2) | async-done | bytes 1048608 | tf_op jit(solution)/shard_map/all_to_all | solution.py:18
  107.2 1.7 broadcast_in_dim.162
  108.9 3.9 all-to-all-start.3
  115.7 19.2 %all-to-all-done.3 = f32[2,32,32,256]{3,2,1,0:T(8,128)S(1)} async-done(((f32[2,32,32,256]{3,2,1,0:T(8,128)}), f32[2,32,32,256]{3,2,1,0:T(8,128)S(1)}, u32[]{:S(2)}, u32[]{:S(2)}) %all-to-all-start.3) | async-done | bytes 2097184 | tf_op jit(solution)/shard_map/all_to_all | solution.py:18
  134.9 1.3 mul.570
  136.8 1.7 copy.87
  138.6 16.3 %copy.88 = f32[8,256,256]{0,2,1:T(8,128)} copy(f32[8,256,256]{2,1,0:T(8,128)S(1)} %bitcast.127) | data formatting | bytes 4194304 | tf_op jit(solution)/shard_map/reshape;reshape;reshape | solution.py:55
  154.9 2.3 gather_fusion
  158.9 5.0 fusion.26
  164.0 3.5 fusion.27
  167.4 3.3 multiply_reduce_fusion.5
  170.8 16.5 %copy.91 = f32[8,256,256]{0,2,1:T(8,128)} copy(f32[8,256,256]{1,2,0:T(8,128)S(1)} %get-tuple-element.54) | data formatting | bytes 4194304 | tf_op jit(solution)/shard_map/pji,pjk->pik/dot_general | solution.py:91
  187.3 2.3 gather_fusion.1
  191.3 4.1 fusion.23
  195.4 3.3 multiply_reduce_fusion.4
  198.7 16.7 %copy.95 = f32[8,256,256]{0,2,1:T(8,128)} copy(f32[8,256,256]{1,2,0:T(8,128)S(1)} %get-tuple-element.56) | data formatting | bytes 4194304 | tf_op jit(solution)/shard_map/pji,pjk->pik/dot_general | solution.py:91
  215.4 2.3 gather_fusion.2
  219.4 4.1 fusion.20
  223.5 2.8 multiply_reduce_fusion.3
  226.3 16.5 %copy.99 = f32[8,256,256]{0,2,1:T(8,128)} copy(f32[8,256,256]{1,2,0:T(8,128)S(1)} %get-tuple-element.58) | data formatting | bytes 4194304 | tf_op jit(solution)/shard_map/pji,pjk->pik/dot_general | solution.py:91
  242.8 2.3 gather_fusion.3
  245.2 4.1 fusion.24
  249.4 2.5 fusion.21
  252.2 2.5 fusion.15
  254.7 1.6 convolution_bitcast_fusion.1
  257.2 5.8 %collective-permute-done = f32[64,8,128]{2,0,1:T(8,128)S(1)} collective-permute-done((f32[64,8,128]{2,0,1:T(8,128)S(1)}, f32[64,8,128]{2,0,1:T(8,128)S(1)}, u32[]{:S(2)}, u32[]{:S(2)}) %collective-permute-start) | collective-permute-done | bytes 262176 | tf_op jit(solution)/shard_map/ppermute | solution.py:61
  263.0 1.9 fusion.117
  265.2 28.3 %all_to_all.42 = f32[2,32,32,256]{3,2,1,0:T(8,128)S(1)} all-to-all(f32[2,32,32,256]{3,2,1,0:T(8,128)S(1)} %bitcast.134), channel_id=1, replica_groups=mesh['rows_0'=4,'rows_1'=8,'rows_2'=2,'cols'=4] {'rows_2'}, dimensions={0} | all-to-all | bytes 4194304 | tf_op jit(solution)/shard_map/all_to_all | solution.py:41
  293.8 35.1 %all_to_all.43 = f32[32,32,256]{2,1,0:T(8,128)S(1)} all-to-all(f32[32,32,256]{2,1,0:T(8,128)S(1)} %reduce_sum.119), channel_id=1, replica_groups=mesh['rows_0'=4,'rows_1'=8,'rows_2'=2,'cols'=4] {'rows_0','rows_1'}, dimensions={0} | all-to-all | bytes 2097152 | tf_op jit(solution)/shard_map/all_to_all | solution.py:48
  330.1 5.1 all-to-all-start.6
  338.3 22.9 %all-to-all-done.6 = f32[32,32,256]{2,1,0:T(8,128)S(1)} async-done(((f32[32,32,256]{2,1,0:T(8,128)}), f32[32,32,256]{2,1,0:T(8,128)S(1)}, u32[]{:S(2)}, u32[]{:S(2)}) %all-to-all-start.6) | async-done | bytes 1048608 | tf_op jit(solution)/shard_map/all_to_all | solution.py:18
  361.2 1.7 broadcast_in_dim.165
  362.9 5.0 all-to-all-start.7
  370.1 17.2 %all-to-all-done.7 = f32[2,32,32,256]{3,2,1,0:T(8,128)} async-done(((f32[2,32,32,256]{3,2,1,0:T(8,128)}), f32[2,32,32,256]{3,2,1,0:T(8,128)}, u32[]{:S(2)}, u32[]{:S(2)}) %all-to-all-start.7) | async-done | bytes 2097184 | tf_op jit(solution)/shard_map/all_to_all | solution.py:18
  387.3 1.7 copy.105
  389.0 16.3 %copy.106 = f32[8,256,256]{0,2,1:T(8,128)} copy(f32[8,256,256]{2,1,0:T(8,128)S(1)} %bitcast.125) | data formatting | bytes 4194304 | tf_op jit(solution)/shard_map/reshape;reshape;reshape | solution.py:55
  405.3 2.3 gather_fusion.4
  408.9 2.6 fusion
  411.5 1.4 reduce_sum.122
  414.0 4.0 fusion.13
  418.0 3.5 fusion.14
  421.5 2.8 multiply_reduce_fusion.2
  424.3 16.7 %copy.109 = f32[8,256,256]{0,2,1:T(8,128)} copy(f32[8,256,256]{1,2,0:T(8,128)S(1)} %get-tuple-element.60) | data formatting | bytes 4194304 | tf_op jit(solution)/shard_map/pji,pjk->pik/dot_general | solution.py:91
  441.0 2.3 gather_fusion.5
  443.7 4.1 fusion.10
  447.8 2.7 multiply_reduce_fusion.1
  450.6 16.5 %copy.113 = f32[8,256,256]{0,2,1:T(8,128)} copy(f32[8,256,256]{1,2,0:T(8,128)S(1)} %get-tuple-element.62) | data formatting | bytes 4194304 | tf_op jit(solution)/shard_map/pji,pjk->pik/dot_general | solution.py:91
  467.1 2.3 gather_fusion.6
  469.8 4.1 fusion.7
  473.8 2.7 multiply_reduce_fusion
  476.6 16.5 %copy.117 = f32[8,256,256]{0,2,1:T(8,128)} copy(f32[8,256,256]{1,2,0:T(8,128)S(1)} %get-tuple-element.64) | data formatting | bytes 4194304 | tf_op jit(solution)/shard_map/pji,pjk->pik/dot_general | solution.py:91
  493.1 2.3 gather_fusion.7
  495.5 4.1 fusion.11
  499.6 2.5 fusion.8
  502.4 2.5 fusion.2
  505.0 1.5 convolution_bitcast_fusion
  507.4 5.8 %collective-permute-done.1 = f32[64,8,128]{2,1,0:T(8,128)S(1)} collective-permute-done((f32[64,8,128]{2,1,0:T(8,128)S(1)}, f32[64,8,128]{2,1,0:T(8,128)S(1)}, u32[]{:S(2)}, u32[]{:S(2)}) %collective-permute-start.1) | collective-permute-done | bytes 262176 | tf_op jit(solution)/shard_map/ppermute | solution.py:61
  513.2 1.3 pad_maximum_fusion
  (133 shorter events, 26.3 us)
Async XLA Ops:
  73.4 6.2 %copy-start.29 = (s32[2,4,256]{2,1,0:T(4,128)S(1)}, s32[2,4,256]{2,1,0:T(4,128)}, u32[]{:S(2)}) copy-start(s32[2,4,256]{2,1,0:T(4,128)} %param.3) | copy-start | bytes 24580
  74.6 32.6 %all-to-all-start.2 = ((f32[32,32,256]{2,1,0:T(8,128)}), f32[32,32,256]{2,1,0:T(8,128)S(1)}, u32[]{:S(2)}, u32[]{:S(2)}) async-start(f32[32,32,256]{2,1,0:T(8,128)} %broadcast_in_dim.161), calls=%async_computation.2 | async-start | bytes 2097152 | tf_op jit(solution)/shard_map/all_to_all | solution.py:18
  80.2 28.7 %copy-start.27 = (s32[1,1,256]{2,1,0:T(1,128)}, s32[1,1,256]{2,1,0:T(1,128)S(1)}, u32[]{:S(2)}) copy-start(s32[1,1,256]{2,1,0:T(1,128)S(1)} %get-tuple-element.15) | copy-start | bytes 3076
  80.2 33.2 %copy-start.26 = (s32[1,1,256]{2,1,0:T(1,128)}, s32[1,1,256]{2,1,0:T(1,128)S(1)}, u32[]{:S(2)}) copy-start(s32[1,1,256]{2,1,0:T(1,128)S(1)} %get-tuple-element.14) | copy-start | bytes 3076
  80.2 34.0 %copy-start.24 = (s32[1,1,256]{2,1,0:T(1,128)}, s32[1,1,256]{2,1,0:T(1,128)S(1)}, u32[]{:S(2)}) copy-start(s32[1,1,256]{2,1,0:T(1,128)S(1)} %get-tuple-element.13) | copy-start | bytes 3076
  80.2 34.7 %copy-start.28 = (s32[1,1,256]{2,1,0:T(1,128)}, s32[1,1,256]{2,1,0:T(1,128)S(1)}, u32[]{:S(2)}) copy-start(s32[1,1,256]{2,1,0:T(1,128)S(1)} %get-tuple-element.16) | copy-start | bytes 3076
  108.9 26.0 %all-to-all-start.3 = ((f32[2,32,32,256]{3,2,1,0:T(8,128)}), f32[2,32,32,256]{3,2,1,0:T(8,128)S(1)}, u32[]{:S(2)}, u32[]{:S(2)}) async-start(f32[2,32,32,256]{3,2,1,0:T(8,128)} %broadcast_in_dim.162), calls=%async_computation.3 | async-start | bytes 4194304 | tf_op jit(solution)/shard_map/all_to_all | solution.py:18
  134.9 1.8 copy-start
  158.9 5.0 copy-start.1
  164.0 3.5 copy-start.11
  191.3 4.1 copy-start.13
  191.3 4.1 copy-start.9
  219.4 4.1 copy-start.15
  219.4 4.1 copy-start.17
  219.4 4.1 copy-start.7
  226.3 18.9 %copy-start.14 = (f32[8,256]{1,0:T(8,128)S(1)}, f32[8,256]{1,0:T(8,128)}, u32[]{:S(2)}) copy-start(f32[8,256]{1,0:T(8,128)} %copy-done.13) | copy-start | bytes 24580
  245.2 4.1 copy-start.16
  245.2 4.1 copy-start.18
  249.3 2.6 copy-start.25
  249.3 2.6 copy-start.30
  249.3 2.6 copy-start.31
  249.4 2.8 copy-start.6
  257.1 7.8 %copy-start.2 = (f32[64,8,1,128]{3,2,0,1:T(1,128)}, f32[64,8,1,128]{3,2,0,1:T(1,128)S(1)}, u32[]{:S(2)}) copy-start(f32[64,8,1,128]{3,2,0,1:T(1,128)S(1)} %get-tuple-element.7) | copy-start | bytes 786436
  257.1 5.9 %collective-permute-start = (f32[64,8,128]{2,0,1:T(8,128)S(1)}, f32[64,8,128]{2,0,1:T(8,128)S(1)}, u32[]{:S(2)}, u32[]{:S(2)}) collective-permute-start(f32[64,8,128]{2,0,1:T(8,128)S(1)} %bitcast.140), channel_id=1, source_target_pairs={{3,0},{0,1},{1,2},{2,3},{7,4},{4,5},{5,6},{6,7},{11,8},{8,9},{9,10... | collective-permute-start | bytes 786440 | tf_op jit(solution)/shard_map/ppermute | solution.py:61
  263.0 1.9 copy-start.4
  328.9 6.2 %copy-start.23 = (s32[1,1,256]{2,1,0:T(1,128)S(1)}, s32[1,1,256]{2,1,0:T(1,128)}, u32[]{:S(2)}) copy-start(s32[1,1,256]{2,1,0:T(1,128)} %get-tuple-element.17) | copy-start | bytes 3076
  328.9 6.8 %copy-start.21 = (s32[1,1,256]{2,1,0:T(1,128)S(1)}, s32[1,1,256]{2,1,0:T(1,128)}, u32[]{:S(2)}) copy-start(s32[1,1,256]{2,1,0:T(1,128)} %get-tuple-element.12) | copy-start | bytes 3076
  328.9 7.4 %copy-start.19 = (s32[1,1,256]{2,1,0:T(1,128)S(1)}, s32[1,1,256]{2,1,0:T(1,128)}, u32[]{:S(2)}) copy-start(s32[1,1,256]{2,1,0:T(1,128)} %get-tuple-element.18) | copy-start | bytes 3076
  330.1 31.2 %all-to-all-start.6 = ((f32[32,32,256]{2,1,0:T(8,128)}), f32[32,32,256]{2,1,0:T(8,128)S(1)}, u32[]{:S(2)}, u32[]{:S(2)}) async-start(f32[32,32,256]{2,1,0:T(8,128)} %broadcast_in_dim.164), calls=%async_computation.6 | async-start | bytes 2097152 | tf_op jit(solution)/shard_map/all_to_all | solution.py:18
  362.9 24.4 %all-to-all-start.7 = ((f32[2,32,32,256]{3,2,1,0:T(8,128)}), f32[2,32,32,256]{3,2,1,0:T(8,128)}, u32[]{:S(2)}, u32[]{:S(2)}) async-start(f32[2,32,32,256]{3,2,1,0:T(8,128)} %broadcast_in_dim.165), calls=%async_computation.7 | async-start | bytes 4194304 | tf_op jit(solution)/shard_map/all_to_all | solution.py:18
  418.0 3.5 copy-start.12
  424.3 19.1 %copy-start.22 = (s32[1,1,256]{2,1,0:T(1,128)S(1)}, s32[1,1,256]{2,1,0:T(1,128)}, u32[]{:S(2)}) copy-start(s32[1,1,256]{2,1,0:T(1,128)} %get-tuple-element.12) | copy-start | bytes 3076
  424.3 19.1 %copy-start.36 = (f32[256]{0:T(256)S(1)}, f32[256]{0:T(256)}, u32[]{:S(2)}) copy-start(f32[256]{0:T(256)} %get-tuple-element.37) | copy-start | bytes 3076
  424.3 19.1 %copy-start.37 = (f32[256]{0:T(256)S(1)}, f32[256]{0:T(256)}, u32[]{:S(2)}) copy-start(f32[256]{0:T(256)} %get-tuple-element.38) | copy-start | bytes 3076
  443.7 4.1 copy-start.10
  450.5 18.9 %copy-start.20 = (s32[1,1,256]{2,1,0:T(1,128)S(1)}, s32[1,1,256]{2,1,0:T(1,128)}, u32[]{:S(2)}) copy-start(s32[1,1,256]{2,1,0:T(1,128)} %get-tuple-element.18) | copy-start | bytes 3076
  450.5 18.9 %copy-start.34 = (f32[256]{0:T(256)S(1)}, f32[256]{0:T(256)}, u32[]{:S(2)}) copy-start(f32[256]{0:T(256)} %get-tuple-element.35) | copy-start | bytes 3076
  450.6 18.9 %copy-start.35 = (f32[256]{0:T(256)S(1)}, f32[256]{0:T(256)}, u32[]{:S(2)}) copy-start(f32[256]{0:T(256)} %get-tuple-element.36) | copy-start | bytes 3076
  469.7 4.1 copy-start.8
  499.6 2.5 copy-start.32
  499.6 2.5 copy-start.33
  502.4 2.5 copy-start.3
  502.4 2.5 copy-start.5
  507.3 5.9 %collective-permute-start.1 = (f32[64,8,128]{2,1,0:T(8,128)S(1)}, f32[64,8,128]{2,1,0:T(8,128)S(1)}, u32[]{:S(2)}, u32[]{:S(2)}) collective-permute-start(f32[64,8,128]{2,1,0:T(8,128)S(1)} %bitcast.139), channel_id=1, source_target_pairs={{3,0},{0,1},{1,2},{2,3},{7,4},{4,5},{5,6},{6,7},{11,8},{8,9},{9,10... | collective-permute-start | bytes 786440 | tf_op jit(solution)/shard_map/ppermute | solution.py:61
where the time goes:
time: 522 us; the launch traced here: 515 us
  local copies, waits for them, and re-layouts  170 us (33%)
  blocking collectives  132 us (25%)
  waiting for transfers between devices  94.6 us (18%)
  matrix products  80.2 us (15%)
  starting transfers between devices  19.2 us (4%)
  other arithmetic  17.6 us (3%)
    dot_general x6, local copies, waits for them, and re-layouts, diagonalize(): jnp.einsum('pji,pjk->pik', rot_now, product, precision=lax.Precision.HIGH...  99.4 us
    all_to_all x4, waiting for transfers between devices, sent_to_all(): return lax.all_to_all(copies, axis, split_axis=0, concat_axis=0, tiled=True)  83 us
    all_to_all x2, blocking collectives, summed_rows(): return jnp.sum(lax.all_to_all(own, far, 0, 0, tiled=True), axis=0)  74 us
    all_to_all x2, blocking collectives, summed_on_arrival(): lax.all_to_all(blocks, axis, split_axis=0, concat_axis=0, tiled=True)  58 us
    another operation x2, local copies, waits for them, and re-layouts, total_of(): return lax.slice_in_dim(whole, 0, len(lines)).reshape(value.shape)  32.6 us
    dot_general x6, matrix products, diagonalize(): jnp.einsum('pij,pjk->pik', grams, rot_now, precision=lax.Precision.HIGHEST)  25.3 us
    dot_general x8, matrix products, diagonalize(): jnp.einsum('pij,pjk->pik', rotation, rot_now, precision=lax.Precision.HIG...  25.1 us
    gather x16, local copies, waits for them, and re-layouts, diagonalize(): diagonal_now = jnp.diagonal(grams, axis1=1, axis2=2)  20.9 us
  transfers between devices with their start and end apart: 6, of which 6 were waited for; matrix products, arithmetic and copies ran while one was open for 2% of the time, Pallas kernels for 0%

commit v1 on v0

v1 whole, which is shorter than its diff:
```python
import functools

import jax
import jax.numpy as jnp
from jax import lax
from jax.experimental import pallas as pl
from jax.experimental.pallas import tpu as pltpu
from jax.sharding import Mesh
from jax.sharding import PartitionSpec as P

STEPS = 2
ROWS = ("x", "z", "yh")
OWNERS = ("x", "yh")
SUMMED = "z"
LINES = 16
CHUNK = 128
F32 = jnp.float32
BF16 = jnp.bfloat16


def one_hot(partner):
    width = partner.shape[1]
    return lax.broadcasted_iota(jnp.int32, (width, width), 0) == partner


def pieces(value):
    high = value.astype(BF16)
    rest = value - high.astype(F32)
    middle = rest.astype(BF16)
    return high, middle, (rest - middle.astype(F32)).astype(BF16)


def permuted(value, table):
    return sum(jnp.dot(part, table, preferred_element_type=F32) for part in pieces(value))


def dot_lines(load, rows, first, second):
    width = first.shape[1]
    table_1 = one_hot(first).astype(BF16)
    table_2 = one_hot(second).astype(BF16)
    total = [jnp.zeros((8, width), F32) for _ in range(10)]
    for start in range(0, rows, CHUNK):
        own = load(start)
        other = permuted(own, table_1)
        own_2 = permuted(own, table_2)
        other_2 = permuted(other, table_2)
        products = (
            own * own,
            other * other,
            own * other,
            own * own_2,
            own * other_2,
            other * own_2,
            other * other_2,
            own_2 * own_2,
            other_2 * other_2,
            own_2 * other_2,
        )
        for i, product in enumerate(products):
            total[i] = total[i] + product.reshape(CHUNK // 8, 8, width).sum(axis=0)
    return [line.sum(axis=0, keepdims=True) for line in total]


def angle(orient, own, other, cross):
    spread = orient * (other - own)
    sign = jnp.where(spread >= 0.0, 1.0, -1.0)
    tangent = sign * 2.0 * cross / (jnp.abs(spread) + jnp.sqrt(spread * spread + 4.0 * cross * cross))
    cosine = 1.0 / jnp.sqrt(1.0 + tangent * tangent)
    return cosine, -orient * (tangent * cosine)


def two_rounds(lines, first, second):
    width = first.shape[1]
    own, other, cross, a, b, c, d, own_2, other_2, cross_2 = (lines[i : i + 1] for i in range(10))
    indices = lax.broadcasted_iota(jnp.int32, (1, width), 1)
    table_2 = one_hot(second)
    wide = jnp.broadcast_to(first.astype(F32).astype(BF16), (16, width))
    far = jnp.dot(wide, table_2.astype(BF16), preferred_element_type=F32)[:1].astype(jnp.int32)
    cos, sin = angle(jnp.where(indices < first, 1.0, -1.0), own, other, cross)
    cos_2, sin_2 = angle(jnp.where(second < far, 1.0, -1.0), own_2, other_2, cross_2)
    diag = cos * cos * own + 2.0 * cos * sin * cross + sin * sin * other
    diag_2 = cos_2 * cos_2 * own_2 + 2.0 * cos_2 * sin_2 * cross_2 + sin_2 * sin_2 * other_2
    joint = cos * cos_2 * a + cos * sin_2 * b + sin * cos_2 * c + sin * sin_2 * d
    cos_b, sin_b = angle(jnp.where(indices < second, 1.0, -1.0), diag, diag_2, joint)
    zero = jnp.zeros((width, width), F32)
    rotation = jnp.where(one_hot(indices), cos_b * cos, zero)
    rotation += jnp.where(one_hot(first), cos_b * sin, zero)
    rotation += jnp.where(table_2, sin_b * cos_2, zero)
    rotation += jnp.where(one_hot(far), sin_b * sin_2, zero)
    return rotation


def write_lines(lines, out_ref):
    lines = lines + [jnp.zeros_like(lines[0])] * (LINES - len(lines))
    block = jnp.concatenate(lines, axis=0)
    for i in range(out_ref.shape[0]):
        out_ref[i] = block


def plan_lines(plan_ref, number):
    return plan_ref[2 * number : 2 * number + 1], plan_ref[2 * number + 1 : 2 * number + 2]


def sort_kernel(in_ref, out_ref):
    rows, owners = out_ref.shape[1], out_ref.shape[0]
    for i in range(owners):
        for half in range(2):
            out_ref[i, :, half * 128 : half * 128 + 128] = in_ref[pl.ds(2 * i + half, rows, 2 * owners), :]


def unsort_kernel(in_ref, out_ref):
    rows, owners = in_ref.shape[1], in_ref.shape[0]
    for i in range(owners):
        for half in range(2):
            out_ref[pl.ds(2 * i + half, rows, 2 * owners), :] = in_ref[i, :, half * 128 : half * 128 + 128]


def first_kernel(number, plan_ref, x_ref, out_ref):
    lines = dot_lines(lambda start: x_ref[start : start + CHUNK], x_ref.shape[0], *plan_lines(plan_ref, number))
    write_lines(lines, out_ref)


def joined_kernel(number, plan_ref, top_ref, bottom_ref, out_ref, x_ref):
    width = top_ref.shape[1]
    x_ref[:, :width] = top_ref[...]
    x_ref[:, width:] = bottom_ref[...]
    lines = dot_lines(lambda start: x_ref[start : start + CHUNK], x_ref.shape[0], *plan_lines(plan_ref, number))
    write_lines(lines, out_ref)


def rotated(number, plan_ref, part_ref, x_ref):
    lines = jnp.sum(part_ref[...], axis=0)
    rotation = two_rounds(lines, *plan_lines(plan_ref, number))
    return jnp.dot(x_ref[...], rotation, precision=lax.Precision.HIGHEST, preferred_element_type=F32)


def middle_kernel(number, plan_ref, part_ref, x_ref, out_ref, y_ref):
    y_ref[...] = rotated(number, plan_ref, part_ref, x_ref)
    lines = dot_lines(lambda start: y_ref[start : start + CHUNK], y_ref.shape[0], *plan_lines(plan_ref, number + 1))
    write_lines(lines, out_ref)


def last_kernel(number, plan_ref, part_ref, x_ref, top_ref, bottom_ref):
    width = top_ref.shape[1]
    result = rotated(number, plan_ref, part_ref, x_ref)
    top_ref[...] = result[:, :width]
    bottom_ref[...] = result[:, width:]


def call(kernel, outs, *args):
    shapes = [jax.ShapeDtypeStruct(shape, F32) for shape in outs]
    single = len(shapes) == 1
    return pl.pallas_call(kernel, out_shape=shapes[0] if single else shapes)(*args)


def exchanged(value, axis):
    return lax.all_to_all(value, axis, split_axis=0, concat_axis=0, tiled=True)


def passed_along(block, axis, distance):
    devices = range(lax.axis_size(axis))
    route = [((i - distance) % len(devices), i) for i in devices]
    return lax.ppermute(block, axis, route)


def body(matrix, plan):
    rows, owners, halves, width = matrix.shape
    peers = lax.axis_size(SUMMED)
    flat = (rows * owners, halves * width)
    half = (rows * owners, width)
    sent = (peers, LINES, halves * width)
    tables = plan.reshape(-1, plan.shape[-1])
    lines = matrix.reshape(rows * owners * halves, width)
    x = exchanged(call(sort_kernel, [(owners, rows, halves * width)], lines), OWNERS).reshape(flat)
    part = call(functools.partial(first_kernel, 0), [sent], tables, x)
    for step in range(STEPS):
        part, x = call(
            functools.partial(middle_kernel, 2 * step), [sent, flat], tables, exchanged(part, SUMMED), x
        )
        top, bottom = call(
            functools.partial(last_kernel, 2 * step + 1), [half, half], tables, exchanged(part, SUMMED), x
        )
        bottom = passed_along(bottom, "cols", 1)
        if step + 1 < STEPS:
            part, x = call(functools.partial(joined_kernel, 2 * step + 2), [sent, flat], tables, top, bottom)
    x = jnp.concatenate([top, bottom], axis=1).reshape(owners, rows, halves * width)
    return call(unsort_kernel, [lines.shape], exchanged(x, OWNERS)).reshape(matrix.shape)


def solution(mesh):
    split = Mesh(mesh.devices.reshape(4, 8, 2, mesh.shape["cols"]), ("x", "z", "yh", "cols"))
    in_specs = (P(ROWS, "cols", None, None), P())
    out_specs = P(ROWS, "cols", None, None)
    return jax.shard_map(body, mesh=split, in_specs=in_specs, out_specs=out_specs, check_vma=False)
```

time: 522 us -> 127 us (0.24); the launches traced: 515 us -> 126 us
  local copies, waits for them, and re-layouts: 170 us -> 2.12 us
  matrix products: 80.2 us -> 0 us
  waiting for transfers between devices: 94.6 us -> 22.3 us
  blocking collectives: 132 us -> 70.6 us
  Pallas kernels: 0 us -> 23.9 us
  other arithmetic: 17.6 us -> 1.02 us
  starting transfers between devices: 19.2 us -> 6.17 us
    dot_general x6 -> x0, local copies, waits for them, and re-layouts: 99.4 us -> none  [diagonalize(): jnp.einsum('pji,pjk->pik', rot_now, product, precision=lax.Precision.HIGH...]
    dot_general x32 -> x0, matrix products: 80.2 us -> none  [the longest x6 25.3 us: diagonalize(): jnp.einsum('pij,pjk->pik', grams, rot_now, precision=lax.Precision.HIGHEST)]
    all_to_all x4 -> x1, waiting for transfers between devices: 83 us -> 10.3 us  [exchanged(): return lax.all_to_all(value, axis, split_axis=0, concat_axis=0, tiled=True)]
    all_to_all x4 -> x5, blocking collectives: 132 us -> 70.6 us  [exchanged(): return lax.all_to_all(value, axis, split_axis=0, concat_axis=0, tiled=True)]
    another operation x4 -> x0, local copies, waits for them, and re-layouts: 33.1 us -> none  [the longest x2 32.6 us: total_of(): return lax.slice_in_dim(whole, 0, len(lines)).reshape(value.shape)]
    pallas_call x0 -> x8, Pallas kernels: none -> 23.9 us  [call(): pl.pallas_call(kernel, out_shape=shapes[0] if single else shapes)(*args)]
    gather x16 -> x0, local copies, waits for them, and re-layouts: 20.9 us -> none  [diagonalize(): diagonal_now = jnp.diagonal(grams, axis1=1, axis2=2)]
    all_to_all x4 -> x1, starting transfers between devices: 19 us -> 6.16 us  [exchanged(): return lax.all_to_all(value, axis, split_axis=0, concat_axis=0, tiled=True)]
  transfers between devices with their start and end apart: 6 -> 3, of which waited for: 6 -> 3; matrix products, arithmetic and copies ran while one was open for 2% -> 0% of each run, Pallas kernels for 0% -> 0%
where the time goes in v1:
time: 127 us; the launch traced here: 126 us
  blocking collectives  70.6 us (56%)
  Pallas kernels  23.9 us (19%)
  waiting for transfers between devices  22.3 us (18%)
  starting transfers between devices  6.17 us (5%)
  local copies, waits for them, and re-layouts  2.12 us (2%)
    all_to_all x5, blocking collectives, exchanged(): return lax.all_to_all(value, axis, split_axis=0, concat_axis=0, tiled=True)  70.6 us
    pallas_call x8, Pallas kernels, call(): pl.pallas_call(kernel, out_shape=shapes[0] if single else shapes)(*args)  23.9 us
    ppermute x2, waiting for transfers between devices, passed_along(): return lax.ppermute(block, axis, route)  12 us
    all_to_all x1, waiting for transfers between devices, exchanged(): return lax.all_to_all(value, axis, split_axis=0, concat_axis=0, tiled=True)  10.3 us
    all_to_all x1, starting transfers between devices, exchanged(): return lax.all_to_all(value, axis, split_axis=0, concat_axis=0, tiled=True)  6.16 us
  transfers between devices with their start and end apart: 3, of which 3 were waited for; matrix products, arithmetic and copies ran while one was open for 0% of the time, Pallas kernels for 0%

profile of v1, /device:TPU:8, one launch (start us, length us, event | category | flops | bytes accessed | tf_op | source)
XLA Modules:
  0.0 126.1 jit_solution(18056427321999514564)
XLA Ops:
  0.0 2.0 %shard_map.28 = f32[8,64,256]{2,1,0:T(8,128)} custom-call(f32[1024,128]{1,0:T(8,128)} %bitcast.7), custom_call_target="tpu_custom_call" | custom-call | tf_op jit(solution)/shard_map/pallas_call | solution.py:153
  2.0 0.0 copy-start.2
  2.0 6.2 %all-to-all-start = ((f32[8,64,256]{2,1,0:T(8,128)}), f32[8,64,256]{2,1,0:T(8,128)S(1)}, u32[]{:S(2)}, u32[]{:S(2)}) async-start(f32[8,64,256]{2,1,0:T(8,128)} %shard_map.28), calls=%async_computation | async-start | bytes 1048576 | tf_op jit(solution)/shard_map/all_to_all | solution.py:157
  8.2 0.0 copy-done.2
  8.2 0.6 reshape.15.plan_ref
  8.8 10.3 %all-to-all-done = f32[8,64,256]{2,1,0:T(8,128)S(1)} async-done(((f32[8,64,256]{2,1,0:T(8,128)}), f32[8,64,256]{2,1,0:T(8,128)S(1)}, u32[]{:S(2)}, u32[]{:S(2)}) %all-to-all-start) | async-done | bytes 524320 | tf_op jit(solution)/shard_map/all_to_all | solution.py:157
  19.0 0.0 copy-start
  19.0 0.8 copy-done
  19.8 2.8 %shard_map.29 = f32[8,16,256]{2,1,0:T(8,128)} custom-call(s32[8,256]{1,0:T(8,128)} %reshape.15.plan_ref, f32[512,256]{1,0:T(8,128)} %bitcast.4), custom_call_target="tpu_custom_call" | custom-call | tf_op jit(solution)/shard_map/pallas_call | solution.py:153
  22.6 17.6 %all_to_all.30.part_ref = f32[8,16,256]{2,1,0:T(8,128)} all-to-all(f32[8,16,256]{2,1,0:T(8,128)} %shard_map.29), channel_id=1, replica_groups=mesh['x'=4,'z'=8,'yh'=2,'cols'=4] {'z'}, dimensions={0} | all-to-all | bytes 262144 | tf_op jit(solution)/shard_map/all_to_all | solution.py:157
  40.3 4.2 %shard_map.30 = (f32[8,16,256]{2,1,0:T(8,128)}, f32[512,256]{1,0:T(8,128)}) custom-call(s32[8,256]{1,0:T(8,128)} %reshape.15.plan_ref, f32[8,16,256]{2,1,0:T(8,128)} %all_to_all.30.part_ref, f32[512,256]{1,0:T(8,128)} %bitcast.5), custom_call_target="tpu_custom_call" | custom-call | tf_op jit(solution)/shard_map/pallas_call | solution.py:153
  44.5 13.0 %all_to_all.31.part_ref = f32[8,16,256]{2,1,0:T(8,128)} all-to-all(f32[8,16,256]{2,1,0:T(8,128)} %get-tuple-element.15), channel_id=1, replica_groups=mesh['x'=4,'z'=8,'yh'=2,'cols'=4] {'z'}, dimensions={0} | all-to-all | bytes 262144 | tf_op jit(solution)/shard_map/all_to_all | solution.py:157
  57.6 2.9 %shard_map.31 = (f32[512,128]{1,0:T(8,128)}, f32[512,128]{1,0:T(8,128)}) custom-call(s32[8,256]{1,0:T(8,128)} %reshape.15.plan_ref, f32[8,16,256]{2,1,0:T(8,128)} %all_to_all.31.part_ref, f32[512,256]{1,0:T(8,128)} %get-tuple-element.16.x_ref), custom_call_target="tpu_custom_call" | custom-call | tf_op jit(solution)/shard_map/pallas_call | solution.py:153
  60.4 0.0 collective-permute-start
  60.4 6.0 %collective-permute-done.bottom_ref = f32[512,128]{1,0:T(8,128)S(1)} collective-permute-done((f32[512,128]{1,0:T(8,128)}, f32[512,128]{1,0:T(8,128)S(1)}, u32[]{:S(2)}, u32[]{:S(2)}) %collective-permute-start) | collective-permute-done | bytes 262176 | tf_op jit(solution)/shard_map/ppermute | solution.py:163
  66.4 0.0 copy-start.1
  66.4 0.7 copy-done.1
  67.2 2.8 %shard_map.32 = (f32[8,16,256]{2,1,0:T(8,128)}, f32[512,256]{1,0:T(8,128)}) custom-call(s32[8,256]{1,0:T(8,128)} %reshape.15.plan_ref, f32[512,128]{1,0:T(8,128)} %get-tuple-element.17.top_ref, f32[512,128]{1,0:T(8,128)} %copy-done.1), custom_call_target="tpu_custom_call" | custom-call | tf_op jit(solution)/shard_map/pallas_call | solution.py:153
  70.0 13.1 %all_to_all.32.part_ref = f32[8,16,256]{2,1,0:T(8,128)} all-to-all(f32[8,16,256]{2,1,0:T(8,128)} %get-tuple-element.19), channel_id=1, replica_groups=mesh['x'=4,'z'=8,'yh'=2,'cols'=4] {'z'}, dimensions={0} | all-to-all | bytes 262144 | tf_op jit(solution)/shard_map/all_to_all | solution.py:157
  83.0 4.2 %shard_map.33 = (f32[8,16,256]{2,1,0:T(8,128)}, f32[512,256]{1,0:T(8,128)}) custom-call(s32[8,256]{1,0:T(8,128)} %reshape.15.plan_ref, f32[8,16,256]{2,1,0:T(8,128)} %all_to_all.32.part_ref, f32[512,256]{1,0:T(8,128)} %get-tuple-element.20.x_ref), custom_call_target="tpu_custom_call" | custom-call | tf_op jit(solution)/shard_map/pallas_call | solution.py:153
  87.3 13.1 %all_to_all.33.part_ref = f32[8,16,256]{2,1,0:T(8,128)} all-to-all(f32[8,16,256]{2,1,0:T(8,128)} %get-tuple-element.21), channel_id=1, replica_groups=mesh['x'=4,'z'=8,'yh'=2,'cols'=4] {'z'}, dimensions={0} | all-to-all | bytes 262144 | tf_op jit(solution)/shard_map/all_to_all | solution.py:157
  100.3 2.9 %shard_map.34 = (f32[512,128]{1,0:T(8,128)}, f32[512,128]{1,0:T(8,128)}) custom-call(s32[8,256]{1,0:T(8,128)} %reshape.15.plan_ref, f32[8,16,256]{2,1,0:T(8,128)} %all_to_all.33.part_ref, f32[512,256]{1,0:T(8,128)} %get-tuple-element.22.x_ref), custom_call_target="tpu_custom_call" | custom-call | tf_op jit(solution)/shard_map/pallas_call | solution.py:153
  103.2 0.0 collective-permute-start.1
  103.2 6.0 %collective-permute-done.1 = f32[512,128]{1,0:T(8,128)S(1)} collective-permute-done((f32[512,128]{1,0:T(8,128)}, f32[512,128]{1,0:T(8,128)S(1)}, u32[]{:S(2)}, u32[]{:S(2)}) %collective-permute-start.1) | collective-permute-done | bytes 262176 | tf_op jit(solution)/shard_map/ppermute | solution.py:163
  109.2 1.0 pad_maximum_fusion
  110.2 13.8 %all_to_all.34.in_ref = f32[8,64,256]{2,1,0:T(8,128)} all-to-all(f32[8,64,256]{2,1,0:T(8,128)S(1)} %bitcast.6), channel_id=1, replica_groups=mesh['x'=4,'z'=8,'yh'=2,'cols'=4] {'x','yh'}, dimensions={0} | all-to-all | bytes 1048576 | tf_op jit(solution)/shard_map/all_to_all | solution.py:157
  124.0 2.1 %shard_map.35 = f32[1024,128]{1,0:T(8,128)} custom-call(f32[8,64,256]{2,1,0:T(8,128)} %all_to_all.34.in_ref), custom_call_target="tpu_custom_call" | custom-call | tf_op jit(solution)/shard_map/pallas_call | solution.py:153
Async XLA Ops:
  2.0 6.2 %copy-start.2 = (s32[2,4,256]{2,1,0:T(4,128)S(1)}, s32[2,4,256]{2,1,0:T(4,128)}, u32[]{:S(2)}) copy-start(s32[2,4,256]{2,1,0:T(4,128)} %param.3) | copy-start | bytes 24580
  2.0 17.0 %all-to-all-start = ((f32[8,64,256]{2,1,0:T(8,128)}), f32[8,64,256]{2,1,0:T(8,128)S(1)}, u32[]{:S(2)}, u32[]{:S(2)}) async-start(f32[8,64,256]{2,1,0:T(8,128)} %shard_map.28), calls=%async_computation | async-start | bytes 1048576 | tf_op jit(solution)/shard_map/all_to_all | solution.py:157
  19.0 0.8 copy-start
  60.4 6.0 %collective-permute-start = (f32[512,128]{1,0:T(8,128)}, f32[512,128]{1,0:T(8,128)S(1)}, u32[]{:S(2)}, u32[]{:S(2)}) collective-permute-start(f32[512,128]{1,0:T(8,128)} %get-tuple-element.18), channel_id=1, source_target_pairs={{3,0},{0,1},{1,2},{2,3},{7,4},{4,5},{5,6},{6,7},{11,8},{8,9},{9,10... | collective-permute-start | bytes 786440 | tf_op jit(solution)/shard_map/ppermute | solution.py:163
  66.4 0.7 copy-start.1
  103.2 6.0 %collective-permute-start.1 = (f32[512,128]{1,0:T(8,128)}, f32[512,128]{1,0:T(8,128)S(1)}, u32[]{:S(2)}, u32[]{:S(2)}) collective-permute-start(f32[512,128]{1,0:T(8,128)} %get-tuple-element.24), channel_id=1, source_target_pairs={{3,0},{0,1},{1,2},{2,3},{7,4},{4,5},{5,6},{6,7},{11,8},{8,9},{9,10... | collective-permute-start | bytes 786440 | tf_op jit(solution)/shard_map/ppermute | solution.py:163

commit v2 on v1

--- a/solution.py
+++ b/solution.py
@@ -12,8 +12,9 @@
 ROWS = ("x", "z", "yh")
 OWNERS = ("x", "yh")
 SUMMED = "z"
-LINES = 16
+LINES = 8
 CHUNK = 128
+VMEM_BYTES = 16 * 1024 * 1024
 F32 = jnp.float32
 BF16 = jnp.bfloat16
 
@@ -34,16 +35,14 @@
     return sum(jnp.dot(part, table, preferred_element_type=F32) for part in pieces(value))
 
 
-def dot_lines(load, rows, first, second):
+def dot_lines(load, rows, first, second, far):
     width = first.shape[1]
-    table_1 = one_hot(first).astype(BF16)
-    table_2 = one_hot(second).astype(BF16)
-    total = [jnp.zeros((8, width), F32) for _ in range(10)]
+    table = jnp.concatenate([one_hot(partner).astype(BF16) for partner in (first, second, far)], axis=1)
+    total = [jnp.zeros((8, width), F32) for _ in range(7)]
     for start in range(0, rows, CHUNK):
         own = load(start)
-        other = permuted(own, table_1)
-        own_2 = permuted(own, table_2)
-        other_2 = permuted(other, table_2)
+        others = permuted(own, table)
+        other, own_2, other_2 = (others[:, i * width : i * width + width] for i in range(3))
         products = (
             own * own,
             other * other,
@@ -52,9 +51,6 @@
             own * other_2,
             other * own_2,
             other * other_2,
-            own_2 * own_2,
-            other_2 * other_2,
-            own_2 * other_2,
         )
         for i, product in enumerate(products):
             total[i] = total[i] + product.reshape(CHUNK // 8, 8, width).sum(axis=0)
@@ -69,13 +65,13 @@
     return cosine, -orient * (tangent * cosine)
 
 
-def two_rounds(lines, first, second):
+def two_rounds(lines, first, second, far):
     width = first.shape[1]
-    own, other, cross, a, b, c, d, own_2, other_2, cross_2 = (lines[i : i + 1] for i in range(10))
+    table_2 = one_hot(second)
+    moved = permuted(lines, table_2.astype(BF16))
+    own, other, cross, a, b, c, d = (lines[i : i + 1] for i in range(7))
+    own_2, other_2, cross_2 = (moved[i : i + 1] for i in range(3))
     indices = lax.broadcasted_iota(jnp.int32, (1, width), 1)
-    table_2 = one_hot(second)
-    wide = jnp.broadcast_to(first.astype(F32).astype(BF16), (16, width))
-    far = jnp.dot(wide, table_2.astype(BF16), preferred_element_type=F32)[:1].astype(jnp.int32)
     cos, sin = angle(jnp.where(indices < first, 1.0, -1.0), own, other, cross)
     cos_2, sin_2 = angle(jnp.where(second < far, 1.0, -1.0), own_2, other_2, cross_2)
     diag = cos * cos * own + 2.0 * cos * sin * cross + sin * sin * other
@@ -98,7 +94,16 @@
 
 
 def plan_lines(plan_ref, number):
-    return plan_ref[2 * number : 2 * number + 1], plan_ref[2 * number + 1 : 2 * number + 2]
+    return tuple(plan_ref[number, i : i + 1] for i in range(3))
+
+
+def plan_kernel(plan_ref, out_ref):
+    width = plan_ref.shape[1]
+    for i in range(out_ref.shape[0]):
+        first, second = plan_ref[2 * i : 2 * i + 1], plan_ref[2 * i + 1 : 2 * i + 2]
+        wide = jnp.broadcast_to(first.astype(F32).astype(BF16), (16, width))
+        far = jnp.dot(wide, one_hot(second).astype(BF16), preferred_element_type=F32)[:1]
+        out_ref[i] = jnp.concatenate([first, second, far.astype(jnp.int32)] + [first] * 5, axis=0)
 
 
 def sort_kernel(in_ref, out_ref):
@@ -148,9 +153,10 @@
 
 
 def call(kernel, outs, *args):
-    shapes = [jax.ShapeDtypeStruct(shape, F32) for shape in outs]
+    shapes = [jax.ShapeDtypeStruct(shape, dtype) for shape, dtype in outs]
     single = len(shapes) == 1
-    return pl.pallas_call(kernel, out_shape=shapes[0] if single else shapes)(*args)
+    params = pltpu.CompilerParams(vmem_limit_bytes=VMEM_BYTES)
+    return pl.pallas_call(kernel, out_shape=shapes[0] if single else shapes, compiler_params=params)(*args)
 
 
 def exchanged(value, axis):
@@ -166,12 +172,14 @@
 def body(matrix, plan):
     rows, owners, halves, width = matrix.shape
     peers = lax.axis_size(SUMMED)
-    flat = (rows * owners, halves * width)
-    half = (rows * owners, width)
-    sent = (peers, LINES, halves * width)
-    tables = plan.reshape(-1, plan.shape[-1])
+    flat = ((rows * owners, halves * width), F32)
+    half = ((rows * owners, width), F32)
+    sorted_rows = ((owners, rows, halves * width), F32)
+    sent = ((peers, LINES, halves * width), F32)
     lines = matrix.reshape(rows * owners * halves, width)
-    x = exchanged(call(sort_kernel, [(owners, rows, halves * width)], lines), OWNERS).reshape(flat)
+    pairs = plan.reshape(-1, plan.shape[-1])
+    x = exchanged(call(sort_kernel, [sorted_rows], lines), OWNERS).reshape(flat[0])
+    tables = call(plan_kernel, [((pairs.shape[0] // 2, 8, pairs.shape[1]), jnp.int32)], pairs)
     part = call(functools.partial(first_kernel, 0), [sent], tables, x)
     for step in range(STEPS):
         part, x = call(
@@ -183,8 +191,8 @@
         bottom = passed_along(bottom, "cols", 1)
         if step + 1 < STEPS:
             part, x = call(functools.partial(joined_kernel, 2 * step + 2), [sent, flat], tables, top, bottom)
-    x = jnp.concatenate([top, bottom], axis=1).reshape(owners, rows, halves * width)
-    return call(unsort_kernel, [lines.shape], exchanged(x, OWNERS)).reshape(matrix.shape)
+    x = jnp.concatenate([top, bottom], axis=1).reshape(sorted_rows[0])
+    return call(unsort_kernel, [(lines.shape, F32)], exchanged(x, OWNERS)).reshape(matrix.shape)
 
 
 def solution(mesh):

time: 127 us -> 103 us (0.81)
  Pallas kernels: 23.9 us -> 10.6 us
  blocking collectives: 70.6 us -> 62.2 us
    pallas_call x8 -> x9, Pallas kernels: 23.9 us -> 10.6 us  [call(): pl.pallas_call(kernel, out_shape=shapes[0] if single else shapes, compile...]
    all_to_all x5, blocking collectives: 70.6 us -> 62.2 us  [exchanged(): return lax.all_to_all(value, axis, split_axis=0, concat_axis=0, tiled=True)]
where the time goes in v2:
time: 103 us
  blocking collectives  62.2 us (60%)
  waiting for transfers between devices  22.2 us (22%)
  Pallas kernels  10.6 us (10%)
  starting transfers between devices  6.33 us (6%)
  local copies, waits for them, and re-layouts  1.05 us (1%)
    all_to_all x5, blocking collectives, exchanged(): return lax.all_to_all(value, axis, split_axis=0, concat_axis=0, tiled=True)  62.2 us
    ppermute x2, waiting for transfers between devices, passed_along(): return lax.ppermute(block, axis, route)  11.6 us
    all_to_all x1, waiting for transfers between devices, exchanged(): return lax.all_to_all(value, axis, split_axis=0, concat_axis=0, tiled=True)  10.7 us
    pallas_call x9, Pallas kernels, call(): pl.pallas_call(kernel, out_shape=shapes[0] if single else shapes, compile...  10.6 us
    all_to_all x1, starting transfers between devices, exchanged(): return lax.all_to_all(value, axis, split_axis=0, concat_axis=0, tiled=True)  6.16 us
  transfers between devices with their start and end apart: 3, of which 3 were waited for; matrix products, arithmetic and copies ran while one was open for 0% of the time, Pallas kernels for 0%

profile of v2, /device:TPU:8, one launch (start us, length us, event | category | flops | bytes accessed | tf_op | source)
XLA Modules:
  0.0 102.6 jit_solution(2146119274536052597)
XLA Ops:
  0.0 0.0 copy-start
  0.0 1.0 %copy-done = f32[64,8,2,128]{3,2,1,0:T(2,128)S(1)} copy-done((f32[64,8,2,128]{3,2,1,0:T(2,128)S(1)}, f32[64,8,2,128]{3,2,1,0:T(2,128)}, u32[]{:S(2)}) %copy-start) | copy-done | bytes 524312
  1.0 1.0 shard_map.29
  2.0 0.0 copy-start.1
  2.0 6.2 %all-to-all-start = ((f32[8,64,256]{2,1,0:T(8,128)}), f32[8,64,256]{2,1,0:T(8,128)S(1)}, u32[]{:S(2)}, u32[]{:S(2)}) async-start(f32[8,64,256]{2,1,0:T(8,128)} %shard_map.29), calls=%async_computation | async-start | bytes 1048576 | tf_op jit(solution)/shard_map/all_to_all | solution.py:163
  8.2 0.0 copy-done.1
  8.2 0.2 shard_map.28.plan_ref
  8.4 10.7 %all-to-all-done = f32[8,64,256]{2,1,0:T(8,128)S(1)} async-done(((f32[8,64,256]{2,1,0:T(8,128)}), f32[8,64,256]{2,1,0:T(8,128)S(1)}, u32[]{:S(2)}, u32[]{:S(2)}) %all-to-all-start) | async-done | bytes 524320 | tf_op jit(solution)/shard_map/all_to_all | solution.py:163
  19.0 0.9 shard_map.30
  19.9 16.6 %all_to_all.30.part_ref = f32[8,8,256]{2,1,0:T(8,128)S(1)} all-to-all(f32[8,8,256]{2,1,0:T(8,128)S(1)} %shard_map.30), channel_id=1, replica_groups=mesh['x'=4,'z'=8,'yh'=2,'cols'=4] {'z'}, dimensions={0} | all-to-all | bytes 131072 | tf_op jit(solution)/shard_map/all_to_all | solution.py:163
  36.5 2.3 %shard_map.31 = (f32[8,8,256]{2,1,0:T(8,128)S(1)}, f32[512,256]{1,0:T(8,128)S(1)}) custom-call(s32[4,8,256]{2,1,0:T(8,128)S(1)} %shard_map.28.plan_ref, f32[8,8,256]{2,1,0:T(8,128)S(1)} %all_to_all.30.part_ref, f32[512,256]{1,0:T(8,128)S(1)} %bitcast.5), custom_call_target="tpu_custom_call" | custom-call | tf_op jit(solution)/shard_map/pallas_call | solution.py:159
  38.8 10.8 %all_to_all.31.part_ref = f32[8,8,256]{2,1,0:T(8,128)S(1)} all-to-all(f32[8,8,256]{2,1,0:T(8,128)S(1)} %get-tuple-element.15), channel_id=1, replica_groups=mesh['x'=4,'z'=8,'yh'=2,'cols'=4] {'z'}, dimensions={0} | all-to-all | bytes 131072 | tf_op jit(solution)/shard_map/all_to_all | solution.py:163
  49.6 1.1 %shard_map.32 = (f32[512,128]{1,0:T(8,128)S(1)}, f32[512,128]{1,0:T(8,128)S(1)}) custom-call(s32[4,8,256]{2,1,0:T(8,128)S(1)} %shard_map.28.plan_ref, f32[8,8,256]{2,1,0:T(8,128)S(1)} %all_to_all.31.part_ref, f32[512,256]{1,0:T(8,128)S(1)} %get-tuple-element.16.x_ref), custom_call_target="tpu_custom_call" | custom-call | tf_op jit(solution)/shard_map/pallas_call | solution.py:159
  50.6 0.1 collective-permute-start
  50.7 5.8 %collective-permute-done.bottom_ref = f32[512,128]{1,0:T(8,128)S(1)} collective-permute-done((f32[512,128]{1,0:T(8,128)S(1)}, f32[512,128]{1,0:T(8,128)S(1)}, u32[]{:S(2)}, u32[]{:S(2)}) %collective-permute-start) | collective-permute-done | bytes 262176 | tf_op jit(solution)/shard_map/ppermute | solution.py:169
  56.5 0.9 shard_map.33
  57.4 10.8 %all_to_all.32.part_ref = f32[8,8,256]{2,1,0:T(8,128)S(1)} all-to-all(f32[8,8,256]{2,1,0:T(8,128)S(1)} %get-tuple-element.19), channel_id=1, replica_groups=mesh['x'=4,'z'=8,'yh'=2,'cols'=4] {'z'}, dimensions={0} | all-to-all | bytes 131072 | tf_op jit(solution)/shard_map/all_to_all | solution.py:163
  68.1 2.3 %shard_map.34 = (f32[8,8,256]{2,1,0:T(8,128)S(1)}, f32[512,256]{1,0:T(8,128)S(1)}) custom-call(s32[4,8,256]{2,1,0:T(8,128)S(1)} %shard_map.28.plan_ref, f32[8,8,256]{2,1,0:T(8,128)S(1)} %all_to_all.32.part_ref, f32[512,256]{1,0:T(8,128)S(1)} %get-tuple-element.20.x_ref), custom_call_target="tpu_custom_call" | custom-call | tf_op jit(solution)/shard_map/pallas_call | solution.py:159
  70.4 10.8 %all_to_all.33.part_ref = f32[8,8,256]{2,1,0:T(8,128)S(1)} all-to-all(f32[8,8,256]{2,1,0:T(8,128)S(1)} %get-tuple-element.21), channel_id=1, replica_groups=mesh['x'=4,'z'=8,'yh'=2,'cols'=4] {'z'}, dimensions={0} | all-to-all | bytes 131072 | tf_op jit(solution)/shard_map/all_to_all | solution.py:163
  81.2 1.1 %shard_map.35 = (f32[512,128]{1,0:T(8,128)S(1)}, f32[512,128]{1,0:T(8,128)S(1)}) custom-call(s32[4,8,256]{2,1,0:T(8,128)S(1)} %shard_map.28.plan_ref, f32[8,8,256]{2,1,0:T(8,128)S(1)} %all_to_all.33.part_ref, f32[512,256]{1,0:T(8,128)S(1)} %get-tuple-element.22.x_ref), custom_call_target="tpu_custom_call" | custom-call | tf_op jit(solution)/shard_map/pallas_call | solution.py:159
  82.2 0.1 collective-permute-start.1
  82.3 5.8 %collective-permute-done.1 = f32[512,128]{1,0:T(8,128)S(1)} collective-permute-done((f32[512,128]{1,0:T(8,128)S(1)}, f32[512,128]{1,0:T(8,128)S(1)}, u32[]{:S(2)}, u32[]{:S(2)}) %collective-permute-start.1) | collective-permute-done | bytes 262176 | tf_op jit(solution)/shard_map/ppermute | solution.py:169
  88.1 0.1 pad_maximum_fusion
  88.2 13.4 %all_to_all.34.in_ref = f32[8,64,256]{2,1,0:T(8,128)S(1)} all-to-all(f32[8,64,256]{2,1,0:T(8,128)S(1)} %bitcast.7), channel_id=1, replica_groups=mesh['x'=4,'z'=8,'yh'=2,'cols'=4] {'x','yh'}, dimensions={0} | all-to-all | bytes 1048576 | tf_op jit(solution)/shard_map/all_to_all | solution.py:163
  101.5 1.0 %shard_map.36 = f32[1024,128]{1,0:T(8,128)} custom-call(f32[8,64,256]{2,1,0:T(8,128)S(1)} %all_to_all.34.in_ref), custom_call_target="tpu_custom_call" | custom-call | tf_op jit(solution)/shard_map/pallas_call | solution.py:159
  (1 shorter events, 0.0 us)
Async XLA Ops:
  0.0 1.0 %copy-start = (f32[64,8,2,128]{3,2,1,0:T(2,128)S(1)}, f32[64,8,2,128]{3,2,1,0:T(2,128)}, u32[]{:S(2)}) copy-start(f32[64,8,2,128]{3,2,1,0:T(2,128)} %param.2) | copy-start | bytes 1572868
  2.0 6.2 %copy-start.1 = (s32[2,4,256]{2,1,0:T(4,128)S(1)}, s32[2,4,256]{2,1,0:T(4,128)}, u32[]{:S(2)}) copy-start(s32[2,4,256]{2,1,0:T(4,128)} %param.3) | copy-start | bytes 24580
  2.0 17.0 %all-to-all-start = ((f32[8,64,256]{2,1,0:T(8,128)}), f32[8,64,256]{2,1,0:T(8,128)S(1)}, u32[]{:S(2)}, u32[]{:S(2)}) async-start(f32[8,64,256]{2,1,0:T(8,128)} %shard_map.29), calls=%async_computation | async-start | bytes 1048576 | tf_op jit(solution)/shard_map/all_to_all | solution.py:163
  50.6 5.9 %collective-permute-start = (f32[512,128]{1,0:T(8,128)S(1)}, f32[512,128]{1,0:T(8,128)S(1)}, u32[]{:S(2)}, u32[]{:S(2)}) collective-permute-start(f32[512,128]{1,0:T(8,128)S(1)} %get-tuple-element.18), channel_id=1, source_target_pairs={{3,0},{0,1},{1,2},{2,3},{7,4},{4,5},{5,6},{6,7},{11,8},{8,9},{9,10... | collective-permute-start | bytes 786440 | tf_op jit(solution)/shard_map/ppermute | solution.py:169
  82.2 5.9 %collective-permute-start.1 = (f32[512,128]{1,0:T(8,128)S(1)}, f32[512,128]{1,0:T(8,128)S(1)}, u32[]{:S(2)}, u32[]{:S(2)}) collective-permute-start(f32[512,128]{1,0:T(8,128)S(1)} %get-tuple-element.24), channel_id=1, source_target_pairs={{3,0},{0,1},{1,2},{2,3},{7,4},{4,5},{5,6},{6,7},{11,8},{8,9},{9,10... | collective-permute-start | bytes 786440 | tf_op jit(solution)/shard_map/ppermute | solution.py:169

commit v3 on v2

--- a/solution.py
+++ b/solution.py
@@ -65,10 +65,9 @@
     return cosine, -orient * (tangent * cosine)
 
 
-def two_rounds(lines, first, second, far):
+def two_rounds(lines, first, second, far, columns):
     width = first.shape[1]
-    table_2 = one_hot(second)
-    moved = permuted(lines, table_2.astype(BF16))
+    moved = permuted(lines, one_hot(second).astype(BF16))
     own, other, cross, a, b, c, d = (lines[i : i + 1] for i in range(7))
     own_2, other_2, cross_2 = (moved[i : i + 1] for i in range(3))
     indices = lax.broadcasted_iota(jnp.int32, (1, width), 1)
@@ -78,12 +77,9 @@
     diag_2 = cos_2 * cos_2 * own_2 + 2.0 * cos_2 * sin_2 * cross_2 + sin_2 * sin_2 * other_2
     joint = cos * cos_2 * a + cos * sin_2 * b + sin * cos_2 * c + sin * sin_2 * d
     cos_b, sin_b = angle(jnp.where(indices < second, 1.0, -1.0), diag, diag_2, joint)
-    zero = jnp.zeros((width, width), F32)
-    rotation = jnp.where(one_hot(indices), cos_b * cos, zero)
-    rotation += jnp.where(one_hot(first), cos_b * sin, zero)
-    rotation += jnp.where(table_2, sin_b * cos_2, zero)
-    rotation += jnp.where(one_hot(far), sin_b * sin_2, zero)
-    return rotation
+    terms = ((indices, cos_b * cos), (first, cos_b * sin), (second, sin_b * cos_2), (far, sin_b * sin_2))
+    line = lax.broadcasted_iota(jnp.int32, (width, columns.stop - columns.start), 0)
+    return sum(jnp.where(line == place[:, columns], value[:, columns], 0.0) for place, value in terms)
 
 
 def write_lines(lines, out_ref):
@@ -125,31 +121,31 @@
     write_lines(lines, out_ref)
 
 
-def joined_kernel(number, plan_ref, top_ref, bottom_ref, out_ref, x_ref):
-    width = top_ref.shape[1]
-    x_ref[:, :width] = top_ref[...]
-    x_ref[:, width:] = bottom_ref[...]
-    lines = dot_lines(lambda start: x_ref[start : start + CHUNK], x_ref.shape[0], *plan_lines(plan_ref, number))
-    write_lines(lines, out_ref)
-
-
-def rotated(number, plan_ref, part_ref, x_ref):
-    lines = jnp.sum(part_ref[...], axis=0)
-    rotation = two_rounds(lines, *plan_lines(plan_ref, number))
+def rotated(number, plan_ref, part_ref, x_ref, columns):
+    rotation = two_rounds(jnp.sum(part_ref[...], axis=0), *plan_lines(plan_ref, number), columns)
     return jnp.dot(x_ref[...], rotation, precision=lax.Precision.HIGHEST, preferred_element_type=F32)
 
 
 def middle_kernel(number, plan_ref, part_ref, x_ref, out_ref, y_ref):
-    y_ref[...] = rotated(number, plan_ref, part_ref, x_ref)
+    y_ref[...] = rotated(number, plan_ref, part_ref, x_ref, slice(0, x_ref.shape[1]))
     lines = dot_lines(lambda start: y_ref[start : start + CHUNK], y_ref.shape[0], *plan_lines(plan_ref, number + 1))
     write_lines(lines, out_ref)
 
 
-def last_kernel(number, plan_ref, part_ref, x_ref, top_ref, bottom_ref):
+def top_kernel(number, plan_ref, part_ref, x_ref, top_ref):
+    top_ref[...] = rotated(number, plan_ref, part_ref, x_ref, slice(0, top_ref.shape[1]))
+
+
+def bottom_kernel(number, plan_ref, part_ref, x_ref, top_ref, y_ref):
     width = top_ref.shape[1]
-    result = rotated(number, plan_ref, part_ref, x_ref)
-    top_ref[...] = result[:, :width]
-    bottom_ref[...] = result[:, width:]
+    y_ref[:, :width] = top_ref[...]
+    y_ref[:, width:] = rotated(number, plan_ref, part_ref, x_ref, slice(width, 2 * width))
+
+
+def joined_kernel(number, plan_ref, part_ref, x_ref, top_ref, out_ref, y_ref):
+    bottom_kernel(number, plan_ref, part_ref, x_ref, top_ref, y_ref)
+    lines = dot_lines(lambda start: y_ref[start : start + CHUNK], y_ref.shape[0], *plan_lines(plan_ref, number + 1))
+    write_lines(lines, out_ref)
 
 
 def call(kernel, outs, *args):
@@ -185,14 +181,19 @@
         part, x = call(
             functools.partial(middle_kernel, 2 * step), [sent, flat], tables, exchanged(part, SUMMED), x
         )
-        top, bottom = call(
-            functools.partial(last_kernel, 2 * step + 1), [half, half], tables, exchanged(part, SUMMED), x
-        )
-        bottom = passed_along(bottom, "cols", 1)
+        x_before = passed_along(x, "cols", 1)
+        part = exchanged(part, SUMMED)
+        part_before = passed_along(part, "cols", 1)
+        number = 2 * step + 1
+        top = call(functools.partial(top_kernel, number), [half], tables, part, x)
         if step + 1 < STEPS:
-            part, x = call(functools.partial(joined_kernel, 2 * step + 2), [sent, flat], tables, top, bottom)
-    x = jnp.concatenate([top, bottom], axis=1).reshape(sorted_rows[0])
-    return call(unsort_kernel, [(lines.shape, F32)], exchanged(x, OWNERS)).reshape(matrix.shape)
+            part, x = call(
+                functools.partial(joined_kernel, number), [sent, flat], tables, part_before, x_before, top
+            )
+        else:
+            x = call(functools.partial(bottom_kernel, number), [flat], tables, part_before, x_before, top)
+    x = exchanged(x.reshape(sorted_rows[0]), OWNERS)
+    return call(unsort_kernel, [(lines.shape, F32)], x).reshape(matrix.shape)
 
 
 def solution(mesh):

time: 103 us -> 100 us (0.971)
  waiting for transfers between devices: 22.2 us -> 15.5 us
  Pallas kernels: 10.6 us -> 12.7 us
  blocking collectives: 62.2 us -> 63.4 us
    ppermute x2 -> x4, waiting for transfers between devices: 11.6 us -> 4.79 us  [passed_along(): return lax.ppermute(block, axis, route)]
    pallas_call x9 -> x10, Pallas kernels: 10.6 us -> 12.7 us  [call(): pl.pallas_call(kernel, out_shape=shapes[0] if single else shapes, compile...]
    all_to_all x5, blocking collectives: 62.2 us -> 63.4 us  [exchanged(): return lax.all_to_all(value, axis, split_axis=0, concat_axis=0, tiled=True)]
  transfers between devices with their start and end apart: 3 -> 5, of which waited for: 3 -> 3; matrix products, arithmetic and copies ran while one was open for 0% -> 0% of each run, Pallas kernels for 0% -> 2%
where the time goes in v3:
time: 100 us; the launch traced here: 99.7 us
  blocking collectives  63.4 us (63%)
  waiting for transfers between devices  15.5 us (16%)
  Pallas kernels  12.7 us (13%)
  starting transfers between devices  6.96 us (7%)
  local copies, waits for them, and re-layouts  1.05 us (1%)
    all_to_all x5, blocking collectives, exchanged(): return lax.all_to_all(value, axis, split_axis=0, concat_axis=0, tiled=True)  63.4 us
    pallas_call x10, Pallas kernels, call(): pl.pallas_call(kernel, out_shape=shapes[0] if single else shapes, compile...  12.7 us
    all_to_all x1, waiting for transfers between devices, exchanged(): return lax.all_to_all(value, axis, split_axis=0, concat_axis=0, tiled=True)  10.7 us
    all_to_all x1, starting transfers between devices, exchanged(): return lax.all_to_all(value, axis, split_axis=0, concat_axis=0, tiled=True)  6.16 us
    ppermute x4, waiting for transfers between devices, passed_along(): return lax.ppermute(block, axis, route)  4.79 us
  transfers between devices with their start and end apart: 5, of which 3 were waited for; matrix products, arithmetic and copies ran while one was open for 0% of the time, Pallas kernels for 2%

profile of v3, /device:TPU:8, one launch (start us, length us, event | category | flops | bytes accessed | tf_op | source)
XLA Modules:
  0.0 99.7 jit_solution(14066259506752648241)
XLA Ops:
  0.0 0.0 copy-start
  0.0 1.0 %copy-done = f32[64,8,2,128]{3,2,1,0:T(2,128)S(1)} copy-done((f32[64,8,2,128]{3,2,1,0:T(2,128)S(1)}, f32[64,8,2,128]{3,2,1,0:T(2,128)}, u32[]{:S(2)}) %copy-start) | copy-done | bytes 524312
  1.0 1.0 shard_map.29
  2.0 0.0 copy-start.1
  2.0 6.2 %all-to-all-start = ((f32[8,64,256]{2,1,0:T(8,128)}), f32[8,64,256]{2,1,0:T(8,128)S(1)}, u32[]{:S(2)}, u32[]{:S(2)}) async-start(f32[8,64,256]{2,1,0:T(8,128)} %shard_map.29), calls=%async_computation | async-start | bytes 1048576 | tf_op jit(solution)/shard_map/all_to_all | solution.py:159
  8.2 0.0 copy-done.1
  8.2 0.2 shard_map.28.plan_ref
  8.4 10.7 %all-to-all-done = f32[8,64,256]{2,1,0:T(8,128)S(1)} async-done(((f32[8,64,256]{2,1,0:T(8,128)}), f32[8,64,256]{2,1,0:T(8,128)S(1)}, u32[]{:S(2)}, u32[]{:S(2)}) %all-to-all-start) | async-done | bytes 524320 | tf_op jit(solution)/shard_map/all_to_all | solution.py:159
  19.0 0.9 shard_map.30
  19.9 16.6 %all_to_all.30.part_ref = f32[8,8,256]{2,1,0:T(8,128)S(1)} all-to-all(f32[8,8,256]{2,1,0:T(8,128)S(1)} %shard_map.30), channel_id=1, replica_groups=mesh['x'=4,'z'=8,'yh'=2,'cols'=4] {'z'}, dimensions={0} | all-to-all | bytes 131072 | tf_op jit(solution)/shard_map/all_to_all | solution.py:159
  36.5 2.3 %shard_map.31 = (f32[8,8,256]{2,1,0:T(8,128)S(1)}, f32[512,256]{1,0:T(8,128)S(1)}) custom-call(s32[4,8,256]{2,1,0:T(8,128)S(1)} %shard_map.28.plan_ref, f32[8,8,256]{2,1,0:T(8,128)S(1)} %all_to_all.30.part_ref, f32[512,256]{1,0:T(8,128)S(1)} %bitcast.5), custom_call_target="tpu_custom_call" | custom-call | tf_op jit(solution)/shard_map/pallas_call | solution.py:155
  38.8 0.1 collective-permute-start.1
  38.9 11.1 %all_to_all.31.part_ref = f32[8,8,256]{2,1,0:T(8,128)S(1)} all-to-all(f32[8,8,256]{2,1,0:T(8,128)S(1)} %get-tuple-element.11), channel_id=1, replica_groups=mesh['x'=4,'z'=8,'yh'=2,'cols'=4] {'z'}, dimensions={0} | all-to-all | bytes 131072 | tf_op jit(solution)/shard_map/all_to_all | solution.py:159
  50.0 0.2 collective-permute-start
  50.2 1.0 shard_map.32.top_ref
  51.2 2.5 %collective-permute-done.part_ref = f32[8,8,256]{2,1,0:T(8,128)S(1)} collective-permute-done((f32[8,8,256]{2,1,0:T(8,128)S(1)}, f32[8,8,256]{2,1,0:T(8,128)S(1)}, u32[]{:S(2)}, u32[]{:S(2)}) %collective-permute-start) | collective-permute-done | bytes 65568 | tf_op jit(solution)/shard_map/ppermute | solution.py:165
  53.7 0.0 collective-permute-done.1.x_ref
  53.7 2.2 %shard_map.33 = (f32[8,8,256]{2,1,0:T(8,128)S(1)}, f32[512,256]{1,0:T(8,128)S(1)}) custom-call(s32[4,8,256]{2,1,0:T(8,128)S(1)} %shard_map.28.plan_ref, f32[8,8,256]{2,1,0:T(8,128)S(1)} %collective-permute-done.part_ref, f32[512,256]{1,0:T(8,128)S(1)} %collective-permute-done.1.x_ref, f32[512,128]{1,0:T(8,128)S(1)} %shard_map.32.top_ref), custom_call_target="tpu_custom_call" | custom-call | tf_op jit(solution)/shard_map/pallas_call | solution.py:155
  55.9 10.8 %all_to_all.32.part_ref = f32[8,8,256]{2,1,0:T(8,128)S(1)} all-to-all(f32[8,8,256]{2,1,0:T(8,128)S(1)} %get-tuple-element.13), channel_id=1, replica_groups=mesh['x'=4,'z'=8,'yh'=2,'cols'=4] {'z'}, dimensions={0} | all-to-all | bytes 131072 | tf_op jit(solution)/shard_map/all_to_all | solution.py:159
  66.6 2.3 %shard_map.34 = (f32[8,8,256]{2,1,0:T(8,128)S(1)}, f32[512,256]{1,0:T(8,128)S(1)}) custom-call(s32[4,8,256]{2,1,0:T(8,128)S(1)} %shard_map.28.plan_ref, f32[8,8,256]{2,1,0:T(8,128)S(1)} %all_to_all.32.part_ref, f32[512,256]{1,0:T(8,128)S(1)} %get-tuple-element.14.x_ref), custom_call_target="tpu_custom_call" | custom-call | tf_op jit(solution)/shard_map/pallas_call | solution.py:155
  68.9 0.1 collective-permute-start.3
  69.0 10.8 %all_to_all.33.part_ref = f32[8,8,256]{2,1,0:T(8,128)S(1)} all-to-all(f32[8,8,256]{2,1,0:T(8,128)S(1)} %get-tuple-element.15), channel_id=1, replica_groups=mesh['x'=4,'z'=8,'yh'=2,'cols'=4] {'z'}, dimensions={0} | all-to-all | bytes 131072 | tf_op jit(solution)/shard_map/all_to_all | solution.py:159
  79.8 0.4 collective-permute-start.2
  80.3 1.0 shard_map.35.top_ref
  81.3 2.3 %collective-permute-done.2.part_ref = f32[8,8,256]{2,1,0:T(8,128)S(1)} collective-permute-done((f32[8,8,256]{2,1,0:T(8,128)S(1)}, f32[8,8,256]{2,1,0:T(8,128)S(1)}, u32[]{:S(2)}, u32[]{:S(2)}) %collective-permute-start.2) | collective-permute-done | bytes 65568 | tf_op jit(solution)/shard_map/ppermute | solution.py:165
  83.5 0.0 collective-permute-done.3.x_ref
  83.5 1.0 shard_map.36
  84.5 14.1 %all_to_all.34.in_ref = f32[8,64,256]{2,1,0:T(8,128)S(1)} all-to-all(f32[8,64,256]{2,1,0:T(8,128)S(1)} %bitcast.6), channel_id=1, replica_groups=mesh['x'=4,'z'=8,'yh'=2,'cols'=4] {'x','yh'}, dimensions={0} | all-to-all | bytes 1048576 | tf_op jit(solution)/shard_map/all_to_all | solution.py:159
  98.6 1.0 %shard_map.37 = f32[1024,128]{1,0:T(8,128)} custom-call(f32[8,64,256]{2,1,0:T(8,128)S(1)} %all_to_all.34.in_ref), custom_call_target="tpu_custom_call" | custom-call | tf_op jit(solution)/shard_map/pallas_call | solution.py:155
  (1 shorter events, 0.0 us)
Async XLA Ops:
  0.0 1.0 %copy-start = (f32[64,8,2,128]{3,2,1,0:T(2,128)S(1)}, f32[64,8,2,128]{3,2,1,0:T(2,128)}, u32[]{:S(2)}) copy-start(f32[64,8,2,128]{3,2,1,0:T(2,128)} %param.2) | copy-start | bytes 1572868
  2.0 6.2 %copy-start.1 = (s32[2,4,256]{2,1,0:T(4,128)S(1)}, s32[2,4,256]{2,1,0:T(4,128)}, u32[]{:S(2)}) copy-start(s32[2,4,256]{2,1,0:T(4,128)} %param.3) | copy-start | bytes 24580
  2.0 17.0 %all-to-all-start = ((f32[8,64,256]{2,1,0:T(8,128)}), f32[8,64,256]{2,1,0:T(8,128)S(1)}, u32[]{:S(2)}, u32[]{:S(2)}) async-start(f32[8,64,256]{2,1,0:T(8,128)} %shard_map.29), calls=%async_computation | async-start | bytes 1048576 | tf_op jit(solution)/shard_map/all_to_all | solution.py:159
  38.8 14.9 %collective-permute-start.1 = (f32[512,256]{1,0:T(8,128)S(1)}, f32[512,256]{1,0:T(8,128)S(1)}, u32[]{:S(2)}, u32[]{:S(2)}) collective-permute-start(f32[512,256]{1,0:T(8,128)S(1)} %get-tuple-element.12.x_ref), channel_id=1, source_target_pairs={{3,0},{0,1},{1,2},{2,3},{7,4},{4,5},{5,6},{6,7},{11,8},{8,9},{9,10... | collective-permute-start | bytes 1572872 | tf_op jit(solution)/shard_map/ppermute | solution.py:165
  50.0 3.7 %collective-permute-start = (f32[8,8,256]{2,1,0:T(8,128)S(1)}, f32[8,8,256]{2,1,0:T(8,128)S(1)}, u32[]{:S(2)}, u32[]{:S(2)}) collective-permute-start(f32[8,8,256]{2,1,0:T(8,128)S(1)} %all_to_all.31.part_ref), channel_id=1, source_target_pairs={{3,0},{0,1},{1,2},{2,3},{7,4},{4,5},{5,6},{6,7},{11,8},{8,9},{9,10... | collective-permute-start | bytes 196616 | tf_op jit(solution)/shard_map/ppermute | solution.py:165
  68.9 14.6 %collective-permute-start.3 = (f32[512,256]{1,0:T(8,128)S(1)}, f32[512,256]{1,0:T(8,128)S(1)}, u32[]{:S(2)}, u32[]{:S(2)}) collective-permute-start(f32[512,256]{1,0:T(8,128)S(1)} %get-tuple-element.16.x_ref), channel_id=1, source_target_pairs={{3,0},{0,1},{1,2},{2,3},{7,4},{4,5},{5,6},{6,7},{11,8},{8,9},{9,10... | collective-permute-start | bytes 1572872 | tf_op jit(solution)/shard_map/ppermute | solution.py:165
  79.8 3.7 %collective-permute-start.2 = (f32[8,8,256]{2,1,0:T(8,128)S(1)}, f32[8,8,256]{2,1,0:T(8,128)S(1)}, u32[]{:S(2)}, u32[]{:S(2)}) collective-permute-start(f32[8,8,256]{2,1,0:T(8,128)S(1)} %all_to_all.33.part_ref), channel_id=1, source_target_pairs={{3,0},{0,1},{1,2},{2,3},{7,4},{4,5},{5,6},{6,7},{11,8},{8,9},{9,10... | collective-permute-start | bytes 196616 | tf_op jit(solution)/shard_map/ppermute | solution.py:165

commit v4 on v3

v4 whole, which is shorter than its diff:
```python
import jax
import jax.numpy as jnp
from jax import lax
from jax.experimental import pallas as pl
from jax.experimental.pallas import tpu as pltpu
from jax.sharding import Mesh
from jax.sharding import PartitionSpec as P

STEPS = 2
ROWS = ("x", "z", "yh")
OWNERS = ("x", "yh")
SUMMED = "z"
ROUNDS = 4
WORDS = 1 << ROUNDS
LINES = 56
VMEM_BYTES = 16 * 1024 * 1024
F32 = jnp.float32
BF16 = jnp.bfloat16


def one_hot(partner):
    width = partner.shape[1]
    return lax.broadcasted_iota(jnp.int32, (width, width), 0) == partner


def pieces(value):
    high = value.astype(BF16)
    rest = value - high.astype(F32)
    middle = rest.astype(BF16)
    return high, middle, (rest - middle.astype(F32)).astype(BF16)


def permuted(value, table):
    return sum(jnp.dot(part, table, preferred_element_type=F32) for part in pieces(value))


def angle(orient, own, other, cross):
    spread = orient * (other - own)
    sign = jnp.where(spread >= 0.0, 1.0, -1.0)
    tangent = sign * 2.0 * cross / (jnp.abs(spread) + jnp.sqrt(spread * spread + 4.0 * cross * cross))
    cosine = 1.0 / jnp.sqrt(1.0 + tangent * tangent)
    return cosine, -orient * (tangent * cosine)


def write_lines(x, words_ref, table_ref, out_ref):
    width = x.shape[1]
    gram = lax.dot_general(
        x, x, (((0,), (0,)), ((), ())), precision=lax.Precision.HIGHEST, preferred_element_type=F32
    )
    parts = pieces(gram)
    line = lax.broadcasted_iota(jnp.int32, (width, width), 0)

    def picked(value, word):
        return jnp.where(line == words_ref[word : word + 1], value, 0.0).sum(axis=0, keepdims=True)

    def written(place, value):
        for i in range(out_ref.shape[0]):
            out_ref[i, place : place + 1] = value

    written(0, picked(gram, 0))
    for number in range(ROUNDS):
        count = 1 << number
        for right in range(count):
            column = (count + right - 1) * width
            moved = sum(
                jnp.dot(part, table_ref[:, column : column + width], preferred_element_type=F32) for part in parts
            )
            for left in range(right + 1):
                written(place_of(number, left, right), picked(moved, left))


def place_of(number, left, right):
    return 1 + sum((1 << i) * ((1 << i) + 1) // 2 for i in range(number)) + right * (right + 1) // 2 + left


def table_of(table_ref, number):
    width = table_ref.shape[0]
    column = ((1 << number) - 1) * width
    return table_ref[:, column : column + width]


def angles_kernel(words_ref, table_ref, part_ref, out_ref, lines_ref, moved_ref, state_ref):
    width = words_ref.shape[1]
    lines = jnp.sum(part_ref[...], axis=0)
    lines_ref[...] = lines
    split = pieces(lines)
    for number in range(ROUNDS):
        table = table_of(table_ref, number)
        moved_ref[number] = sum(jnp.dot(part, table, preferred_element_type=F32) for part in split)
    indices = lax.broadcasted_iota(jnp.int32, (1, width), 1)
    state_ref[...] = jnp.zeros_like(state_ref)
    diag, diag_2 = lines_ref[:1], moved_ref[0, :1]
    weights, weights_2 = [jnp.ones((1, width), F32)], [jnp.ones((1, width), F32)]
    for number in range(ROUNDS):
        count = 1 << number
        if number:
            for i, value in enumerate([diag] + weights):
                state_ref[i : i + 1] = value
            other = permuted(state_ref[...], table_of(table_ref, number))
            diag_2, *weights_2 = (other[i : i + 1] for i in range(1 + count))
        cross = jnp.zeros((1, width), F32)
        for left in range(count):
            inner = jnp.zeros((1, width), F32)
            for right in range(count):
                place = place_of(number, min(left, right), max(left, right))
                source = lines_ref[place : place + 1] if left <= right else moved_ref[number, place : place + 1]
                inner += weights_2[right] * source
            cross += weights[left] * inner
        orient = jnp.where(indices < words_ref[count : count + 1], 1.0, -1.0)
        cos, sin = angle(orient, diag, diag_2, cross)
        diag = cos * cos * diag + 2.0 * cos * sin * cross + sin * sin * diag_2
        weights = [cos * value for value in weights] + [sin * value for value in weights_2]
    for i, value in enumerate(weights):
        out_ref[i : i + 1] = value


def plan_kernel(plan_ref, *out_refs):
    width = plan_ref.shape[1]
    steps = len(out_refs) // 2
    for step in range(steps):
        words_ref, table_ref = out_refs[step], out_refs[steps + step]
        words_ref[:1] = lax.broadcasted_iota(jnp.int32, (1, width), 1)
        for number in range(ROUNDS):
            count = 1 << number
            partner = plan_ref[step * ROUNDS + number : step * ROUNDS + number + 1]
            table = one_hot(partner).astype(BF16)
            known = words_ref[...].astype(F32).astype(BF16)
            moved = jnp.dot(known, table, preferred_element_type=F32)
            for i in range(count):
                words_ref[count + i : count + i + 1] = moved[i : i + 1].astype(jnp.int32)
        for word in range(1, WORDS):
            column = (word - 1) * width
            table_ref[:, column : column + width] = one_hot(words_ref[word : word + 1]).astype(BF16)


def sort_kernel(in_ref, out_ref):
    rows, owners = out_ref.shape[1], out_ref.shape[0]
    for i in range(owners):
        for half in range(2):
            out_ref[i, :, half * 128 : half * 128 + 128] = in_ref[pl.ds(2 * i + half, rows, 2 * owners), :]


def unsort_kernel(in_ref, out_ref):
    rows, owners = in_ref.shape[1], in_ref.shape[0]
    for i in range(owners):
        for half in range(2):
            out_ref[pl.ds(2 * i + half, rows, 2 * owners), :] = in_ref[i, :, half * 128 : half * 128 + 128]


def rotated(words_ref, weights_ref, x_ref, columns):
    line = lax.broadcasted_iota(jnp.int32, (x_ref.shape[1], columns.stop - columns.start), 0)
    rotation = jnp.zeros(line.shape, F32)
    for i in range(WORDS):
        rotation += jnp.where(line == words_ref[i : i + 1, columns], weights_ref[i : i + 1, columns], 0.0)
    return jnp.dot(x_ref[...], rotation, precision=lax.Precision.HIGHEST, preferred_element_type=F32)


def first_kernel(words_ref, table_ref, x_ref, out_ref):
    write_lines(x_ref[...], words_ref, table_ref, out_ref)


def top_kernel(words_ref, weights_ref, x_ref, top_ref):
    top_ref[...] = rotated(words_ref, weights_ref, x_ref, slice(0, top_ref.shape[1]))


def bottom_kernel(words_ref, weights_ref, x_ref, top_ref, y_ref):
    width = top_ref.shape[1]
    y_ref[:, :width] = top_ref[...]
    y_ref[:, width:] = rotated(words_ref, weights_ref, x_ref, slice(width, 2 * width))


def joined_kernel(words_ref, weights_ref, x_ref, top_ref, next_words_ref, next_table_ref, out_ref, y_ref):
    bottom_kernel(words_ref, weights_ref, x_ref, top_ref, y_ref)
    write_lines(y_ref[...], next_words_ref, next_table_ref, out_ref)


def call(kernel, outs, *args, scratch=()):
    shapes = [jax.ShapeDtypeStruct(shape, dtype) for shape, dtype in outs]
    single = len(shapes) == 1
    return pl.pallas_call(
        kernel,
        out_shape=shapes[0] if single else shapes,
        scratch_shapes=[pltpu.VMEM(shape, F32) for shape in scratch],
        compiler_params=pltpu.CompilerParams(vmem_limit_bytes=VMEM_BYTES),
    )(*args)


def exchanged(value, axis):
    return lax.all_to_all(value, axis, split_axis=0, concat_axis=0, tiled=True)


def passed_along(block, axis, distance):
    devices = range(lax.axis_size(axis))
    route = [((i - distance) % len(devices), i) for i in devices]
    return lax.ppermute(block, axis, route)


def body(matrix, plan):
    rows, owners, halves, width = matrix.shape
    peers = lax.axis_size(SUMMED)
    across = halves * width
    flat = ((rows * owners, across), F32)
    half = ((rows * owners, width), F32)
    sorted_rows = ((owners, rows, across), F32)
    sent = ((peers, LINES, across), F32)
    weights_shape = ((WORDS, across), F32)
    scratch = [(LINES, across), (ROUNDS, LINES, across), (16, across)]
    lines = matrix.reshape(rows * owners * halves, width)
    x = exchanged(call(sort_kernel, [sorted_rows], lines), OWNERS).reshape(flat[0])
    words_shape = ((WORDS, across), jnp.int32)
    table_shape = ((across, (WORDS - 1) * across), BF16)
    plans = call(plan_kernel, [words_shape] * STEPS + [table_shape] * STEPS, plan.reshape(-1, across))
    words, tables = plans[:STEPS], plans[STEPS:]
    part = call(first_kernel, [sent], words[0], tables[0], x)
    for step in range(STEPS):
        x_before = passed_along(x, "cols", 1)
        part = exchanged(part, SUMMED)
        weights = call(angles_kernel, [weights_shape], words[step], tables[step], part, scratch=scratch)
        weights_before = passed_along(weights, "cols", 1)
        top = call(top_kernel, [half], words[step], weights, x)
        args = (words[step], weights_before, x_before, top)
        if step + 1 < STEPS:
            part, x = call(joined_kernel, [sent, flat], *args, words[step + 1], tables[step + 1])
        else:
            x = call(bottom_kernel, [flat], *args)
    x = exchanged(x.reshape(sorted_rows[0]), OWNERS)
    return call(unsort_kernel, [(lines.shape, F32)], x).reshape(matrix.shape)


def solution(mesh):
    split = Mesh(mesh.devices.reshape(4, 8, 2, mesh.shape["cols"]), ("x", "z", "yh", "cols"))
    in_specs = (P(ROWS, "cols", None, None), P())
    out_specs = P(ROWS, "cols", None, None)
    return jax.shard_map(body, mesh=split, in_specs=in_specs, out_specs=out_specs, check_vma=False)
```

time: 100 us -> 99.2 us (level)
  blocking collectives: 63.4 us -> 13.7 us
  waiting for transfers between devices: 15.5 us -> 42.7 us
  starting transfers between devices: 6.96 us -> 18.4 us
  local copies, waits for them, and re-layouts: 1.05 us -> 6.2 us
  Pallas kernels: 12.7 us -> 17.6 us
    all_to_all x5 -> x1, blocking collectives: 63.4 us -> 13.7 us  [exchanged(): return lax.all_to_all(value, axis, split_axis=0, concat_axis=0, tiled=True)]
    all_to_all x1 -> x3, waiting for transfers between devices: 10.7 us -> 38 us  [exchanged(): return lax.all_to_all(value, axis, split_axis=0, concat_axis=0, tiled=True)]
    all_to_all x1 -> x3, starting transfers between devices: 6.16 us -> 18 us  [exchanged(): return lax.all_to_all(value, axis, split_axis=0, concat_axis=0, tiled=True)]
    unnamed x4 -> x12, local copies, waits for them, and re-layouts: 1.04 us -> 6.19 us
    pallas_call x10, Pallas kernels: 12.7 us -> 17.6 us  [call(): pl.pallas_call(kernel, out_shape=shapes[0] if single else shapes, scratch...]
  transfers between devices with their start and end apart: 5 -> 7, of which waited for: 3 -> 5; matrix products, arithmetic and copies ran while one was open for 0% -> 0% of each run, Pallas kernels for 2% -> 6%
where the time goes in v4:
time: 99.2 us; the launch traced here: 98.7 us
  waiting for transfers between devices  42.7 us (43%)
  starting transfers between devices  18.4 us (19%)
  Pallas kernels  17.6 us (18%)
  blocking collectives  13.7 us (14%)
  local copies, waits for them, and re-layouts  6.2 us (6%)
    all_to_all x3, waiting for transfers between devices, exchanged(): return lax.all_to_all(value, axis, split_axis=0, concat_axis=0, tiled=True)  38 us
    all_to_all x3, starting transfers between devices, exchanged(): return lax.all_to_all(value, axis, split_axis=0, concat_axis=0, tiled=True)  18 us
    pallas_call x10, Pallas kernels, call(): pl.pallas_call(kernel, out_shape=shapes[0] if single else shapes, scratch...  17.6 us
    all_to_all x1, blocking collectives, exchanged(): return lax.all_to_all(value, axis, split_axis=0, concat_axis=0, tiled=True)  13.7 us
    unnamed x12, local copies, waits for them, and re-layouts  6.19 us
    ppermute x4, waiting for transfers between devices, passed_along(): return lax.ppermute(block, axis, route)  4.7 us
  transfers between devices with their start and end apart: 7, of which 5 were waited for; matrix products, arithmetic and copies ran while one was open for 0% of the time, Pallas kernels for 6%

profile of v4, /device:TPU:8, one launch (start us, length us, event | category | flops | bytes accessed | tf_op | source)
XLA Modules:
  0.0 98.7 jit_solution(6604169106675681246)
XLA Ops:
  0.0 0.0 copy-start.3
  0.0 1.0 %copy-done.3 = f32[64,8,2,128]{3,2,1,0:T(2,128)S(1)} copy-done((f32[64,8,2,128]{3,2,1,0:T(2,128)S(1)}, f32[64,8,2,128]{3,2,1,0:T(2,128)}, u32[]{:S(2)}) %copy-start.3) | copy-done | bytes 524312
  1.0 0.0 copy-start.5
  1.0 1.0 shard_map.29
  2.0 6.0 %all-to-all-start = ((f32[8,64,256]{2,1,0:T(8,128)}), f32[8,64,256]{2,1,0:T(8,128)S(1)}, u32[]{:S(2)}, u32[]{:S(2)}) async-start(f32[8,64,256]{2,1,0:T(8,128)} %shard_map.29), calls=%async_computation | async-start | bytes 1048576 | tf_op jit(solution)/shard_map/all_to_all | solution.py:189
  8.0 0.0 copy-done.5
  8.1 2.2 %shard_map.28 = (s32[16,256]{1,0:T(8,128)S(1)}, s32[16,256]{1,0:T(8,128)S(1)}, bf16[256,3840]{1,0:T(8,128)(2,1)S(1)}, bf16[256,3840]{1,0:T(8,128)(2,1)S(1)}) custom-call(s32[8,256]{1,0:T(8,128)S(1)} %reshape.15.plan_ref), custom_call_target="tpu_custom_call" | custom-call | tf_op jit(solution)/shard_map/pallas_call | solution.py:180
  10.3 0.0 copy-start
  10.3 1.3 %copy-done = bf16[256,3840]{1,0:T(8,128)(2,1)} copy-done((bf16[256,3840]{1,0:T(8,128)(2,1)}, bf16[256,3840]{1,0:T(8,128)(2,1)S(1)}, u32[]{:S(2)}) %copy-start) | copy-done | bytes 1966104
  11.6 7.4 %all-to-all-done = f32[8,64,256]{2,1,0:T(8,128)S(1)} async-done(((f32[8,64,256]{2,1,0:T(8,128)}), f32[8,64,256]{2,1,0:T(8,128)S(1)}, u32[]{:S(2)}, u32[]{:S(2)}) %all-to-all-start) | async-done | bytes 524320 | tf_op jit(solution)/shard_map/all_to_all | solution.py:189
  18.9 0.0 copy-start.1
  18.9 1.5 %copy-done.1 = bf16[256,3840]{1,0:T(8,128)(2,1)S(1)} copy-done((bf16[256,3840]{1,0:T(8,128)(2,1)S(1)}, bf16[256,3840]{1,0:T(8,128)(2,1)}, u32[]{:S(2)}) %copy-start.1) | copy-done | bytes 1966104
  20.5 4.5 %shard_map.30 = f32[8,56,256]{2,1,0:T(8,128)} custom-call(s32[16,256]{1,0:T(8,128)S(1)} %get-tuple-element.13.words_ref, bf16[256,3840]{1,0:T(8,128)(2,1)S(1)} %copy-done.1, f32[512,256]{1,0:T(8,128)S(1)} %bitcast.4), custom_call_target="tpu_custom_call" | custom-call | tf_op jit(solution)/shard_map/pallas_call | solution.py:180
  24.9 8.5 %all-to-all-start.1 = ((f32[8,56,256]{2,1,0:T(8,128)}), f32[8,56,256]{2,1,0:T(8,128)S(1)}, u32[]{:S(2)}, u32[]{:S(2)}) async-start(f32[8,56,256]{2,1,0:T(8,128)} %shard_map.30), calls=%async_computation.1 | async-start | bytes 917504 | tf_op jit(solution)/shard_map/all_to_all | solution.py:189
  33.4 0.0 collective-permute-start.1
  33.4 15.1 %all-to-all-done.1.part_ref = f32[8,56,256]{2,1,0:T(8,128)S(1)} async-done(((f32[8,56,256]{2,1,0:T(8,128)}), f32[8,56,256]{2,1,0:T(8,128)S(1)}, u32[]{:S(2)}, u32[]{:S(2)}) %all-to-all-start.1) | async-done | bytes 458784 | tf_op jit(solution)/shard_map/all_to_all | solution.py:189
  48.5 0.0 copy-start.2
  48.5 1.5 %copy-done.2 = bf16[256,3840]{1,0:T(8,128)(2,1)S(1)} copy-done((bf16[256,3840]{1,0:T(8,128)(2,1)S(1)}, bf16[256,3840]{1,0:T(8,128)(2,1)}, u32[]{:S(2)}) %copy-start.2) | copy-done | bytes 1966104
  50.1 1.1 %shard_map.31.weights_ref = f32[16,256]{1,0:T(8,128)S(1)} custom-call(s32[16,256]{1,0:T(8,128)S(1)} %get-tuple-element.13.words_ref, bf16[256,3840]{1,0:T(8,128)(2,1)S(1)} %copy-done.2, f32[8,56,256]{2,1,0:T(8,128)S(1)} %all-to-all-done.1.part_ref), custom_call_target="tpu_custom_call" | custom-call | tf_op jit(solution)/shard_map/pallas_call | solution.py:180
  51.2 0.3 collective-permute-start
  51.4 0.8 shard_map.32.top_ref
  52.2 0.0 collective-permute-done.1.x_ref
  52.3 2.3 %collective-permute-done.weights_ref = f32[16,256]{1,0:T(8,128)S(1)} collective-permute-done((f32[16,256]{1,0:T(8,128)S(1)}, f32[16,256]{1,0:T(8,128)S(1)}, u32[]{:S(2)}, u32[]{:S(2)}) %collective-permute-start) | collective-permute-done | bytes 16416 | tf_op jit(solution)/shard_map/ppermute | solution.py:195
  54.6 4.4 %shard_map.33 = (f32[8,56,256]{2,1,0:T(8,128)S(1)}, f32[512,256]{1,0:T(8,128)S(1)}) custom-call(s32[16,256]{1,0:T(8,128)S(1)} %get-tuple-element.13.words_ref, f32[16,256]{1,0:T(8,128)S(1)} %collective-permute-done.weights_ref, f32[512,256]{1,0:T(8,128)S(1)} %collective-permute-done.1.x_ref, f32[512,128]{1,0:T(8,128)S(1)} %shard_map.32.top_ref, ...), custom_call_target="tpu_custom_call" | custom-call | tf_op jit(solution)/shard_map/pallas_call | solution.py:180
  59.0 0.0 copy-start.4
  59.0 0.8 copy-done.4
  59.8 3.5 %all-to-all-start.2 = ((f32[8,56,256]{2,1,0:T(8,128)}), f32[8,56,256]{2,1,0:T(8,128)S(1)}, u32[]{:S(2)}, u32[]{:S(2)}) async-start(f32[8,56,256]{2,1,0:T(8,128)} %copy-done.4), calls=%async_computation.2 | async-start | bytes 917504 | tf_op jit(solution)/shard_map/all_to_all | solution.py:189
  63.2 0.1 collective-permute-start.3
  63.3 15.5 %all-to-all-done.2.part_ref = f32[8,56,256]{2,1,0:T(8,128)S(1)} async-done(((f32[8,56,256]{2,1,0:T(8,128)}), f32[8,56,256]{2,1,0:T(8,128)S(1)}, u32[]{:S(2)}, u32[]{:S(2)}) %all-to-all-start.2) | async-done | bytes 458784 | tf_op jit(solution)/shard_map/all_to_all | solution.py:189
  78.9 1.1 %shard_map.34.weights_ref = f32[16,256]{1,0:T(8,128)S(1)} custom-call(s32[16,256]{1,0:T(8,128)S(1)} %get-tuple-element.11.next_words_ref.words_ref, bf16[256,3840]{1,0:T(8,128)(2,1)S(1)} %get-tuple-element.12.next_table_ref.table_ref, f32[8,56,256]{2,1,0:T(8,128)S(1)} %all-to-all-done.2.part_ref), custom_call_target="tpu_custom_call" | custom-call | tf_op jit(solution)/shard_map/pallas_call | solution.py:180
  79.9 0.1 collective-permute-start.2
  80.0 0.8 shard_map.35.top_ref
  80.8 0.0 collective-permute-done.3.x_ref
  80.8 2.3 %collective-permute-done.2.weights_ref = f32[16,256]{1,0:T(8,128)S(1)} collective-permute-done((f32[16,256]{1,0:T(8,128)S(1)}, f32[16,256]{1,0:T(8,128)S(1)}, u32[]{:S(2)}, u32[]{:S(2)}) %collective-permute-start.2) | collective-permute-done | bytes 16416 | tf_op jit(solution)/shard_map/ppermute | solution.py:195
  83.2 0.8 shard_map.36
  84.0 13.7 %all_to_all.20.in_ref = f32[8,64,256]{2,1,0:T(8,128)S(1)} all-to-all(f32[8,64,256]{2,1,0:T(8,128)S(1)} %bitcast.7), channel_id=1, replica_groups=mesh['x'=4,'z'=8,'yh'=2,'cols'=4] {'x','yh'}, dimensions={0} | all-to-all | bytes 1048576 | tf_op jit(solution)/shard_map/all_to_all | solution.py:189
  97.7 1.0 %shard_map.37 = f32[1024,128]{1,0:T(8,128)} custom-call(f32[8,64,256]{2,1,0:T(8,128)S(1)} %all_to_all.20.in_ref), custom_call_target="tpu_custom_call" | custom-call | tf_op jit(solution)/shard_map/pallas_call | solution.py:180
  (1 shorter events, 0.0 us)
Async XLA Ops:
  0.0 1.0 %copy-start.3 = (f32[64,8,2,128]{3,2,1,0:T(2,128)S(1)}, f32[64,8,2,128]{3,2,1,0:T(2,128)}, u32[]{:S(2)}) copy-start(f32[64,8,2,128]{3,2,1,0:T(2,128)} %param.2) | copy-start | bytes 1572868
  1.0 7.0 %copy-start.5 = (s32[2,4,256]{2,1,0:T(4,128)S(1)}, s32[2,4,256]{2,1,0:T(4,128)}, u32[]{:S(2)}) copy-start(s32[2,4,256]{2,1,0:T(4,128)} %param.3) | copy-start | bytes 24580
  2.0 16.9 %all-to-all-start = ((f32[8,64,256]{2,1,0:T(8,128)}), f32[8,64,256]{2,1,0:T(8,128)S(1)}, u32[]{:S(2)}, u32[]{:S(2)}) async-start(f32[8,64,256]{2,1,0:T(8,128)} %shard_map.29), calls=%async_computation | async-start | bytes 1048576 | tf_op jit(solution)/shard_map/all_to_all | solution.py:189
  10.3 1.3 %copy-start = (bf16[256,3840]{1,0:T(8,128)(2,1)}, bf16[256,3840]{1,0:T(8,128)(2,1)S(1)}, u32[]{:S(2)}) copy-start(bf16[256,3840]{1,0:T(8,128)(2,1)S(1)} %get-tuple-element.14.table_ref) | copy-start | bytes 5898244
  18.9 1.5 %copy-start.1 = (bf16[256,3840]{1,0:T(8,128)(2,1)S(1)}, bf16[256,3840]{1,0:T(8,128)(2,1)}, u32[]{:S(2)}) copy-start(bf16[256,3840]{1,0:T(8,128)(2,1)} %copy-done) | copy-start | bytes 5898244
  24.9 23.6 %all-to-all-start.1 = ((f32[8,56,256]{2,1,0:T(8,128)}), f32[8,56,256]{2,1,0:T(8,128)S(1)}, u32[]{:S(2)}, u32[]{:S(2)}) async-start(f32[8,56,256]{2,1,0:T(8,128)} %shard_map.30), calls=%async_computation.1 | async-start | bytes 917504 | tf_op jit(solution)/shard_map/all_to_all | solution.py:189
  33.4 18.9 %collective-permute-start.1 = (f32[512,256]{1,0:T(8,128)S(1)}, f32[512,256]{1,0:T(8,128)S(1)}, u32[]{:S(2)}, u32[]{:S(2)}) collective-permute-start(f32[512,256]{1,0:T(8,128)S(1)} %bitcast.5), channel_id=1, source_target_pairs={{3,0},{0,1},{1,2},{2,3},{7,4},{4,5},{5,6},{6,7},{11,8},{8,9},{9,10... | collective-permute-start | bytes 1572872 | tf_op jit(solution)/shard_map/ppermute | solution.py:195
  48.5 1.5 %copy-start.2 = (bf16[256,3840]{1,0:T(8,128)(2,1)S(1)}, bf16[256,3840]{1,0:T(8,128)(2,1)}, u32[]{:S(2)}) copy-start(bf16[256,3840]{1,0:T(8,128)(2,1)} %copy-done) | copy-start | bytes 5898244
  51.2 3.4 %collective-permute-start = (f32[16,256]{1,0:T(8,128)S(1)}, f32[16,256]{1,0:T(8,128)S(1)}, u32[]{:S(2)}, u32[]{:S(2)}) collective-permute-start(f32[16,256]{1,0:T(8,128)S(1)} %shard_map.31.weights_ref), channel_id=1, source_target_pairs={{3,0},{0,1},{1,2},{2,3},{7,4},{4,5},{5,6},{6,7},{11,8},{8,9},{9,10... | collective-permute-start | bytes 49160 | tf_op jit(solution)/shard_map/ppermute | solution.py:195
  59.0 0.8 copy-start.4
  59.8 19.1 %all-to-all-start.2 = ((f32[8,56,256]{2,1,0:T(8,128)}), f32[8,56,256]{2,1,0:T(8,128)S(1)}, u32[]{:S(2)}, u32[]{:S(2)}) async-start(f32[8,56,256]{2,1,0:T(8,128)} %copy-done.4), calls=%async_computation.2 | async-start | bytes 917504 | tf_op jit(solution)/shard_map/all_to_all | solution.py:189
  63.2 17.6 %collective-permute-start.3 = (f32[512,256]{1,0:T(8,128)S(1)}, f32[512,256]{1,0:T(8,128)S(1)}, u32[]{:S(2)}, u32[]{:S(2)}) collective-permute-start(f32[512,256]{1,0:T(8,128)S(1)} %get-tuple-element.16.x_ref), channel_id=1, source_target_pairs={{3,0},{0,1},{1,2},{2,3},{7,4},{4,5},{5,6},{6,7},{11,8},{8,9},{9,10... | collective-permute-start | bytes 1572872 | tf_op jit(solution)/shard_map/ppermute | solution.py:195
  79.9 3.2 %collective-permute-start.2 = (f32[16,256]{1,0:T(8,128)S(1)}, f32[16,256]{1,0:T(8,128)S(1)}, u32[]{:S(2)}, u32[]{:S(2)}) collective-permute-start(f32[16,256]{1,0:T(8,128)S(1)} %shard_map.34.weights_ref), channel_id=1, source_target_pairs={{3,0},{0,1},{1,2},{2,3},{7,4},{4,5},{5,6},{6,7},{11,8},{8,9},{9,10... | collective-permute-start | bytes 49160 | tf_op jit(solution)/shard_map/ppermute | solution.py:195

commit v5 on v4

--- a/solution.py
+++ b/solution.py
@@ -42,50 +42,54 @@
     return cosine, -orient * (tangent * cosine)
 
 
-def write_lines(x, words_ref, table_ref, out_ref):
+def write_lines(x, words_ref, out_ref, moved_ref, lines_ref):
     width = x.shape[1]
     gram = lax.dot_general(
         x, x, (((0,), (0,)), ((), ())), precision=lax.Precision.HIGHEST, preferred_element_type=F32
     )
     parts = pieces(gram)
-    line = lax.broadcasted_iota(jnp.int32, (width, width), 0)
-
-    def picked(value, word):
-        return jnp.where(line == words_ref[word : word + 1], value, 0.0).sum(axis=0, keepdims=True)
-
-    def written(place, value):
-        for i in range(out_ref.shape[0]):
-            out_ref[i, place : place + 1] = value
-
-    written(0, picked(gram, 0))
+    moved_ref[0] = gram
+    for left in range(1, moved_ref.shape[0]):
+        table = one_hot(words_ref[left : left + 1]).astype(BF16)
+        moved_ref[left] = sum(jnp.dot(part, table, preferred_element_type=F32) for part in parts)
+    line = lax.broadcasted_iota(jnp.int32, (8, width), 0)
+
+    def pick(word, places):
+        row = words_ref[word : word + 1]
+        found = [jnp.zeros((8, width), F32) for _ in places]
+        for start in range(0, width, 8):
+            here = line == row - start
+            for i in range(len(places)):
+                found[i] = jnp.where(here, moved_ref[i, start : start + 8], found[i])
+        for value, place in zip(found, places):
+            lines_ref[place : place + 1] = value.sum(axis=0, keepdims=True)
+
+    lines_ref[LINES - 8 :] = jnp.zeros((8, width), F32)
+    pick(0, [0])
     for number in range(ROUNDS):
-        count = 1 << number
-        for right in range(count):
-            column = (count + right - 1) * width
-            moved = sum(
-                jnp.dot(part, table_ref[:, column : column + width], preferred_element_type=F32) for part in parts
-            )
-            for left in range(right + 1):
-                written(place_of(number, left, right), picked(moved, left))
+        for right in range(1 << number):
+            pick((1 << number) + right, [place_of(number, left, right) for left in range(right + 1)])
+    lines = lines_ref[...]
+    for i in range(out_ref.shape[0]):
+        out_ref[i] = lines
 
 
 def place_of(number, left, right):
     return 1 + sum((1 << i) * ((1 << i) + 1) // 2 for i in range(number)) + right * (right + 1) // 2 + left
 
 
-def table_of(table_ref, number):
-    width = table_ref.shape[0]
-    column = ((1 << number) - 1) * width
-    return table_ref[:, column : column + width]
-
-
-def angles_kernel(words_ref, table_ref, part_ref, out_ref, lines_ref, moved_ref, state_ref):
+def table_of(words_ref, number):
+    count = 1 << number
+    return one_hot(words_ref[count : count + 1]).astype(BF16)
+
+
+def angles_kernel(words_ref, part_ref, out_ref, lines_ref, moved_ref, state_ref):
     width = words_ref.shape[1]
     lines = jnp.sum(part_ref[...], axis=0)
     lines_ref[...] = lines
     split = pieces(lines)
-    for number in range(ROUNDS):
-        table = table_of(table_ref, number)
+    tables = [table_of(words_ref, number) for number in range(ROUNDS)]
+    for number, table in enumerate(tables):
         moved_ref[number] = sum(jnp.dot(part, table, preferred_element_type=F32) for part in split)
     indices = lax.broadcasted_iota(jnp.int32, (1, width), 1)
     state_ref[...] = jnp.zeros_like(state_ref)
@@ -96,7 +100,7 @@
         if number:
             for i, value in enumerate([diag] + weights):
                 state_ref[i : i + 1] = value
-            other = permuted(state_ref[...], table_of(table_ref, number))
+            other = permuted(state_ref[...], tables[number])
             diag_2, *weights_2 = (other[i : i + 1] for i in range(1 + count))
         cross = jnp.zeros((1, width), F32)
         for left in range(count):
@@ -114,23 +118,16 @@
         out_ref[i : i + 1] = value
 
 
-def plan_kernel(plan_ref, *out_refs):
+def plan_kernel(plan_ref, *words_refs):
     width = plan_ref.shape[1]
-    steps = len(out_refs) // 2
-    for step in range(steps):
-        words_ref, table_ref = out_refs[step], out_refs[steps + step]
-        words_ref[:1] = lax.broadcasted_iota(jnp.int32, (1, width), 1)
+    for step, words_ref in enumerate(words_refs):
+        words = lax.broadcasted_iota(jnp.int32, (1, width), 1)
         for number in range(ROUNDS):
-            count = 1 << number
             partner = plan_ref[step * ROUNDS + number : step * ROUNDS + number + 1]
-            table = one_hot(partner).astype(BF16)
-            known = words_ref[...].astype(F32).astype(BF16)
-            moved = jnp.dot(known, table, preferred_element_type=F32)
-            for i in range(count):
-                words_ref[count + i : count + i + 1] = moved[i : i + 1].astype(jnp.int32)
-        for word in range(1, WORDS):
-            column = (word - 1) * width
-            table_ref[:, column : column + width] = one_hot(words_ref[word : word + 1]).astype(BF16)
+            known = jnp.concatenate([words] * (WORDS // words.shape[0]), axis=0).astype(F32).astype(BF16)
+            moved = jnp.dot(known, one_hot(partner).astype(BF16), preferred_element_type=F32)
+            words = jnp.concatenate([words, moved[: words.shape[0]].astype(jnp.int32)], axis=0)
+        words_ref[...] = words
 
 
 def sort_kernel(in_ref, out_ref):
@@ -155,8 +152,8 @@
     return jnp.dot(x_ref[...], rotation, precision=lax.Precision.HIGHEST, preferred_element_type=F32)
 
 
-def first_kernel(words_ref, table_ref, x_ref, out_ref):
-    write_lines(x_ref[...], words_ref, table_ref, out_ref)
+def first_kernel(words_ref, x_ref, out_ref, moved_ref, lines_ref):
+    write_lines(x_ref[...], words_ref, out_ref, moved_ref, lines_ref)
 
 
 def top_kernel(words_ref, weights_ref, x_ref, top_ref):
@@ -169,9 +166,11 @@
     y_ref[:, width:] = rotated(words_ref, weights_ref, x_ref, slice(width, 2 * width))
 
 
-def joined_kernel(words_ref, weights_ref, x_ref, top_ref, next_words_ref, next_table_ref, out_ref, y_ref):
+def joined_kernel(
+    words_ref, weights_ref, x_ref, top_ref, next_words_ref, out_ref, y_ref, moved_ref, lines_ref
+):
     bottom_kernel(words_ref, weights_ref, x_ref, top_ref, y_ref)
-    write_lines(y_ref[...], next_words_ref, next_table_ref, out_ref)
+    write_lines(y_ref[...], next_words_ref, out_ref, moved_ref, lines_ref)
 
 
 def call(kernel, outs, *args, scratch=()):
@@ -208,19 +207,18 @@
     lines = matrix.reshape(rows * owners * halves, width)
     x = exchanged(call(sort_kernel, [sorted_rows], lines), OWNERS).reshape(flat[0])
     words_shape = ((WORDS, across), jnp.int32)
-    table_shape = ((across, (WORDS - 1) * across), BF16)
-    plans = call(plan_kernel, [words_shape] * STEPS + [table_shape] * STEPS, plan.reshape(-1, across))
-    words, tables = plans[:STEPS], plans[STEPS:]
-    part = call(first_kernel, [sent], words[0], tables[0], x)
+    cut = [(WORDS // 2, across, across), (LINES, across)]
+    words = call(plan_kernel, [words_shape] * STEPS, plan.reshape(-1, across))
+    part = call(first_kernel, [sent], words[0], x, scratch=cut)
     for step in range(STEPS):
         x_before = passed_along(x, "cols", 1)
         part = exchanged(part, SUMMED)
-        weights = call(angles_kernel, [weights_shape], words[step], tables[step], part, scratch=scratch)
+        weights = call(angles_kernel, [weights_shape], words[step], part, scratch=scratch)
         weights_before = passed_along(weights, "cols", 1)
         top = call(top_kernel, [half], words[step], weights, x)
         args = (words[step], weights_before, x_before, top)
         if step + 1 < STEPS:
-            part, x = call(joined_kernel, [sent, flat], *args, words[step + 1], tables[step + 1])
+            part, x = call(joined_kernel, [sent, flat], *args, words[step + 1], scratch=cut)
         else:
             x = call(bottom_kernel, [flat], *args)
     x = exchanged(x.reshape(sorted_rows[0]), OWNERS)

time: 99.2 us -> 94.2 us (0.950)
  local copies, waits for them, and re-layouts: 6.2 us -> 1.05 us
  waiting for transfers between devices: 42.7 us -> 45.4 us
  Pallas kernels: 17.6 us -> 15.2 us
    unnamed x12 -> x4, local copies, waits for them, and re-layouts: 6.19 us -> 1.04 us
    all_to_all x3, waiting for transfers between devices: 38 us -> 40.7 us  [exchanged(): return lax.all_to_all(value, axis, split_axis=0, concat_axis=0, tiled=True)]
    pallas_call x10, Pallas kernels: 17.6 us -> 15.2 us  [call(): pl.pallas_call(kernel, out_shape=shapes[0] if single else shapes, scratch...]
  transfers between devices with their start and end apart: 7 -> 7, of which waited for: 5 -> 5; matrix products, arithmetic and copies ran while one was open for 0% -> 0% of each run, Pallas kernels for 6% -> 5%
where the time goes in v5:
time: 94.2 us; the launch traced here: 93.7 us
  waiting for transfers between devices  45.4 us (48%)
  starting transfers between devices  18.4 us (20%)
  Pallas kernels  15.2 us (16%)
  blocking collectives  13.7 us (15%)
  local copies, waits for them, and re-layouts  1.05 us (1%)
    all_to_all x3, waiting for transfers between devices, exchanged(): return lax.all_to_all(value, axis, split_axis=0, concat_axis=0, tiled=True)  40.7 us
    all_to_all x3, starting transfers between devices, exchanged(): return lax.all_to_all(value, axis, split_axis=0, concat_axis=0, tiled=True)  18.1 us
    pallas_call x10, Pallas kernels, call(): pl.pallas_call(kernel, out_shape=shapes[0] if single else shapes, scratch...  15.2 us
    all_to_all x1, blocking collectives, exchanged(): return lax.all_to_all(value, axis, split_axis=0, concat_axis=0, tiled=True)  13.7 us
    ppermute x4, waiting for transfers between devices, passed_along(): return lax.ppermute(block, axis, route)  4.7 us
  transfers between devices with their start and end apart: 7, of which 5 were waited for; matrix products, arithmetic and copies ran while one was open for 0% of the time, Pallas kernels for 5%

profile of v5, /device:TPU:8, one launch (start us, length us, event | category | flops | bytes accessed | tf_op | source)
XLA Modules:
  0.0 93.7 jit_solution(6027370892007117358)
XLA Ops:
  0.0 0.0 copy-start
  0.0 1.0 %copy-done = f32[64,8,2,128]{3,2,1,0:T(2,128)S(1)} copy-done((f32[64,8,2,128]{3,2,1,0:T(2,128)S(1)}, f32[64,8,2,128]{3,2,1,0:T(2,128)}, u32[]{:S(2)}) %copy-start) | copy-done | bytes 524312
  1.0 1.0 %shard_map.29 = f32[8,64,256]{2,1,0:T(8,128)} custom-call(f32[1024,128]{1,0:T(8,128)S(1)} %bitcast.8), custom_call_target="tpu_custom_call" | custom-call | tf_op jit(solution)/shard_map/pallas_call | solution.py:179
  2.0 0.0 copy-start.1
  2.0 6.2 %all-to-all-start = ((f32[8,64,256]{2,1,0:T(8,128)}), f32[8,64,256]{2,1,0:T(8,128)S(1)}, u32[]{:S(2)}, u32[]{:S(2)}) async-start(f32[8,64,256]{2,1,0:T(8,128)} %shard_map.29), calls=%async_computation | async-start | bytes 1048576 | tf_op jit(solution)/shard_map/all_to_all | solution.py:188
  8.2 0.0 copy-done.1
  8.2 0.8 shard_map.28
  9.0 10.1 %all-to-all-done = f32[8,64,256]{2,1,0:T(8,128)S(1)} async-done(((f32[8,64,256]{2,1,0:T(8,128)}), f32[8,64,256]{2,1,0:T(8,128)S(1)}, u32[]{:S(2)}, u32[]{:S(2)}) %all-to-all-start) | async-done | bytes 524320 | tf_op jit(solution)/shard_map/all_to_all | solution.py:188
  19.0 3.4 %shard_map.30 = f32[8,56,256]{2,1,0:T(8,128)} custom-call(s32[16,256]{1,0:T(8,128)S(1)} %get-tuple-element.10.words_ref, f32[512,256]{1,0:T(8,128)S(1)} %bitcast.4), custom_call_target="tpu_custom_call" | custom-call | tf_op jit(solution)/shard_map/pallas_call | solution.py:179
  22.5 8.5 %all-to-all-start.1 = ((f32[8,56,256]{2,1,0:T(8,128)}), f32[8,56,256]{2,1,0:T(8,128)S(1)}, u32[]{:S(2)}, u32[]{:S(2)}) async-start(f32[8,56,256]{2,1,0:T(8,128)} %shard_map.30), calls=%async_computation.1 | async-start | bytes 917504 | tf_op jit(solution)/shard_map/all_to_all | solution.py:188
  30.9 0.0 collective-permute-start.1
  30.9 15.1 %all-to-all-done.1.part_ref = f32[8,56,256]{2,1,0:T(8,128)S(1)} async-done(((f32[8,56,256]{2,1,0:T(8,128)}), f32[8,56,256]{2,1,0:T(8,128)S(1)}, u32[]{:S(2)}, u32[]{:S(2)}) %all-to-all-start.1) | async-done | bytes 458784 | tf_op jit(solution)/shard_map/all_to_all | solution.py:188
  46.1 1.1 %shard_map.31.weights_ref = f32[16,256]{1,0:T(8,128)S(1)} custom-call(s32[16,256]{1,0:T(8,128)S(1)} %get-tuple-element.10.words_ref, f32[8,56,256]{2,1,0:T(8,128)S(1)} %all-to-all-done.1.part_ref), custom_call_target="tpu_custom_call" | custom-call | tf_op jit(solution)/shard_map/pallas_call | solution.py:179
  47.2 0.1 collective-permute-start
  47.3 0.8 shard_map.32.top_ref
  48.1 0.0 collective-permute-done.1.x_ref
  48.1 2.3 %collective-permute-done.weights_ref = f32[16,256]{1,0:T(8,128)S(1)} collective-permute-done((f32[16,256]{1,0:T(8,128)S(1)}, f32[16,256]{1,0:T(8,128)S(1)}, u32[]{:S(2)}, u32[]{:S(2)}) %collective-permute-start) | collective-permute-done | bytes 16416 | tf_op jit(solution)/shard_map/ppermute | solution.py:194
  50.4 4.4 %shard_map.33 = (f32[8,56,256]{2,1,0:T(8,128)}, f32[512,256]{1,0:T(8,128)S(1)}) custom-call(s32[16,256]{1,0:T(8,128)S(1)} %get-tuple-element.10.words_ref, f32[16,256]{1,0:T(8,128)S(1)} %collective-permute-done.weights_ref, f32[512,256]{1,0:T(8,128)S(1)} %collective-permute-done.1.x_ref, f32[512,128]{1,0:T(8,128)S(1)} %shard_map.32.top_ref, ...), custom_call_target="tpu_custom_call" | custom-call | tf_op jit(solution)/shard_map/pallas_call | solution.py:179
  54.8 3.5 %all-to-all-start.2 = ((f32[8,56,256]{2,1,0:T(8,128)}), f32[8,56,256]{2,1,0:T(8,128)S(1)}, u32[]{:S(2)}, u32[]{:S(2)}) async-start(f32[8,56,256]{2,1,0:T(8,128)} %get-tuple-element.11), calls=%async_computation.2 | async-start | bytes 917504 | tf_op jit(solution)/shard_map/all_to_all | solution.py:188
  58.3 0.1 collective-permute-start.3
  58.4 15.5 %all-to-all-done.2.part_ref = f32[8,56,256]{2,1,0:T(8,128)S(1)} async-done(((f32[8,56,256]{2,1,0:T(8,128)}), f32[8,56,256]{2,1,0:T(8,128)S(1)}, u32[]{:S(2)}, u32[]{:S(2)}) %all-to-all-start.2) | async-done | bytes 458784 | tf_op jit(solution)/shard_map/all_to_all | solution.py:188
  73.9 1.1 %shard_map.34.weights_ref = f32[16,256]{1,0:T(8,128)S(1)} custom-call(s32[16,256]{1,0:T(8,128)S(1)} %get-tuple-element.9.next_words_ref.words_ref, f32[8,56,256]{2,1,0:T(8,128)S(1)} %all-to-all-done.2.part_ref), custom_call_target="tpu_custom_call" | custom-call | tf_op jit(solution)/shard_map/pallas_call | solution.py:179
  75.0 0.1 collective-permute-start.2
  75.1 0.8 shard_map.35.top_ref
  75.9 0.0 collective-permute-done.3.x_ref
  75.9 2.3 %collective-permute-done.2.weights_ref = f32[16,256]{1,0:T(8,128)S(1)} collective-permute-done((f32[16,256]{1,0:T(8,128)S(1)}, f32[16,256]{1,0:T(8,128)S(1)}, u32[]{:S(2)}, u32[]{:S(2)}) %collective-permute-start.2) | collective-permute-done | bytes 16416 | tf_op jit(solution)/shard_map/ppermute | solution.py:194
  78.2 0.8 shard_map.36
  79.0 13.7 %all_to_all.20.in_ref = f32[8,64,256]{2,1,0:T(8,128)S(1)} all-to-all(f32[8,64,256]{2,1,0:T(8,128)S(1)} %bitcast.7), channel_id=1, replica_groups=mesh['x'=4,'z'=8,'yh'=2,'cols'=4] {'x','yh'}, dimensions={0} | all-to-all | bytes 1048576 | tf_op jit(solution)/shard_map/all_to_all | solution.py:188
  92.7 1.0 %shard_map.37 = f32[1024,128]{1,0:T(8,128)} custom-call(f32[8,64,256]{2,1,0:T(8,128)S(1)} %all_to_all.20.in_ref), custom_call_target="tpu_custom_call" | custom-call | tf_op jit(solution)/shard_map/pallas_call | solution.py:179
  (1 shorter events, 0.0 us)
Async XLA Ops:
  0.0 1.0 %copy-start = (f32[64,8,2,128]{3,2,1,0:T(2,128)S(1)}, f32[64,8,2,128]{3,2,1,0:T(2,128)}, u32[]{:S(2)}) copy-start(f32[64,8,2,128]{3,2,1,0:T(2,128)} %param.2) | copy-start | bytes 1572868
  2.0 6.2 %copy-start.1 = (s32[2,4,256]{2,1,0:T(4,128)S(1)}, s32[2,4,256]{2,1,0:T(4,128)}, u32[]{:S(2)}) copy-start(s32[2,4,256]{2,1,0:T(4,128)} %param.3) | copy-start | bytes 24580
  2.0 17.0 %all-to-all-start = ((f32[8,64,256]{2,1,0:T(8,128)}), f32[8,64,256]{2,1,0:T(8,128)S(1)}, u32[]{:S(2)}, u32[]{:S(2)}) async-start(f32[8,64,256]{2,1,0:T(8,128)} %shard_map.29), calls=%async_computation | async-start | bytes 1048576 | tf_op jit(solution)/shard_map/all_to_all | solution.py:188
  22.5 23.6 %all-to-all-start.1 = ((f32[8,56,256]{2,1,0:T(8,128)}), f32[8,56,256]{2,1,0:T(8,128)S(1)}, u32[]{:S(2)}, u32[]{:S(2)}) async-start(f32[8,56,256]{2,1,0:T(8,128)} %shard_map.30), calls=%async_computation.1 | async-start | bytes 917504 | tf_op jit(solution)/shard_map/all_to_all | solution.py:188
  30.9 17.1 %collective-permute-start.1 = (f32[512,256]{1,0:T(8,128)S(1)}, f32[512,256]{1,0:T(8,128)S(1)}, u32[]{:S(2)}, u32[]{:S(2)}) collective-permute-start(f32[512,256]{1,0:T(8,128)S(1)} %bitcast.5), channel_id=1, source_target_pairs={{3,0},{0,1},{1,2},{2,3},{7,4},{4,5},{5,6},{6,7},{11,8},{8,9},{9,10... | collective-permute-start | bytes 1572872 | tf_op jit(solution)/shard_map/ppermute | solution.py:194
  47.2 3.2 %collective-permute-start = (f32[16,256]{1,0:T(8,128)S(1)}, f32[16,256]{1,0:T(8,128)S(1)}, u32[]{:S(2)}, u32[]{:S(2)}) collective-permute-start(f32[16,256]{1,0:T(8,128)S(1)} %shard_map.31.weights_ref), channel_id=1, source_target_pairs={{3,0},{0,1},{1,2},{2,3},{7,4},{4,5},{5,6},{6,7},{11,8},{8,9},{9,10... | collective-permute-start | bytes 49160 | tf_op jit(solution)/shard_map/ppermute | solution.py:194
  54.8 19.1 %all-to-all-start.2 = ((f32[8,56,256]{2,1,0:T(8,128)}), f32[8,56,256]{2,1,0:T(8,128)S(1)}, u32[]{:S(2)}, u32[]{:S(2)}) async-start(f32[8,56,256]{2,1,0:T(8,128)} %get-tuple-element.11), calls=%async_computation.2 | async-start | bytes 917504 | tf_op jit(solution)/shard_map/all_to_all | solution.py:188
  58.3 17.6 %collective-permute-start.3 = (f32[512,256]{1,0:T(8,128)S(1)}, f32[512,256]{1,0:T(8,128)S(1)}, u32[]{:S(2)}, u32[]{:S(2)}) collective-permute-start(f32[512,256]{1,0:T(8,128)S(1)} %get-tuple-element.12.x_ref), channel_id=1, source_target_pairs={{3,0},{0,1},{1,2},{2,3},{7,4},{4,5},{5,6},{6,7},{11,8},{8,9},{9,10... | collective-permute-start | bytes 1572872 | tf_op jit(solution)/shard_map/ppermute | solution.py:194
  75.0 3.2 %collective-permute-start.2 = (f32[16,256]{1,0:T(8,128)S(1)}, f32[16,256]{1,0:T(8,128)S(1)}, u32[]{:S(2)}, u32[]{:S(2)}) collective-permute-start(f32[16,256]{1,0:T(8,128)S(1)} %shard_map.34.weights_ref), channel_id=1, source_target_pairs={{3,0},{0,1},{1,2},{2,3},{7,4},{4,5},{5,6},{6,7},{11,8},{8,9},{9,10... | collective-permute-start | bytes 49160 | tf_op jit(solution)/shard_map/ppermute | solution.py:194

commit v6 on v5

--- a/solution.py
+++ b/solution.py
@@ -83,7 +83,7 @@
     return one_hot(words_ref[count : count + 1]).astype(BF16)
 
 
-def angles_kernel(words_ref, part_ref, out_ref, lines_ref, moved_ref, state_ref):
+def angles_kernel(words_ref, part_ref, x_ref, out_ref, bottom_ref, lines_ref, moved_ref, state_ref):
     width = words_ref.shape[1]
     lines = jnp.sum(part_ref[...], axis=0)
     lines_ref[...] = lines
@@ -116,6 +116,7 @@
         weights = [cos * value for value in weights] + [sin * value for value in weights_2]
     for i, value in enumerate(weights):
         out_ref[i : i + 1] = value
+    bottom_ref[...] = rotated(words_ref, out_ref, x_ref, slice(width - bottom_ref.shape[1], width))
 
 
 def plan_kernel(plan_ref, *words_refs):
@@ -130,7 +131,8 @@
         words_ref[...] = words
 
 
-def sort_kernel(in_ref, out_ref):
+def sort_kernel(words_ref, in_ref, out_ref):
+    del words_ref
     rows, owners = out_ref.shape[1], out_ref.shape[0]
     for i in range(owners):
         for half in range(2):
@@ -160,17 +162,11 @@
     top_ref[...] = rotated(words_ref, weights_ref, x_ref, slice(0, top_ref.shape[1]))
 
 
-def bottom_kernel(words_ref, weights_ref, x_ref, top_ref, y_ref):
+def joined_kernel(words_ref, top_ref, bottom_ref, out_ref, y_ref, moved_ref, lines_ref):
     width = top_ref.shape[1]
     y_ref[:, :width] = top_ref[...]
-    y_ref[:, width:] = rotated(words_ref, weights_ref, x_ref, slice(width, 2 * width))
-
-
-def joined_kernel(
-    words_ref, weights_ref, x_ref, top_ref, next_words_ref, out_ref, y_ref, moved_ref, lines_ref
-):
-    bottom_kernel(words_ref, weights_ref, x_ref, top_ref, y_ref)
-    write_lines(y_ref[...], next_words_ref, out_ref, moved_ref, lines_ref)
+    y_ref[:, width:] = bottom_ref[...]
+    write_lines(y_ref[...], words_ref, out_ref, moved_ref, lines_ref)
 
 
 def call(kernel, outs, *args, scratch=()):
@@ -205,23 +201,19 @@
     weights_shape = ((WORDS, across), F32)
     scratch = [(LINES, across), (ROUNDS, LINES, across), (16, across)]
     lines = matrix.reshape(rows * owners * halves, width)
-    x = exchanged(call(sort_kernel, [sorted_rows], lines), OWNERS).reshape(flat[0])
     words_shape = ((WORDS, across), jnp.int32)
     cut = [(WORDS // 2, across, across), (LINES, across)]
     words = call(plan_kernel, [words_shape] * STEPS, plan.reshape(-1, across))
+    x = exchanged(call(sort_kernel, [sorted_rows], words[0], lines), OWNERS).reshape(flat[0])
     part = call(first_kernel, [sent], words[0], x, scratch=cut)
     for step in range(STEPS):
-        x_before = passed_along(x, "cols", 1)
         part = exchanged(part, SUMMED)
-        weights = call(angles_kernel, [weights_shape], words[step], part, scratch=scratch)
-        weights_before = passed_along(weights, "cols", 1)
+        weights, bottom = call(angles_kernel, [weights_shape, half], words[step], part, x, scratch=scratch)
+        bottom = passed_along(bottom, "cols", 1)
         top = call(top_kernel, [half], words[step], weights, x)
-        args = (words[step], weights_before, x_before, top)
         if step + 1 < STEPS:
-            part, x = call(joined_kernel, [sent, flat], *args, words[step + 1], scratch=cut)
-        else:
-            x = call(bottom_kernel, [flat], *args)
-    x = exchanged(x.reshape(sorted_rows[0]), OWNERS)
+            part, x = call(joined_kernel, [sent, flat], words[step + 1], top, bottom, scratch=cut)
+    x = exchanged(jnp.concatenate([top, bottom], axis=1).reshape(sorted_rows[0]), OWNERS)
     return call(unsort_kernel, [(lines.shape, F32)], x).reshape(matrix.shape)
 
 

time: 94.2 us -> 96.1 us (1.020)
  blocking collectives: 13.7 us -> 70.8 us
  waiting for transfers between devices: 45.4 us -> 9.98 us
  starting transfers between devices: 18.4 us -> 0.17 us
  Pallas kernels: 15.2 us -> 12.9 us
    all_to_all x1 -> x4, blocking collectives: 13.7 us -> 70.8 us  [exchanged(): return lax.all_to_all(value, axis, split_axis=0, concat_axis=0, tiled=True)]
    all_to_all x3 -> x0, waiting for transfers between devices: 40.7 us -> none  [exchanged(): return lax.all_to_all(value, axis, split_axis=0, concat_axis=0, tiled=True)]
    all_to_all x3 -> x0, starting transfers between devices: 18.1 us -> none  [exchanged(): return lax.all_to_all(value, axis, split_axis=0, concat_axis=0, tiled=True)]
    ppermute x4 -> x2, waiting for transfers between devices: 4.7 us -> 9.98 us  [passed_along(): return lax.ppermute(block, axis, route)]
    pallas_call x10 -> x9, Pallas kernels: 15.2 us -> 12.9 us  [call(): pl.pallas_call(kernel, out_shape=shapes[0] if single else shapes, scratch...]
  transfers between devices with their start and end apart: 7 -> 2, of which waited for: 5 -> 2; matrix products, arithmetic and copies ran while one was open for 0% -> 0% of each run, Pallas kernels for 5% -> 2%
where the time goes in v6:
time: 96.1 us; the launch traced here: 95.7 us
  blocking collectives  70.8 us (74%)
  Pallas kernels  12.9 us (13%)
  waiting for transfers between devices  9.98 us (10%)
  local copies, waits for them, and re-layouts  1.75 us (2%)
    all_to_all x4, blocking collectives, exchanged(): return lax.all_to_all(value, axis, split_axis=0, concat_axis=0, tiled=True)  70.8 us
    pallas_call x9, Pallas kernels, call(): pl.pallas_call(kernel, out_shape=shapes[0] if single else shapes, scratch...  12.9 us
    ppermute x2, waiting for transfers between devices, passed_along(): return lax.ppermute(block, axis, route)  9.98 us
  transfers between devices with their start and end apart: 2, of which 2 were waited for; matrix products, arithmetic and copies ran while one was open for 0% of the time, Pallas kernels for 2%

profile of v6, /device:TPU:8, one launch (start us, length us, event | category | flops | bytes accessed | tf_op | source)
XLA Modules:
  0.0 95.7 jit_solution(15994189881622072808)
XLA Ops:
  0.0 0.7 reshape.15.plan_ref
  0.7 0.8 shard_map.28
  1.5 0.0 copy-start
  1.5 1.0 %copy-done = f32[64,8,2,128]{3,2,1,0:T(2,128)S(1)} copy-done((f32[64,8,2,128]{3,2,1,0:T(2,128)S(1)}, f32[64,8,2,128]{3,2,1,0:T(2,128)}, u32[]{:S(2)}) %copy-start) | copy-done | bytes 524312
  2.5 0.2 shard_map.29
  2.7 17.1 %all_to_all.20 = f32[8,64,256]{2,1,0:T(8,128)S(1)} all-to-all(f32[8,64,256]{2,1,0:T(8,128)S(1)} %shard_map.29), channel_id=1, replica_groups=mesh['x'=4,'z'=8,'yh'=2,'cols'=4] {'x','yh'}, dimensions={0} | all-to-all | bytes 1048576 | tf_op jit(solution)/shard_map/all_to_all | solution.py:184
  19.8 2.6 %shard_map.30 = f32[8,56,256]{2,1,0:T(8,128)S(1)} custom-call(s32[16,256]{1,0:T(8,128)S(1)} %get-tuple-element.14.words_ref, f32[512,256]{1,0:T(8,128)S(1)} %bitcast.4), custom_call_target="tpu_custom_call" | custom-call | tf_op jit(solution)/shard_map/pallas_call | solution.py:175
  22.4 22.6 %all_to_all.21.part_ref = f32[8,56,256]{2,1,0:T(8,128)S(1)} all-to-all(f32[8,56,256]{2,1,0:T(8,128)S(1)} %shard_map.30), channel_id=1, replica_groups=mesh['x'=4,'z'=8,'yh'=2,'cols'=4] {'z'}, dimensions={0} | all-to-all | bytes 917504 | tf_op jit(solution)/shard_map/all_to_all | solution.py:184
  45.0 2.0 %shard_map.31 = (f32[16,256]{1,0:T(8,128)S(1)}, f32[512,128]{1,0:T(8,128)S(1)}) custom-call(s32[16,256]{1,0:T(8,128)S(1)} %get-tuple-element.14.words_ref, f32[8,56,256]{2,1,0:T(8,128)S(1)} %all_to_all.21.part_ref, f32[512,256]{1,0:T(8,128)S(1)} %bitcast.5), custom_call_target="tpu_custom_call" | custom-call | tf_op jit(solution)/shard_map/pallas_call | solution.py:175
  47.0 0.1 collective-permute-start
  47.1 0.8 shard_map.32.top_ref
  47.9 5.0 %collective-permute-done.bottom_ref = f32[512,128]{1,0:T(8,128)S(1)} collective-permute-done((f32[512,128]{1,0:T(8,128)S(1)}, f32[512,128]{1,0:T(8,128)S(1)}, u32[]{:S(2)}, u32[]{:S(2)}) %collective-permute-start) | collective-permute-done | bytes 262176 | tf_op jit(solution)/shard_map/ppermute | solution.py:190
  52.9 2.6 %shard_map.33 = (f32[8,56,256]{2,1,0:T(8,128)S(1)}, f32[512,256]{1,0:T(8,128)S(1)}) custom-call(s32[16,256]{1,0:T(8,128)S(1)} %get-tuple-element.13.words_ref, f32[512,128]{1,0:T(8,128)S(1)} %shard_map.32.top_ref, f32[512,128]{1,0:T(8,128)S(1)} %collective-permute-done.bottom_ref), custom_call_target="tpu_custom_call" | custom-call | tf_op jit(solution)/shard_map/pallas_call | solution.py:175
  55.5 17.9 %all_to_all.22.part_ref = f32[8,56,256]{2,1,0:T(8,128)S(1)} all-to-all(f32[8,56,256]{2,1,0:T(8,128)S(1)} %get-tuple-element.17), channel_id=1, replica_groups=mesh['x'=4,'z'=8,'yh'=2,'cols'=4] {'z'}, dimensions={0} | all-to-all | bytes 917504 | tf_op jit(solution)/shard_map/all_to_all | solution.py:184
  73.5 2.0 %shard_map.34 = (f32[16,256]{1,0:T(8,128)S(1)}, f32[512,128]{1,0:T(8,128)S(1)}) custom-call(s32[16,256]{1,0:T(8,128)S(1)} %get-tuple-element.13.words_ref, f32[8,56,256]{2,1,0:T(8,128)S(1)} %all_to_all.22.part_ref, f32[512,256]{1,0:T(8,128)S(1)} %get-tuple-element.18.x_ref), custom_call_target="tpu_custom_call" | custom-call | tf_op jit(solution)/shard_map/pallas_call | solution.py:175
  75.5 0.1 collective-permute-start.1
  75.6 0.8 shard_map.35
  76.4 5.0 %collective-permute-done.1 = f32[512,128]{1,0:T(8,128)S(1)} collective-permute-done((f32[512,128]{1,0:T(8,128)S(1)}, f32[512,128]{1,0:T(8,128)S(1)}, u32[]{:S(2)}, u32[]{:S(2)}) %collective-permute-start.1) | collective-permute-done | bytes 262176 | tf_op jit(solution)/shard_map/ppermute | solution.py:190
  81.4 13.2 %all_to_all.23.in_ref = f32[8,64,256]{2,1,0:T(8,128)S(1)} all-to-all(f32[8,64,256]{2,1,0:T(8,128)S(1)} %bitcast.8), channel_id=1, replica_groups=mesh['x'=4,'z'=8,'yh'=2,'cols'=4] {'x','yh'}, dimensions={0} | all-to-all | bytes 1048576 | tf_op jit(solution)/shard_map/all_to_all | solution.py:184
  94.7 1.0 %shard_map.36 = f32[1024,128]{1,0:T(8,128)} custom-call(f32[8,64,256]{2,1,0:T(8,128)S(1)} %all_to_all.23.in_ref), custom_call_target="tpu_custom_call" | custom-call | tf_op jit(solution)/shard_map/pallas_call | solution.py:175
  (1 shorter events, 0.0 us)
Async XLA Ops:
  1.5 1.0 %copy-start = (f32[64,8,2,128]{3,2,1,0:T(2,128)S(1)}, f32[64,8,2,128]{3,2,1,0:T(2,128)}, u32[]{:S(2)}) copy-start(f32[64,8,2,128]{3,2,1,0:T(2,128)} %param.2) | copy-start | bytes 1572868
  47.0 5.9 %collective-permute-start = (f32[512,128]{1,0:T(8,128)S(1)}, f32[512,128]{1,0:T(8,128)S(1)}, u32[]{:S(2)}, u32[]{:S(2)}) collective-permute-start(f32[512,128]{1,0:T(8,128)S(1)} %get-tuple-element.16), channel_id=1, source_target_pairs={{3,0},{0,1},{1,2},{2,3},{7,4},{4,5},{5,6},{6,7},{11,8},{8,9},{9,10... | collective-permute-start | bytes 786440 | tf_op jit(solution)/shard_map/ppermute | solution.py:190
  75.5 5.9 %collective-permute-start.1 = (f32[512,128]{1,0:T(8,128)S(1)}, f32[512,128]{1,0:T(8,128)S(1)}, u32[]{:S(2)}, u32[]{:S(2)}) collective-permute-start(f32[512,128]{1,0:T(8,128)S(1)} %get-tuple-element.20), channel_id=1, source_target_pairs={{3,0},{0,1},{1,2},{2,3},{7,4},{4,5},{5,6},{6,7},{11,8},{8,9},{9,10... | collective-permute-start | bytes 786440 | tf_op jit(solution)/shard_map/ppermute | solution.py:190

commit v7 on v5

--- a/solution.py
+++ b/solution.py
@@ -12,7 +12,8 @@
 SUMMED = "z"
 ROUNDS = 4
 WORDS = 1 << ROUNDS
-LINES = 56
+LINES = 48
+CHUNKS = 4
 VMEM_BYTES = 16 * 1024 * 1024
 F32 = jnp.float32
 BF16 = jnp.bfloat16
@@ -54,28 +55,41 @@
         moved_ref[left] = sum(jnp.dot(part, table, preferred_element_type=F32) for part in parts)
     line = lax.broadcasted_iota(jnp.int32, (8, width), 0)
 
-    def pick(word, places):
+    def pick(word, count):
         row = words_ref[word : word + 1]
-        found = [jnp.zeros((8, width), F32) for _ in places]
+        found = [jnp.zeros((8, width), F32) for _ in range(count)]
         for start in range(0, width, 8):
             here = line == row - start
-            for i in range(len(places)):
+            for i in range(count):
                 found[i] = jnp.where(here, moved_ref[i, start : start + 8], found[i])
-        for value, place in zip(found, places):
-            lines_ref[place : place + 1] = value.sum(axis=0, keepdims=True)
+        return [value.sum(axis=0, keepdims=True) for value in found]
+
+    def store(place, value):
+        lines_ref[place : place + 1] = value
 
     lines_ref[LINES - 8 :] = jnp.zeros((8, width), F32)
-    pick(0, [0])
+    store(0, pick(0, 1)[0])
+    indices = lax.broadcasted_iota(jnp.int32, (1, width), 1)
     for number in range(ROUNDS):
-        for right in range(1 << number):
-            pick((1 << number) + right, [place_of(number, left, right) for left in range(right + 1)])
+        count = 1 << number
+        first = indices < words_ref[count : count + 1]
+        for right in range(count):
+            *found, same = pick(count + right, right + 1)
+            for left, value in enumerate(found):
+                store(place_of(number, left, right), value)
+            place = place_of(number, right, right)
+            store(place, jnp.where(first, lines_ref[place : place + 1], same) if right % 2 else same)
     lines = lines_ref[...]
     for i in range(out_ref.shape[0]):
         out_ref[i] = lines
 
 
 def place_of(number, left, right):
-    return 1 + sum((1 << i) * ((1 << i) + 1) // 2 for i in range(number)) + right * (right + 1) // 2 + left
+    count = 1 << number
+    start = (0, 2, 4, 12)[number] if number else 1
+    if left == right:
+        return start + count * (count - 1) // 2 + left // 2
+    return start + right * (right - 1) // 2 + left
 
 
 def table_of(words_ref, number):
@@ -102,15 +116,18 @@
                 state_ref[i : i + 1] = value
             other = permuted(state_ref[...], tables[number])
             diag_2, *weights_2 = (other[i : i + 1] for i in range(1 + count))
+        first = indices < words_ref[count : count + 1]
         cross = jnp.zeros((1, width), F32)
         for left in range(count):
             inner = jnp.zeros((1, width), F32)
             for right in range(count):
                 place = place_of(number, min(left, right), max(left, right))
-                source = lines_ref[place : place + 1] if left <= right else moved_ref[number, place : place + 1]
-                inner += weights_2[right] * source
+                line, moved = lines_ref[place : place + 1], moved_ref[number, place : place + 1]
+                if left == right and number:
+                    line = jnp.where(first, moved, line) if left % 2 else jnp.where(first, line, moved)
+                inner += weights_2[right] * (line if left <= right else moved)
             cross += weights[left] * inner
-        orient = jnp.where(indices < words_ref[count : count + 1], 1.0, -1.0)
+        orient = jnp.where(first, 1.0, -1.0)
         cos, sin = angle(orient, diag, diag_2, cross)
         diag = cos * cos * diag + 2.0 * cos * sin * cross + sin * sin * diag_2
         weights = [cos * value for value in weights] + [sin * value for value in weights_2]
@@ -130,18 +147,75 @@
         words_ref[...] = words
 
 
-def sort_kernel(in_ref, out_ref):
-    rows, owners = out_ref.shape[1], out_ref.shape[0]
-    for i in range(owners):
-        for half in range(2):
-            out_ref[i, :, half * 128 : half * 128 + 128] = in_ref[pl.ds(2 * i + half, rows, 2 * owners), :]
-
-
-def unsort_kernel(in_ref, out_ref):
-    rows, owners = in_ref.shape[1], in_ref.shape[0]
-    for i in range(owners):
-        for half in range(2):
-            out_ref[pl.ds(2 * i + half, rows, 2 * owners), :] = in_ref[i, :, half * 128 : half * 128 + 128]
+def sort_kernel(in_ref, out_ref, held_ref, ready_ref, in_sem, out_sem):
+    owners = out_ref.shape[0]
+    lines, rows = held_ref.shape[1], ready_ref.shape[2]
+    reads = [
+        pltpu.make_async_copy(in_ref.at[pl.ds(i * lines, lines)], held_ref.at[i], in_sem.at[i]) for i in range(CHUNKS)
+    ]
+    writes = [
+        pltpu.make_async_copy(ready_ref.at[i], out_ref.at[:, pl.ds(i * rows, rows)], out_sem.at[i])
+        for i in range(CHUNKS)
+    ]
+    for read in reads:
+        read.start()
+    for i in range(CHUNKS):
+        reads[i].wait()
+        for j in range(2 * owners):
+            half = j % 2 * 128
+            ready_ref[i, j // 2, :, half : half + 128] = held_ref[i, pl.ds(j, rows, 2 * owners), :]
+        writes[i].start()
+    for write in writes:
+        write.wait()
+
+
+def unsort_kernel(in_ref, out_ref, ready_ref, out_sem):
+    owners = in_ref.shape[0]
+    lines = ready_ref.shape[1]
+    rows = lines // (2 * owners)
+    writes = [
+        pltpu.make_async_copy(ready_ref.at[i], out_ref.at[pl.ds(i * lines, lines)], out_sem.at[i])
+        for i in range(CHUNKS)
+    ]
+    for i in range(CHUNKS):
+        for j in range(2 * owners):
+            half = j % 2 * 128
+            ready_ref[i, pl.ds(j, rows, 2 * owners), :] = in_ref[
+                j // 2, i * rows : i * rows + rows, half : half + 128
+            ]
+        writes[i].start()
+    for write in writes:
+        write.wait()
+
+
+def sorted_rows_of(lines, shape):
+    owners, rows, across = shape
+    return pl.pallas_call(
+        sort_kernel,
+        out_shape=pltpu.HBM(shape, F32),
+        in_specs=[pl.BlockSpec(memory_space=pltpu.HBM)],
+        out_specs=pl.BlockSpec(memory_space=pltpu.HBM),
+        scratch_shapes=[
+            pltpu.VMEM((CHUNKS, lines.shape[0] // CHUNKS, lines.shape[1]), F32),
+            pltpu.VMEM((CHUNKS, owners, rows // CHUNKS, across), F32),
+            pltpu.SemaphoreType.DMA((CHUNKS,)),
+            pltpu.SemaphoreType.DMA((CHUNKS,)),
+        ],
+        compiler_params=pltpu.CompilerParams(vmem_limit_bytes=VMEM_BYTES),
+    )(pltpu.with_memory_space_constraint(lines, pltpu.HBM))
+
+
+def lines_from(value, shape):
+    return pl.pallas_call(
+        unsort_kernel,
+        out_shape=pltpu.HBM(shape, F32),
+        out_specs=pl.BlockSpec(memory_space=pltpu.HBM),
+        scratch_shapes=[
+            pltpu.VMEM((CHUNKS, shape[0] // CHUNKS, shape[1]), F32),
+            pltpu.SemaphoreType.DMA((CHUNKS,)),
+        ],
+        compiler_params=pltpu.CompilerParams(vmem_limit_bytes=VMEM_BYTES),
+    )(value)
 
 
 def rotated(words_ref, weights_ref, x_ref, columns):
@@ -200,12 +274,12 @@
     across = halves * width
     flat = ((rows * owners, across), F32)
     half = ((rows * owners, width), F32)
-    sorted_rows = ((owners, rows, across), F32)
+    sorted_rows = (owners, rows, across)
     sent = ((peers, LINES, across), F32)
     weights_shape = ((WORDS, across), F32)
     scratch = [(LINES, across), (ROUNDS, LINES, across), (16, across)]
     lines = matrix.reshape(rows * owners * halves, width)
-    x = exchanged(call(sort_kernel, [sorted_rows], lines), OWNERS).reshape(flat[0])
+    x = exchanged(sorted_rows_of(lines, sorted_rows), OWNERS).reshape(flat[0])
     words_shape = ((WORDS, across), jnp.int32)
     cut = [(WORDS // 2, across, across), (LINES, across)]
     words = call(plan_kernel, [words_shape] * STEPS, plan.reshape(-1, across))
@@ -221,8 +295,8 @@
             part, x = call(joined_kernel, [sent, flat], *args, words[step + 1], scratch=cut)
         else:
             x = call(bottom_kernel, [flat], *args)
-    x = exchanged(x.reshape(sorted_rows[0]), OWNERS)
-    return call(unsort_kernel, [(lines.shape, F32)], x).reshape(matrix.shape)
+    x = exchanged(x.reshape(sorted_rows), OWNERS)
+    return lines_from(x, lines.shape).reshape(matrix.shape)
 
 
 def solution(mesh):

time: 94.2 us -> 90.9 us (0.965)
  waiting for transfers between devices: 45.4 us -> 42.6 us
  local copies, waits for them, and re-layouts: 1.05 us -> 0.02 us
    all_to_all x3, waiting for transfers between devices: 40.7 us -> 37.9 us  [exchanged(): return lax.all_to_all(value, axis, split_axis=0, concat_axis=0, tiled=True)]
    pallas_call x0 -> x2, Pallas kernels: none -> 2.71 us  [the longest x1 1.86 us: sorted_rows_of(): pl.pallas_call(sort_kernel, out_shape=pltpu.HBM(shape, F32), in_specs=[pl...]
    pallas_call x10 -> x8, Pallas kernels: 15.2 us -> 13.1 us  [call(): pl.pallas_call(kernel, out_shape=shapes[0] if single else shapes, scratch...]
    unnamed x4 -> x2, local copies, waits for them, and re-layouts: 1.04 us -> 0.01 us
where the time goes in v7:
time: 90.9 us; the launch traced here: 90.4 us
  waiting for transfers between devices  42.6 us (47%)
  starting transfers between devices  18.2 us (20%)
  Pallas kernels  15.8 us (17%)
  blocking collectives  13.7 us (15%)
    all_to_all x3, waiting for transfers between devices, exchanged(): return lax.all_to_all(value, axis, split_axis=0, concat_axis=0, tiled=True)  37.9 us
    all_to_all x3, starting transfers between devices, exchanged(): return lax.all_to_all(value, axis, split_axis=0, concat_axis=0, tiled=True)  18 us
    all_to_all x1, blocking collectives, exchanged(): return lax.all_to_all(value, axis, split_axis=0, concat_axis=0, tiled=True)  13.7 us
    pallas_call x8, Pallas kernels, call(): pl.pallas_call(kernel, out_shape=shapes[0] if single else shapes, scratch...  13.1 us
    ppermute x4, waiting for transfers between devices, passed_along(): return lax.ppermute(block, axis, route)  4.7 us
    pallas_call x1, Pallas kernels, sorted_rows_of(): pl.pallas_call(sort_kernel, out_shape=pltpu.HBM(shape, F32), in_specs=[pl...  1.86 us
  transfers between devices with their start and end apart: 7, of which 5 were waited for; matrix products, arithmetic and copies ran while one was open for 0% of the time, Pallas kernels for 5%

profile of v7, /device:TPU:8, one launch (start us, length us, event | category | flops | bytes accessed | tf_op | source)
XLA Modules:
  0.0 90.4 jit_solution(7048641728104669597)
XLA Ops:
  0.0 1.9 %shard_map.29 = f32[8,64,256]{2,1,0:T(8,128)} custom-call(f32[1024,128]{1,0:T(8,128)} %bitcast.8), custom_call_target="tpu_custom_call" | custom-call | tf_op jit(solution)/shard_map/pallas_call | solution.py:193
  1.9 0.0 copy-start
  1.9 6.0 %all-to-all-start = ((f32[8,64,256]{2,1,0:T(8,128)}), f32[8,64,256]{2,1,0:T(8,128)S(1)}, u32[]{:S(2)}, u32[]{:S(2)}) async-start(f32[8,64,256]{2,1,0:T(8,128)} %shard_map.29), calls=%async_computation | async-start | bytes 1048576 | tf_op jit(solution)/shard_map/all_to_all | solution.py:262
  7.9 0.0 copy-done
  7.9 0.8 shard_map.28
  8.7 10.1 %all-to-all-done = f32[8,64,256]{2,1,0:T(8,128)S(1)} async-done(((f32[8,64,256]{2,1,0:T(8,128)}), f32[8,64,256]{2,1,0:T(8,128)S(1)}, u32[]{:S(2)}, u32[]{:S(2)}) %all-to-all-start) | async-done | bytes 524320 | tf_op jit(solution)/shard_map/all_to_all | solution.py:262
  18.8 3.5 %shard_map.30 = f32[8,48,256]{2,1,0:T(8,128)} custom-call(s32[16,256]{1,0:T(8,128)S(1)} %get-tuple-element.10.words_ref, f32[512,256]{1,0:T(8,128)S(1)} %bitcast.4), custom_call_target="tpu_custom_call" | custom-call | tf_op jit(solution)/shard_map/pallas_call | solution.py:253
  22.3 8.5 %all-to-all-start.1 = ((f32[8,48,256]{2,1,0:T(8,128)}), f32[8,48,256]{2,1,0:T(8,128)S(1)}, u32[]{:S(2)}, u32[]{:S(2)}) async-start(f32[8,48,256]{2,1,0:T(8,128)} %shard_map.30), calls=%async_computation.1 | async-start | bytes 786432 | tf_op jit(solution)/shard_map/all_to_all | solution.py:262
  30.7 0.0 collective-permute-start.1
  30.7 13.7 %all-to-all-done.1.part_ref = f32[8,48,256]{2,1,0:T(8,128)S(1)} async-done(((f32[8,48,256]{2,1,0:T(8,128)}), f32[8,48,256]{2,1,0:T(8,128)S(1)}, u32[]{:S(2)}, u32[]{:S(2)}) %all-to-all-start.1) | async-done | bytes 393248 | tf_op jit(solution)/shard_map/all_to_all | solution.py:262
  44.5 1.1 %shard_map.31.weights_ref = f32[16,256]{1,0:T(8,128)S(1)} custom-call(s32[16,256]{1,0:T(8,128)S(1)} %get-tuple-element.10.words_ref, f32[8,48,256]{2,1,0:T(8,128)S(1)} %all-to-all-done.1.part_ref), custom_call_target="tpu_custom_call" | custom-call | tf_op jit(solution)/shard_map/pallas_call | solution.py:253
  45.6 0.1 collective-permute-start
  45.7 0.8 shard_map.32.top_ref
  46.5 0.0 collective-permute-done.1.x_ref
  46.5 2.3 %collective-permute-done.weights_ref = f32[16,256]{1,0:T(8,128)S(1)} collective-permute-done((f32[16,256]{1,0:T(8,128)S(1)}, f32[16,256]{1,0:T(8,128)S(1)}, u32[]{:S(2)}, u32[]{:S(2)}) %collective-permute-start) | collective-permute-done | bytes 16416 | tf_op jit(solution)/shard_map/ppermute | solution.py:268
  48.8 4.3 %shard_map.33 = (f32[8,48,256]{2,1,0:T(8,128)}, f32[512,256]{1,0:T(8,128)S(1)}) custom-call(s32[16,256]{1,0:T(8,128)S(1)} %get-tuple-element.10.words_ref, f32[16,256]{1,0:T(8,128)S(1)} %collective-permute-done.weights_ref, f32[512,256]{1,0:T(8,128)S(1)} %collective-permute-done.1.x_ref, f32[512,128]{1,0:T(8,128)S(1)} %shard_map.32.top_ref, ...), custom_call_target="tpu_custom_call" | custom-call | tf_op jit(solution)/shard_map/pallas_call | solution.py:253
  53.1 3.5 %all-to-all-start.2 = ((f32[8,48,256]{2,1,0:T(8,128)}), f32[8,48,256]{2,1,0:T(8,128)S(1)}, u32[]{:S(2)}, u32[]{:S(2)}) async-start(f32[8,48,256]{2,1,0:T(8,128)} %get-tuple-element.11), calls=%async_computation.2 | async-start | bytes 786432 | tf_op jit(solution)/shard_map/all_to_all | solution.py:262
  56.6 0.1 collective-permute-start.3
  56.7 14.1 %all-to-all-done.2.part_ref = f32[8,48,256]{2,1,0:T(8,128)S(1)} async-done(((f32[8,48,256]{2,1,0:T(8,128)}), f32[8,48,256]{2,1,0:T(8,128)S(1)}, u32[]{:S(2)}, u32[]{:S(2)}) %all-to-all-start.2) | async-done | bytes 393248 | tf_op jit(solution)/shard_map/all_to_all | solution.py:262
  70.8 1.1 %shard_map.34.weights_ref = f32[16,256]{1,0:T(8,128)S(1)} custom-call(s32[16,256]{1,0:T(8,128)S(1)} %get-tuple-element.9.next_words_ref.words_ref, f32[8,48,256]{2,1,0:T(8,128)S(1)} %all-to-all-done.2.part_ref), custom_call_target="tpu_custom_call" | custom-call | tf_op jit(solution)/shard_map/pallas_call | solution.py:253
  71.9 0.1 collective-permute-start.2
  72.0 0.8 shard_map.35.top_ref
  72.8 0.0 collective-permute-done.3.x_ref
  72.8 2.3 %collective-permute-done.2.weights_ref = f32[16,256]{1,0:T(8,128)S(1)} collective-permute-done((f32[16,256]{1,0:T(8,128)S(1)}, f32[16,256]{1,0:T(8,128)S(1)}, u32[]{:S(2)}, u32[]{:S(2)}) %collective-permute-start.2) | collective-permute-done | bytes 16416 | tf_op jit(solution)/shard_map/ppermute | solution.py:268
  75.1 0.8 shard_map.36
  75.9 13.7 %all_to_all.20.in_ref = f32[8,64,256]{2,1,0:T(8,128)S(1)} all-to-all(f32[8,64,256]{2,1,0:T(8,128)S(1)} %bitcast.7), channel_id=1, replica_groups=mesh['x'=4,'z'=8,'yh'=2,'cols'=4] {'x','yh'}, dimensions={0} | all-to-all | bytes 1048576 | tf_op jit(solution)/shard_map/all_to_all | solution.py:262
  89.6 0.9 shard_map.37
  (1 shorter events, 0.0 us)
Async XLA Ops:
  1.9 6.1 %copy-start = (s32[2,4,256]{2,1,0:T(4,128)S(1)}, s32[2,4,256]{2,1,0:T(4,128)}, u32[]{:S(2)}) copy-start(s32[2,4,256]{2,1,0:T(4,128)} %param.3) | copy-start | bytes 24580
  1.9 16.9 %all-to-all-start = ((f32[8,64,256]{2,1,0:T(8,128)}), f32[8,64,256]{2,1,0:T(8,128)S(1)}, u32[]{:S(2)}, u32[]{:S(2)}) async-start(f32[8,64,256]{2,1,0:T(8,128)} %shard_map.29), calls=%async_computation | async-start | bytes 1048576 | tf_op jit(solution)/shard_map/all_to_all | solution.py:262
  22.3 22.2 %all-to-all-start.1 = ((f32[8,48,256]{2,1,0:T(8,128)}), f32[8,48,256]{2,1,0:T(8,128)S(1)}, u32[]{:S(2)}, u32[]{:S(2)}) async-start(f32[8,48,256]{2,1,0:T(8,128)} %shard_map.30), calls=%async_computation.1 | async-start | bytes 786432 | tf_op jit(solution)/shard_map/all_to_all | solution.py:262
  30.7 15.7 %collective-permute-start.1 = (f32[512,256]{1,0:T(8,128)S(1)}, f32[512,256]{1,0:T(8,128)S(1)}, u32[]{:S(2)}, u32[]{:S(2)}) collective-permute-start(f32[512,256]{1,0:T(8,128)S(1)} %bitcast.5), channel_id=1, source_target_pairs={{3,0},{0,1},{1,2},{2,3},{7,4},{4,5},{5,6},{6,7},{11,8},{8,9},{9,10... | collective-permute-start | bytes 1572872 | tf_op jit(solution)/shard_map/ppermute | solution.py:268
  45.6 3.2 %collective-permute-start = (f32[16,256]{1,0:T(8,128)S(1)}, f32[16,256]{1,0:T(8,128)S(1)}, u32[]{:S(2)}, u32[]{:S(2)}) collective-permute-start(f32[16,256]{1,0:T(8,128)S(1)} %shard_map.31.weights_ref), channel_id=1, source_target_pairs={{3,0},{0,1},{1,2},{2,3},{7,4},{4,5},{5,6},{6,7},{11,8},{8,9},{9,10... | collective-permute-start | bytes 49160 | tf_op jit(solution)/shard_map/ppermute | solution.py:268
  53.1 17.7 %all-to-all-start.2 = ((f32[8,48,256]{2,1,0:T(8,128)}), f32[8,48,256]{2,1,0:T(8,128)S(1)}, u32[]{:S(2)}, u32[]{:S(2)}) async-start(f32[8,48,256]{2,1,0:T(8,128)} %get-tuple-element.11), calls=%async_computation.2 | async-start | bytes 786432 | tf_op jit(solution)/shard_map/all_to_all | solution.py:262
  56.6 16.2 %collective-permute-start.3 = (f32[512,256]{1,0:T(8,128)S(1)}, f32[512,256]{1,0:T(8,128)S(1)}, u32[]{:S(2)}, u32[]{:S(2)}) collective-permute-start(f32[512,256]{1,0:T(8,128)S(1)} %get-tuple-element.12.x_ref), channel_id=1, source_target_pairs={{3,0},{0,1},{1,2},{2,3},{7,4},{4,5},{5,6},{6,7},{11,8},{8,9},{9,10... | collective-permute-start | bytes 1572872 | tf_op jit(solution)/shard_map/ppermute | solution.py:268
  71.9 3.2 %collective-permute-start.2 = (f32[16,256]{1,0:T(8,128)S(1)}, f32[16,256]{1,0:T(8,128)S(1)}, u32[]{:S(2)}, u32[]{:S(2)}) collective-permute-start(f32[16,256]{1,0:T(8,128)S(1)} %shard_map.34.weights_ref), channel_id=1, source_target_pairs={{3,0},{0,1},{1,2},{2,3},{7,4},{4,5},{5,6},{6,7},{11,8},{8,9},{9,10... | collective-permute-start | bytes 49160 | tf_op jit(solution)/shard_map/ppermute | solution.py:268

commit v8 on v7

--- a/solution.py
+++ b/solution.py
@@ -12,7 +12,8 @@
 SUMMED = "z"
 ROUNDS = 4
 WORDS = 1 << ROUNDS
-LINES = 48
+LINES = 44
+SENT = ((0, 24), (24, 64), (64, 88))
 CHUNKS = 4
 VMEM_BYTES = 16 * 1024 * 1024
 F32 = jnp.float32
@@ -43,7 +44,7 @@
     return cosine, -orient * (tangent * cosine)
 
 
-def write_lines(x, words_ref, out_ref, moved_ref, lines_ref):
+def write_lines(x, words_ref, out_ref, moved_ref, lines_ref, sem):
     width = x.shape[1]
     gram = lax.dot_general(
         x, x, (((0,), (0,)), ((), ())), precision=lax.Precision.HIGHEST, preferred_element_type=F32
@@ -65,9 +66,22 @@
         return [value.sum(axis=0, keepdims=True) for value in found]
 
     def store(place, value):
-        lines_ref[place : place + 1] = value
-
-    lines_ref[LINES - 8 :] = jnp.zeros((8, width), F32)
+        lines_ref[2 * place : 2 * place + 1] = value[:, : width // 2]
+        lines_ref[2 * place + 1 : 2 * place + 2] = value[:, width // 2 :]
+
+    def loaded(place):
+        halves = (lines_ref[2 * place : 2 * place + 1], lines_ref[2 * place + 1 : 2 * place + 2])
+        return jnp.concatenate(halves, axis=1)
+
+    copies = []
+
+    def send(group):
+        start, end = SENT[group]
+        rows = pl.ds(start, end - start)
+        for i in range(out_ref.shape[0]):
+            copies.append(pltpu.make_async_copy(lines_ref.at[rows], out_ref.at[i, rows], sem.at[group, i]))
+            copies[-1].start()
+
     store(0, pick(0, 1)[0])
     indices = lax.broadcasted_iota(jnp.int32, (1, width), 1)
     for number in range(ROUNDS):
@@ -78,10 +92,14 @@
             for left, value in enumerate(found):
                 store(place_of(number, left, right), value)
             place = place_of(number, right, right)
-            store(place, jnp.where(first, lines_ref[place : place + 1], same) if right % 2 else same)
-    lines = lines_ref[...]
-    for i in range(out_ref.shape[0]):
-        out_ref[i] = lines
+            store(place, jnp.where(first, loaded(place), same) if right % 2 else same)
+            if number == 3 and right == 6:
+                send(1)
+        if number == 2:
+            send(0)
+    send(2)
+    for copy in copies:
+        copy.wait()
 
 
 def place_of(number, left, right):
@@ -97,11 +115,14 @@
     return one_hot(words_ref[count : count + 1]).astype(BF16)
 
 
-def angles_kernel(words_ref, part_ref, out_ref, lines_ref, moved_ref, state_ref):
+def angles_kernel(words_ref, part_ref, out_ref, sum_ref, lines_ref, moved_ref, state_ref):
     width = words_ref.shape[1]
-    lines = jnp.sum(part_ref[...], axis=0)
-    lines_ref[...] = lines
-    split = pieces(lines)
+    sum_ref[...] = jnp.sum(part_ref[...], axis=0)
+    lines_ref[LINES:] = jnp.zeros((lines_ref.shape[0] - LINES, width), F32)
+    for half in range(2):
+        columns = slice(half * width // 2, (half + 1) * width // 2)
+        lines_ref[:LINES, columns] = sum_ref[pl.ds(half, LINES, 2), :]
+    split = pieces(lines_ref[...])
     tables = [table_of(words_ref, number) for number in range(ROUNDS)]
     for number, table in enumerate(tables):
         moved_ref[number] = sum(jnp.dot(part, table, preferred_element_type=F32) for part in split)
@@ -226,8 +247,8 @@
     return jnp.dot(x_ref[...], rotation, precision=lax.Precision.HIGHEST, preferred_element_type=F32)
 
 
-def first_kernel(words_ref, x_ref, out_ref, moved_ref, lines_ref):
-    write_lines(x_ref[...], words_ref, out_ref, moved_ref, lines_ref)
+def first_kernel(words_ref, x_ref, out_ref, moved_ref, lines_ref, sem):
+    write_lines(x_ref[...], words_ref, out_ref, moved_ref, lines_ref, sem)
 
 
 def top_kernel(words_ref, weights_ref, x_ref, top_ref):
@@ -241,10 +262,10 @@
 
 
 def joined_kernel(
-    words_ref, weights_ref, x_ref, top_ref, next_words_ref, out_ref, y_ref, moved_ref, lines_ref
+    words_ref, weights_ref, x_ref, top_ref, next_words_ref, out_ref, y_ref, moved_ref, lines_ref, sem
 ):
     bottom_kernel(words_ref, weights_ref, x_ref, top_ref, y_ref)
-    write_lines(y_ref[...], next_words_ref, out_ref, moved_ref, lines_ref)
+    write_lines(y_ref[...], next_words_ref, out_ref, moved_ref, lines_ref, sem)
 
 
 def call(kernel, outs, *args, scratch=()):
@@ -258,6 +279,21 @@
     )(*args)
 
 
+def call_with_lines(kernel, sent, outs, *args):
+    across = sent[1] * sent[2] // LINES
+    return pl.pallas_call(
+        kernel,
+        out_shape=[pltpu.HBM(sent, F32)] + [jax.ShapeDtypeStruct(shape, F32) for shape in outs],
+        out_specs=[pl.BlockSpec(memory_space=pltpu.HBM)] + [pl.BlockSpec(memory_space=pltpu.VMEM) for _ in outs],
+        scratch_shapes=[
+            pltpu.VMEM((WORDS // 2, across, across), F32),
+            pltpu.VMEM(sent[1:], F32),
+            pltpu.SemaphoreType.DMA((len(SENT), sent[0])),
+        ],
+        compiler_params=pltpu.CompilerParams(vmem_limit_bytes=VMEM_BYTES),
+    )(*args)
+
+
 def exchanged(value, axis):
     return lax.all_to_all(value, axis, split_axis=0, concat_axis=0, tiled=True)
 
@@ -275,15 +311,14 @@
     flat = ((rows * owners, across), F32)
     half = ((rows * owners, width), F32)
     sorted_rows = (owners, rows, across)
-    sent = ((peers, LINES, across), F32)
+    sent = (peers, 2 * LINES, across // 2)
     weights_shape = ((WORDS, across), F32)
-    scratch = [(LINES, across), (ROUNDS, LINES, across), (16, across)]
+    scratch = [sent[1:], (48, across), (ROUNDS, 48, across), (16, across)]
     lines = matrix.reshape(rows * owners * halves, width)
     x = exchanged(sorted_rows_of(lines, sorted_rows), OWNERS).reshape(flat[0])
     words_shape = ((WORDS, across), jnp.int32)
-    cut = [(WORDS // 2, across, across), (LINES, across)]
     words = call(plan_kernel, [words_shape] * STEPS, plan.reshape(-1, across))
-    part = call(first_kernel, [sent], words[0], x, scratch=cut)
+    part = call_with_lines(first_kernel, sent, [], words[0], x)[0]
     for step in range(STEPS):
         x_before = passed_along(x, "cols", 1)
         part = exchanged(part, SUMMED)
@@ -292,7 +327,7 @@
         top = call(top_kernel, [half], words[step], weights, x)
         args = (words[step], weights_before, x_before, top)
         if step + 1 < STEPS:
-            part, x = call(joined_kernel, [sent, flat], *args, words[step + 1], scratch=cut)
+            part, x = call_with_lines(joined_kernel, sent, [flat[0]], *args, words[step + 1])
         else:
             x = call(bottom_kernel, [flat], *args)
     x = exchanged(x.reshape(sorted_rows), OWNERS)

time: 90.9 us -> 89.6 us (0.986)
  waiting for transfers between devices: 42.6 us -> 41.2 us
    pallas_call x0 -> x2, Pallas kernels: none -> 7.86 us  [call_with_lines(): pl.pallas_call(kernel, out_shape=[pltpu.HBM(sent, F32)] + [jax.ShapeDtype...]
    pallas_call x8 -> x6, Pallas kernels: 13.1 us -> 5.35 us  [call(): pl.pallas_call(kernel, out_shape=shapes[0] if single else shapes, scratch...]
    all_to_all x3, waiting for transfers between devices: 37.9 us -> 36.5 us  [exchanged(): return lax.all_to_all(value, axis, split_axis=0, concat_axis=0, tiled=True)]
where the time goes in v8:
time: 89.6 us; the launch traced here: 89.1 us
  waiting for transfers between devices  41.2 us (46%)
  starting transfers between devices  18.2 us (20%)
  Pallas kernels  15.9 us (18%)
  blocking collectives  13.7 us (15%)
    all_to_all x3, waiting for transfers between devices, exchanged(): return lax.all_to_all(value, axis, split_axis=0, concat_axis=0, tiled=True)  36.5 us
    all_to_all x3, starting transfers between devices, exchanged(): return lax.all_to_all(value, axis, split_axis=0, concat_axis=0, tiled=True)  18 us
    all_to_all x1, blocking collectives, exchanged(): return lax.all_to_all(value, axis, split_axis=0, concat_axis=0, tiled=True)  13.7 us
    pallas_call x2, Pallas kernels, call_with_lines(): pl.pallas_call(kernel, out_shape=[pltpu.HBM(sent, F32)] + [jax.ShapeDtype...  7.86 us
    pallas_call x6, Pallas kernels, call(): pl.pallas_call(kernel, out_shape=shapes[0] if single else shapes, scratch...  5.35 us
    ppermute x4, waiting for transfers between devices, passed_along(): return lax.ppermute(block, axis, route)  4.7 us
    pallas_call x1, Pallas kernels, sorted_rows_of(): pl.pallas_call(sort_kernel, out_shape=pltpu.HBM(shape, F32), in_specs=[pl...  1.86 us
  transfers between devices with their start and end apart: 7, of which 5 were waited for; matrix products, arithmetic and copies ran while one was open for 0% of the time, Pallas kernels for 5%

profile of v8, /device:TPU:8, one launch (start us, length us, event | category | flops | bytes accessed | tf_op | source)
XLA Modules:
  0.0 89.1 jit_solution(15496331444286633724)
XLA Ops:
  0.0 1.9 %shard_map.29 = f32[8,64,256]{2,1,0:T(8,128)} custom-call(f32[1024,128]{1,0:T(8,128)} %bitcast.8), custom_call_target="tpu_custom_call" | custom-call | tf_op jit(solution)/shard_map/pallas_call | solution.py:214
  1.9 0.0 copy-start
  1.9 6.0 %all-to-all-start = ((f32[8,64,256]{2,1,0:T(8,128)}), f32[8,64,256]{2,1,0:T(8,128)S(1)}, u32[]{:S(2)}, u32[]{:S(2)}) async-start(f32[8,64,256]{2,1,0:T(8,128)} %shard_map.29), calls=%async_computation | async-start | bytes 1048576 | tf_op jit(solution)/shard_map/all_to_all | solution.py:298
  7.9 0.0 copy-done
  7.9 0.8 shard_map.28
  8.7 10.1 %all-to-all-done = f32[8,64,256]{2,1,0:T(8,128)S(1)} async-done(((f32[8,64,256]{2,1,0:T(8,128)}), f32[8,64,256]{2,1,0:T(8,128)S(1)}, u32[]{:S(2)}, u32[]{:S(2)}) %all-to-all-start) | async-done | bytes 524320 | tf_op jit(solution)/shard_map/all_to_all | solution.py:298
  18.8 3.5 %shard_map.30 = f32[8,88,128]{2,1,0:T(8,128)} custom-call(s32[16,256]{1,0:T(8,128)S(1)} %get-tuple-element.10.words_ref, f32[512,256]{1,0:T(8,128)S(1)} %bitcast.4), custom_call_target="tpu_custom_call" | custom-call | tf_op jit(solution)/shard_map/pallas_call | solution.py:284
  22.3 8.5 %all-to-all-start.1 = ((f32[8,88,128]{2,1,0:T(8,128)}), f32[8,88,128]{2,1,0:T(8,128)S(1)}, u32[]{:S(2)}, u32[]{:S(2)}) async-start(f32[8,88,128]{2,1,0:T(8,128)} %shard_map.30), calls=%async_computation.1 | async-start | bytes 720896 | tf_op jit(solution)/shard_map/all_to_all | solution.py:298
  30.8 0.0 collective-permute-start.1
  30.8 13.0 %all-to-all-done.1.part_ref = f32[8,88,128]{2,1,0:T(8,128)S(1)} async-done(((f32[8,88,128]{2,1,0:T(8,128)}), f32[8,88,128]{2,1,0:T(8,128)S(1)}, u32[]{:S(2)}, u32[]{:S(2)}) %all-to-all-start.1) | async-done | bytes 360480 | tf_op jit(solution)/shard_map/all_to_all | solution.py:298
  43.8 1.1 %shard_map.31.weights_ref = f32[16,256]{1,0:T(8,128)S(1)} custom-call(s32[16,256]{1,0:T(8,128)S(1)} %get-tuple-element.10.words_ref, f32[8,88,128]{2,1,0:T(8,128)S(1)} %all-to-all-done.1.part_ref), custom_call_target="tpu_custom_call" | custom-call | tf_op jit(solution)/shard_map/pallas_call | solution.py:274
  44.9 0.1 collective-permute-start
  45.0 0.8 shard_map.32.top_ref
  45.8 0.0 collective-permute-done.1.x_ref
  45.8 2.3 %collective-permute-done.weights_ref = f32[16,256]{1,0:T(8,128)S(1)} collective-permute-done((f32[16,256]{1,0:T(8,128)S(1)}, f32[16,256]{1,0:T(8,128)S(1)}, u32[]{:S(2)}, u32[]{:S(2)}) %collective-permute-start) | collective-permute-done | bytes 16416 | tf_op jit(solution)/shard_map/ppermute | solution.py:304
  48.2 4.4 %shard_map.33 = (f32[8,88,128]{2,1,0:T(8,128)}, f32[512,256]{1,0:T(8,128)S(1)}) custom-call(s32[16,256]{1,0:T(8,128)S(1)} %get-tuple-element.10.words_ref, f32[16,256]{1,0:T(8,128)S(1)} %collective-permute-done.weights_ref, f32[512,256]{1,0:T(8,128)S(1)} %collective-permute-done.1.x_ref, f32[512,128]{1,0:T(8,128)S(1)} %shard_map.32.top_ref, ...), custom_call_target="tpu_custom_call" | custom-call | tf_op jit(solution)/shard_map/pallas_call | solution.py:284
  52.5 3.5 %all-to-all-start.2 = ((f32[8,88,128]{2,1,0:T(8,128)}), f32[8,88,128]{2,1,0:T(8,128)S(1)}, u32[]{:S(2)}, u32[]{:S(2)}) async-start(f32[8,88,128]{2,1,0:T(8,128)} %get-tuple-element.11), calls=%async_computation.2 | async-start | bytes 720896 | tf_op jit(solution)/shard_map/all_to_all | solution.py:298
  56.0 0.1 collective-permute-start.3
  56.1 13.4 %all-to-all-done.2.part_ref = f32[8,88,128]{2,1,0:T(8,128)S(1)} async-done(((f32[8,88,128]{2,1,0:T(8,128)}), f32[8,88,128]{2,1,0:T(8,128)S(1)}, u32[]{:S(2)}, u32[]{:S(2)}) %all-to-all-start.2) | async-done | bytes 360480 | tf_op jit(solution)/shard_map/all_to_all | solution.py:298
  69.5 1.1 %shard_map.34.weights_ref = f32[16,256]{1,0:T(8,128)S(1)} custom-call(s32[16,256]{1,0:T(8,128)S(1)} %get-tuple-element.9.next_words_ref.words_ref, f32[8,88,128]{2,1,0:T(8,128)S(1)} %all-to-all-done.2.part_ref), custom_call_target="tpu_custom_call" | custom-call | tf_op jit(solution)/shard_map/pallas_call | solution.py:274
  70.6 0.1 collective-permute-start.2
  70.7 0.8 shard_map.35.top_ref
  71.5 0.0 collective-permute-done.3.x_ref
  71.5 2.3 %collective-permute-done.2.weights_ref = f32[16,256]{1,0:T(8,128)S(1)} collective-permute-done((f32[16,256]{1,0:T(8,128)S(1)}, f32[16,256]{1,0:T(8,128)S(1)}, u32[]{:S(2)}, u32[]{:S(2)}) %collective-permute-start.2) | collective-permute-done | bytes 16416 | tf_op jit(solution)/shard_map/ppermute | solution.py:304
  73.8 0.8 shard_map.36
  74.6 13.7 %all_to_all.20.in_ref = f32[8,64,256]{2,1,0:T(8,128)S(1)} all-to-all(f32[8,64,256]{2,1,0:T(8,128)S(1)} %bitcast.7), channel_id=1, replica_groups=mesh['x'=4,'z'=8,'yh'=2,'cols'=4] {'x','yh'}, dimensions={0} | all-to-all | bytes 1048576 | tf_op jit(solution)/shard_map/all_to_all | solution.py:298
  88.3 0.9 shard_map.37
  (1 shorter events, 0.0 us)
Async XLA Ops:
  1.9 6.1 %copy-start = (s32[2,4,256]{2,1,0:T(4,128)S(1)}, s32[2,4,256]{2,1,0:T(4,128)}, u32[]{:S(2)}) copy-start(s32[2,4,256]{2,1,0:T(4,128)} %param.3) | copy-start | bytes 24580
  1.9 16.9 %all-to-all-start = ((f32[8,64,256]{2,1,0:T(8,128)}), f32[8,64,256]{2,1,0:T(8,128)S(1)}, u32[]{:S(2)}, u32[]{:S(2)}) async-start(f32[8,64,256]{2,1,0:T(8,128)} %shard_map.29), calls=%async_computation | async-start | bytes 1048576 | tf_op jit(solution)/shard_map/all_to_all | solution.py:298
  22.3 21.5 %all-to-all-start.1 = ((f32[8,88,128]{2,1,0:T(8,128)}), f32[8,88,128]{2,1,0:T(8,128)S(1)}, u32[]{:S(2)}, u32[]{:S(2)}) async-start(f32[8,88,128]{2,1,0:T(8,128)} %shard_map.30), calls=%async_computation.1 | async-start | bytes 720896 | tf_op jit(solution)/shard_map/all_to_all | solution.py:298
  30.8 15.0 %collective-permute-start.1 = (f32[512,256]{1,0:T(8,128)S(1)}, f32[512,256]{1,0:T(8,128)S(1)}, u32[]{:S(2)}, u32[]{:S(2)}) collective-permute-start(f32[512,256]{1,0:T(8,128)S(1)} %bitcast.5), channel_id=1, source_target_pairs={{3,0},{0,1},{1,2},{2,3},{7,4},{4,5},{5,6},{6,7},{11,8},{8,9},{9,10... | collective-permute-start | bytes 1572872 | tf_op jit(solution)/shard_map/ppermute | solution.py:304
  44.9 3.2 %collective-permute-start = (f32[16,256]{1,0:T(8,128)S(1)}, f32[16,256]{1,0:T(8,128)S(1)}, u32[]{:S(2)}, u32[]{:S(2)}) collective-permute-start(f32[16,256]{1,0:T(8,128)S(1)} %shard_map.31.weights_ref), channel_id=1, source_target_pairs={{3,0},{0,1},{1,2},{2,3},{7,4},{4,5},{5,6},{6,7},{11,8},{8,9},{9,10... | collective-permute-start | bytes 49160 | tf_op jit(solution)/shard_map/ppermute | solution.py:304
  52.5 17.0 %all-to-all-start.2 = ((f32[8,88,128]{2,1,0:T(8,128)}), f32[8,88,128]{2,1,0:T(8,128)S(1)}, u32[]{:S(2)}, u32[]{:S(2)}) async-start(f32[8,88,128]{2,1,0:T(8,128)} %get-tuple-element.11), calls=%async_computation.2 | async-start | bytes 720896 | tf_op jit(solution)/shard_map/all_to_all | solution.py:298
  56.0 15.5 %collective-permute-start.3 = (f32[512,256]{1,0:T(8,128)S(1)}, f32[512,256]{1,0:T(8,128)S(1)}, u32[]{:S(2)}, u32[]{:S(2)}) collective-permute-start(f32[512,256]{1,0:T(8,128)S(1)} %get-tuple-element.12.x_ref), channel_id=1, source_target_pairs={{3,0},{0,1},{1,2},{2,3},{7,4},{4,5},{5,6},{6,7},{11,8},{8,9},{9,10... | collective-permute-start | bytes 1572872 | tf_op jit(solution)/shard_map/ppermute | solution.py:304
  70.6 3.2 %collective-permute-start.2 = (f32[16,256]{1,0:T(8,128)S(1)}, f32[16,256]{1,0:T(8,128)S(1)}, u32[]{:S(2)}, u32[]{:S(2)}) collective-permute-start(f32[16,256]{1,0:T(8,128)S(1)} %shard_map.34.weights_ref), channel_id=1, source_target_pairs={{3,0},{0,1},{1,2},{2,3},{7,4},{4,5},{5,6},{6,7},{11,8},{8,9},{9,10... | collective-permute-start | bytes 49160 | tf_op jit(solution)/shard_map/ppermute | solution.py:304

commit v9 on v8

--- a/solution.py
+++ b/solution.py
@@ -32,6 +32,13 @@
     return high, middle, (rest - middle.astype(F32)).astype(BF16)
 
 
+def product(left, right, contracted):
+    (high, middle, _), (high_2, middle_2, _) = pieces(left), pieces(right)
+    dims = (((contracted,), (0,)), ((), ()))
+    pairs = ((high, middle_2), (middle, high_2), (high, high_2))
+    return sum(lax.dot_general(a, b, dims, preferred_element_type=F32) for a, b in pairs)
+
+
 def permuted(value, table):
     return sum(jnp.dot(part, table, preferred_element_type=F32) for part in pieces(value))
 
@@ -46,9 +53,7 @@
 
 def write_lines(x, words_ref, out_ref, moved_ref, lines_ref, sem):
     width = x.shape[1]
-    gram = lax.dot_general(
-        x, x, (((0,), (0,)), ((), ())), precision=lax.Precision.HIGHEST, preferred_element_type=F32
-    )
+    gram = product(x, x, 0)
     parts = pieces(gram)
     moved_ref[0] = gram
     for left in range(1, moved_ref.shape[0]):
@@ -244,7 +249,7 @@
     rotation = jnp.zeros(line.shape, F32)
     for i in range(WORDS):
         rotation += jnp.where(line == words_ref[i : i + 1, columns], weights_ref[i : i + 1, columns], 0.0)
-    return jnp.dot(x_ref[...], rotation, precision=lax.Precision.HIGHEST, preferred_element_type=F32)
+    return product(x_ref[...], rotation, 1)
 
 
 def first_kernel(words_ref, x_ref, out_ref, moved_ref, lines_ref, sem):

time: 89.6 us -> 88.1 us (0.983)
  Pallas kernels: 15.9 us -> 14 us
    pallas_call x2, Pallas kernels: 7.86 us -> 6.56 us  [call_with_lines(): pl.pallas_call(kernel, out_shape=[pltpu.HBM(sent, F32)] + [jax.ShapeDtype...]
where the time goes in v9:
time: 88.1 us; the launch traced here: 87.7 us
  waiting for transfers between devices  41.6 us (47%)
  starting transfers between devices  18.2 us (21%)
  Pallas kernels  14 us (16%)
  blocking collectives  13.7 us (16%)
    all_to_all x3, waiting for transfers between devices, exchanged(): return lax.all_to_all(value, axis, split_axis=0, concat_axis=0, tiled=True)  36.5 us
    all_to_all x3, starting transfers between devices, exchanged(): return lax.all_to_all(value, axis, split_axis=0, concat_axis=0, tiled=True)  18 us
    all_to_all x1, blocking collectives, exchanged(): return lax.all_to_all(value, axis, split_axis=0, concat_axis=0, tiled=True)  13.7 us
    pallas_call x2, Pallas kernels, call_with_lines(): pl.pallas_call(kernel, out_shape=[pltpu.HBM(sent, F32)] + [jax.ShapeDtype...  6.56 us
    ppermute x4, waiting for transfers between devices, passed_along(): return lax.ppermute(block, axis, route)  5.12 us
    pallas_call x6, Pallas kernels, call(): pl.pallas_call(kernel, out_shape=shapes[0] if single else shapes, scratch...  4.7 us
    pallas_call x1, Pallas kernels, sorted_rows_of(): pl.pallas_call(sort_kernel, out_shape=pltpu.HBM(shape, F32), in_specs=[pl...  1.86 us
  transfers between devices with their start and end apart: 7, of which 5 were waited for; matrix products, arithmetic and copies ran while one was open for 0% of the time, Pallas kernels for 5%

profile of v9, /device:TPU:8, one launch (start us, length us, event | category | flops | bytes accessed | tf_op | source)
XLA Modules:
  0.0 87.7 jit_solution(8555804409703954242)
XLA Ops:
  0.0 1.9 %shard_map.29 = f32[8,64,256]{2,1,0:T(8,128)} custom-call(f32[1024,128]{1,0:T(8,128)} %bitcast.8), custom_call_target="tpu_custom_call" | custom-call | tf_op jit(solution)/shard_map/pallas_call | solution.py:219
  1.9 0.0 copy-start
  1.9 6.0 %all-to-all-start = ((f32[8,64,256]{2,1,0:T(8,128)}), f32[8,64,256]{2,1,0:T(8,128)S(1)}, u32[]{:S(2)}, u32[]{:S(2)}) async-start(f32[8,64,256]{2,1,0:T(8,128)} %shard_map.29), calls=%async_computation | async-start | bytes 1048576 | tf_op jit(solution)/shard_map/all_to_all | solution.py:303
  7.9 0.0 copy-done
  7.9 0.8 shard_map.28
  8.7 10.1 %all-to-all-done = f32[8,64,256]{2,1,0:T(8,128)S(1)} async-done(((f32[8,64,256]{2,1,0:T(8,128)}), f32[8,64,256]{2,1,0:T(8,128)S(1)}, u32[]{:S(2)}, u32[]{:S(2)}) %all-to-all-start) | async-done | bytes 524320 | tf_op jit(solution)/shard_map/all_to_all | solution.py:303
  18.8 3.0 %shard_map.30 = f32[8,88,128]{2,1,0:T(8,128)} custom-call(s32[16,256]{1,0:T(8,128)S(1)} %get-tuple-element.10.words_ref, f32[512,256]{1,0:T(8,128)S(1)} %bitcast.4), custom_call_target="tpu_custom_call" | custom-call | tf_op jit(solution)/shard_map/pallas_call | solution.py:289
  21.8 8.5 %all-to-all-start.1 = ((f32[8,88,128]{2,1,0:T(8,128)}), f32[8,88,128]{2,1,0:T(8,128)S(1)}, u32[]{:S(2)}, u32[]{:S(2)}) async-start(f32[8,88,128]{2,1,0:T(8,128)} %shard_map.30), calls=%async_computation.1 | async-start | bytes 720896 | tf_op jit(solution)/shard_map/all_to_all | solution.py:303
  30.3 0.0 collective-permute-start.1
  30.3 13.0 %all-to-all-done.1.part_ref = f32[8,88,128]{2,1,0:T(8,128)S(1)} async-done(((f32[8,88,128]{2,1,0:T(8,128)}), f32[8,88,128]{2,1,0:T(8,128)S(1)}, u32[]{:S(2)}, u32[]{:S(2)}) %all-to-all-start.1) | async-done | bytes 360480 | tf_op jit(solution)/shard_map/all_to_all | solution.py:303
  43.4 1.1 %shard_map.31.weights_ref = f32[16,256]{1,0:T(8,128)S(1)} custom-call(s32[16,256]{1,0:T(8,128)S(1)} %get-tuple-element.10.words_ref, f32[8,88,128]{2,1,0:T(8,128)S(1)} %all-to-all-done.1.part_ref), custom_call_target="tpu_custom_call" | custom-call | tf_op jit(solution)/shard_map/pallas_call | solution.py:279
  44.5 0.1 collective-permute-start
  44.6 0.6 shard_map.32.top_ref
  45.1 0.0 collective-permute-done.1.x_ref
  45.1 2.6 %collective-permute-done.weights_ref = f32[16,256]{1,0:T(8,128)S(1)} collective-permute-done((f32[16,256]{1,0:T(8,128)S(1)}, f32[16,256]{1,0:T(8,128)S(1)}, u32[]{:S(2)}, u32[]{:S(2)}) %collective-permute-start) | collective-permute-done | bytes 16416 | tf_op jit(solution)/shard_map/ppermute | solution.py:309
  47.7 3.5 %shard_map.33 = (f32[8,88,128]{2,1,0:T(8,128)}, f32[512,256]{1,0:T(8,128)S(1)}) custom-call(s32[16,256]{1,0:T(8,128)S(1)} %get-tuple-element.10.words_ref, f32[16,256]{1,0:T(8,128)S(1)} %collective-permute-done.weights_ref, f32[512,256]{1,0:T(8,128)S(1)} %collective-permute-done.1.x_ref, f32[512,128]{1,0:T(8,128)S(1)} %shard_map.32.top_ref, ...), custom_call_target="tpu_custom_call" | custom-call | tf_op jit(solution)/shard_map/pallas_call | solution.py:289
  51.2 3.5 %all-to-all-start.2 = ((f32[8,88,128]{2,1,0:T(8,128)}), f32[8,88,128]{2,1,0:T(8,128)S(1)}, u32[]{:S(2)}, u32[]{:S(2)}) async-start(f32[8,88,128]{2,1,0:T(8,128)} %get-tuple-element.11), calls=%async_computation.2 | async-start | bytes 720896 | tf_op jit(solution)/shard_map/all_to_all | solution.py:303
  54.7 0.1 collective-permute-start.3
  54.8 13.4 %all-to-all-done.2.part_ref = f32[8,88,128]{2,1,0:T(8,128)S(1)} async-done(((f32[8,88,128]{2,1,0:T(8,128)}), f32[8,88,128]{2,1,0:T(8,128)S(1)}, u32[]{:S(2)}, u32[]{:S(2)}) %all-to-all-start.2) | async-done | bytes 360480 | tf_op jit(solution)/shard_map/all_to_all | solution.py:303
  68.2 1.1 %shard_map.34.weights_ref = f32[16,256]{1,0:T(8,128)S(1)} custom-call(s32[16,256]{1,0:T(8,128)S(1)} %get-tuple-element.9.next_words_ref.words_ref, f32[8,88,128]{2,1,0:T(8,128)S(1)} %all-to-all-done.2.part_ref), custom_call_target="tpu_custom_call" | custom-call | tf_op jit(solution)/shard_map/pallas_call | solution.py:279
  69.3 0.1 collective-permute-start.2
  69.4 0.6 shard_map.35.top_ref
  70.0 0.0 collective-permute-done.3.x_ref
  70.0 2.6 %collective-permute-done.2.weights_ref = f32[16,256]{1,0:T(8,128)S(1)} collective-permute-done((f32[16,256]{1,0:T(8,128)S(1)}, f32[16,256]{1,0:T(8,128)S(1)}, u32[]{:S(2)}, u32[]{:S(2)}) %collective-permute-start.2) | collective-permute-done | bytes 16416 | tf_op jit(solution)/shard_map/ppermute | solution.py:309
  72.6 0.6 shard_map.36
  73.1 13.7 %all_to_all.20.in_ref = f32[8,64,256]{2,1,0:T(8,128)S(1)} all-to-all(f32[8,64,256]{2,1,0:T(8,128)S(1)} %bitcast.7), channel_id=1, replica_groups=mesh['x'=4,'z'=8,'yh'=2,'cols'=4] {'x','yh'}, dimensions={0} | all-to-all | bytes 1048576 | tf_op jit(solution)/shard_map/all_to_all | solution.py:303
  86.8 0.9 shard_map.37
  (1 shorter events, 0.0 us)
Async XLA Ops:
  1.9 6.1 %copy-start = (s32[2,4,256]{2,1,0:T(4,128)S(1)}, s32[2,4,256]{2,1,0:T(4,128)}, u32[]{:S(2)}) copy-start(s32[2,4,256]{2,1,0:T(4,128)} %param.3) | copy-start | bytes 24580
  1.9 16.9 %all-to-all-start = ((f32[8,64,256]{2,1,0:T(8,128)}), f32[8,64,256]{2,1,0:T(8,128)S(1)}, u32[]{:S(2)}, u32[]{:S(2)}) async-start(f32[8,64,256]{2,1,0:T(8,128)} %shard_map.29), calls=%async_computation | async-start | bytes 1048576 | tf_op jit(solution)/shard_map/all_to_all | solution.py:303
  21.8 21.5 %all-to-all-start.1 = ((f32[8,88,128]{2,1,0:T(8,128)}), f32[8,88,128]{2,1,0:T(8,128)S(1)}, u32[]{:S(2)}, u32[]{:S(2)}) async-start(f32[8,88,128]{2,1,0:T(8,128)} %shard_map.30), calls=%async_computation.1 | async-start | bytes 720896 | tf_op jit(solution)/shard_map/all_to_all | solution.py:303
  30.3 14.8 %collective-permute-start.1 = (f32[512,256]{1,0:T(8,128)S(1)}, f32[512,256]{1,0:T(8,128)S(1)}, u32[]{:S(2)}, u32[]{:S(2)}) collective-permute-start(f32[512,256]{1,0:T(8,128)S(1)} %bitcast.5), channel_id=1, source_target_pairs={{3,0},{0,1},{1,2},{2,3},{7,4},{4,5},{5,6},{6,7},{11,8},{8,9},{9,10... | collective-permute-start | bytes 1572872 | tf_op jit(solution)/shard_map/ppermute | solution.py:309
  44.5 3.2 %collective-permute-start = (f32[16,256]{1,0:T(8,128)S(1)}, f32[16,256]{1,0:T(8,128)S(1)}, u32[]{:S(2)}, u32[]{:S(2)}) collective-permute-start(f32[16,256]{1,0:T(8,128)S(1)} %shard_map.31.weights_ref), channel_id=1, source_target_pairs={{3,0},{0,1},{1,2},{2,3},{7,4},{4,5},{5,6},{6,7},{11,8},{8,9},{9,10... | collective-permute-start | bytes 49160 | tf_op jit(solution)/shard_map/ppermute | solution.py:309
  51.2 17.0 %all-to-all-start.2 = ((f32[8,88,128]{2,1,0:T(8,128)}), f32[8,88,128]{2,1,0:T(8,128)S(1)}, u32[]{:S(2)}, u32[]{:S(2)}) async-start(f32[8,88,128]{2,1,0:T(8,128)} %get-tuple-element.11), calls=%async_computation.2 | async-start | bytes 720896 | tf_op jit(solution)/shard_map/all_to_all | solution.py:303
  54.7 15.3 %collective-permute-start.3 = (f32[512,256]{1,0:T(8,128)S(1)}, f32[512,256]{1,0:T(8,128)S(1)}, u32[]{:S(2)}, u32[]{:S(2)}) collective-permute-start(f32[512,256]{1,0:T(8,128)S(1)} %get-tuple-element.12.x_ref), channel_id=1, source_target_pairs={{3,0},{0,1},{1,2},{2,3},{7,4},{4,5},{5,6},{6,7},{11,8},{8,9},{9,10... | collective-permute-start | bytes 1572872 | tf_op jit(solution)/shard_map/ppermute | solution.py:309
  69.3 3.2 %collective-permute-start.2 = (f32[16,256]{1,0:T(8,128)S(1)}, f32[16,256]{1,0:T(8,128)S(1)}, u32[]{:S(2)}, u32[]{:S(2)}) collective-permute-start(f32[16,256]{1,0:T(8,128)S(1)} %shard_map.34.weights_ref), channel_id=1, source_target_pairs={{3,0},{0,1},{1,2},{2,3},{7,4},{4,5},{5,6},{6,7},{11,8},{8,9},{9,10... | collective-permute-start | bytes 49160 | tf_op jit(solution)/shard_map/ppermute | solution.py:309

commit v10 on v9

--- a/solution.py
+++ b/solution.py
@@ -13,7 +13,7 @@
 ROUNDS = 4
 WORDS = 1 << ROUNDS
 LINES = 44
-SENT = ((0, 24), (24, 64), (64, 88))
+SENT = ((0, 64), (64, 88))
 CHUNKS = 4
 VMEM_BYTES = 16 * 1024 * 1024
 F32 = jnp.float32
@@ -40,7 +40,9 @@
 
 
 def permuted(value, table):
-    return sum(jnp.dot(part, table, preferred_element_type=F32) for part in pieces(value))
+    rows = value.shape[0]
+    moved = jnp.dot(jnp.concatenate(pieces(value), axis=0), table, preferred_element_type=F32)
+    return moved[:rows] + moved[rows : 2 * rows] + moved[2 * rows :]
 
 
 def angle(orient, own, other, cross):
@@ -54,11 +56,12 @@
 def write_lines(x, words_ref, out_ref, moved_ref, lines_ref, sem):
     width = x.shape[1]
     gram = product(x, x, 0)
-    parts = pieces(gram)
+    stacked = jnp.concatenate(pieces(gram), axis=0)
     moved_ref[0] = gram
     for left in range(1, moved_ref.shape[0]):
         table = one_hot(words_ref[left : left + 1]).astype(BF16)
-        moved_ref[left] = sum(jnp.dot(part, table, preferred_element_type=F32) for part in parts)
+        moved = jnp.dot(stacked, table, preferred_element_type=F32)
+        moved_ref[left] = moved[:width] + moved[width : 2 * width] + moved[2 * width :]
     line = lax.broadcasted_iota(jnp.int32, (8, width), 0)
 
     def pick(word, count):
@@ -99,10 +102,8 @@
             place = place_of(number, right, right)
             store(place, jnp.where(first, loaded(place), same) if right % 2 else same)
             if number == 3 and right == 6:
-                send(1)
-        if number == 2:
-            send(0)
-    send(2)
+                send(0)
+    send(1)
     for copy in copies:
         copy.wait()
 
@@ -127,10 +128,9 @@
     for half in range(2):
         columns = slice(half * width // 2, (half + 1) * width // 2)
         lines_ref[:LINES, columns] = sum_ref[pl.ds(half, LINES, 2), :]
-    split = pieces(lines_ref[...])
     tables = [table_of(words_ref, number) for number in range(ROUNDS)]
     for number, table in enumerate(tables):
-        moved_ref[number] = sum(jnp.dot(part, table, preferred_element_type=F32) for part in split)
+        moved_ref[number] = permuted(lines_ref[...], table)
     indices = lax.broadcasted_iota(jnp.int32, (1, width), 1)
     state_ref[...] = jnp.zeros_like(state_ref)
     diag, diag_2 = lines_ref[:1], moved_ref[0, :1]

time: 88.1 us -> 87.3 us (level)
  transfers between devices with their start and end apart: 7 -> 7, of which waited for: 5 -> 5; matrix products, arithmetic and copies ran while one was open for 0% -> 0% of each run, Pallas kernels for 5% -> 4%
where the time goes in v10:
time: 87.3 us; the launch traced here: 86.8 us
  waiting for transfers between devices  41.6 us (48%)
  starting transfers between devices  18.2 us (21%)
  blocking collectives  13.7 us (16%)
  Pallas kernels  13.2 us (15%)
    all_to_all x3, waiting for transfers between devices, exchanged(): return lax.all_to_all(value, axis, split_axis=0, concat_axis=0, tiled=True)  36.5 us
    all_to_all x3, starting transfers between devices, exchanged(): return lax.all_to_all(value, axis, split_axis=0, concat_axis=0, tiled=True)  18 us
    all_to_all x1, blocking collectives, exchanged(): return lax.all_to_all(value, axis, split_axis=0, concat_axis=0, tiled=True)  13.7 us
    pallas_call x2, Pallas kernels, call_with_lines(): pl.pallas_call(kernel, out_shape=[pltpu.HBM(sent, F32)] + [jax.ShapeDtype...  6.18 us
    ppermute x4, waiting for transfers between devices, passed_along(): return lax.ppermute(block, axis, route)  5.12 us
    pallas_call x6, Pallas kernels, call(): pl.pallas_call(kernel, out_shape=shapes[0] if single else shapes, scratch...  4.27 us
    pallas_call x1, Pallas kernels, sorted_rows_of(): pl.pallas_call(sort_kernel, out_shape=pltpu.HBM(shape, F32), in_specs=[pl...  1.86 us
  transfers between devices with their start and end apart: 7, of which 5 were waited for; matrix products, arithmetic and copies ran while one was open for 0% of the time, Pallas kernels for 4%

profile of v10, /device:TPU:8, one launch (start us, length us, event | category | flops | bytes accessed | tf_op | source)
XLA Modules:
  0.0 86.8 jit_solution(9248027414941222331)
XLA Ops:
  0.0 1.9 %shard_map.29 = f32[8,64,256]{2,1,0:T(8,128)} custom-call(f32[1024,128]{1,0:T(8,128)} %bitcast.8), custom_call_target="tpu_custom_call" | custom-call | tf_op jit(solution)/shard_map/pallas_call | solution.py:219
  1.9 0.0 copy-start
  1.9 6.0 %all-to-all-start = ((f32[8,64,256]{2,1,0:T(8,128)}), f32[8,64,256]{2,1,0:T(8,128)S(1)}, u32[]{:S(2)}, u32[]{:S(2)}) async-start(f32[8,64,256]{2,1,0:T(8,128)} %shard_map.29), calls=%async_computation | async-start | bytes 1048576 | tf_op jit(solution)/shard_map/all_to_all | solution.py:303
  7.9 0.0 copy-done
  7.9 0.8 shard_map.28
  8.7 10.1 %all-to-all-done = f32[8,64,256]{2,1,0:T(8,128)S(1)} async-done(((f32[8,64,256]{2,1,0:T(8,128)}), f32[8,64,256]{2,1,0:T(8,128)S(1)}, u32[]{:S(2)}, u32[]{:S(2)}) %all-to-all-start) | async-done | bytes 524320 | tf_op jit(solution)/shard_map/all_to_all | solution.py:303
  18.8 2.9 %shard_map.30 = f32[8,88,128]{2,1,0:T(8,128)} custom-call(s32[16,256]{1,0:T(8,128)S(1)} %get-tuple-element.10.words_ref, f32[512,256]{1,0:T(8,128)S(1)} %bitcast.4), custom_call_target="tpu_custom_call" | custom-call | tf_op jit(solution)/shard_map/pallas_call | solution.py:289
  21.7 8.5 %all-to-all-start.1 = ((f32[8,88,128]{2,1,0:T(8,128)}), f32[8,88,128]{2,1,0:T(8,128)S(1)}, u32[]{:S(2)}, u32[]{:S(2)}) async-start(f32[8,88,128]{2,1,0:T(8,128)} %shard_map.30), calls=%async_computation.1 | async-start | bytes 720896 | tf_op jit(solution)/shard_map/all_to_all | solution.py:303
  30.2 0.0 collective-permute-start.1
  30.2 13.0 %all-to-all-done.1.part_ref = f32[8,88,128]{2,1,0:T(8,128)S(1)} async-done(((f32[8,88,128]{2,1,0:T(8,128)}), f32[8,88,128]{2,1,0:T(8,128)S(1)}, u32[]{:S(2)}, u32[]{:S(2)}) %all-to-all-start.1) | async-done | bytes 360480 | tf_op jit(solution)/shard_map/all_to_all | solution.py:303
  43.2 0.9 %shard_map.31.weights_ref = f32[16,256]{1,0:T(8,128)S(1)} custom-call(s32[16,256]{1,0:T(8,128)S(1)} %get-tuple-element.10.words_ref, f32[8,88,128]{2,1,0:T(8,128)S(1)} %all-to-all-done.1.part_ref), custom_call_target="tpu_custom_call" | custom-call | tf_op jit(solution)/shard_map/pallas_call | solution.py:279
  44.1 0.1 collective-permute-start
  44.2 0.6 shard_map.32.top_ref
  44.8 0.0 collective-permute-done.1.x_ref
  44.8 2.6 %collective-permute-done.weights_ref = f32[16,256]{1,0:T(8,128)S(1)} collective-permute-done((f32[16,256]{1,0:T(8,128)S(1)}, f32[16,256]{1,0:T(8,128)S(1)}, u32[]{:S(2)}, u32[]{:S(2)}) %collective-permute-start) | collective-permute-done | bytes 16416 | tf_op jit(solution)/shard_map/ppermute | solution.py:309
  47.3 3.3 %shard_map.33 = (f32[8,88,128]{2,1,0:T(8,128)}, f32[512,256]{1,0:T(8,128)S(1)}) custom-call(s32[16,256]{1,0:T(8,128)S(1)} %get-tuple-element.10.words_ref, f32[16,256]{1,0:T(8,128)S(1)} %collective-permute-done.weights_ref, f32[512,256]{1,0:T(8,128)S(1)} %collective-permute-done.1.x_ref, f32[512,128]{1,0:T(8,128)S(1)} %shard_map.32.top_ref, ...), custom_call_target="tpu_custom_call" | custom-call | tf_op jit(solution)/shard_map/pallas_call | solution.py:289
  50.6 3.5 %all-to-all-start.2 = ((f32[8,88,128]{2,1,0:T(8,128)}), f32[8,88,128]{2,1,0:T(8,128)S(1)}, u32[]{:S(2)}, u32[]{:S(2)}) async-start(f32[8,88,128]{2,1,0:T(8,128)} %get-tuple-element.11), calls=%async_computation.2 | async-start | bytes 720896 | tf_op jit(solution)/shard_map/all_to_all | solution.py:303
  54.1 0.1 collective-permute-start.3
  54.2 13.4 %all-to-all-done.2.part_ref = f32[8,88,128]{2,1,0:T(8,128)S(1)} async-done(((f32[8,88,128]{2,1,0:T(8,128)}), f32[8,88,128]{2,1,0:T(8,128)S(1)}, u32[]{:S(2)}, u32[]{:S(2)}) %all-to-all-start.2) | async-done | bytes 360480 | tf_op jit(solution)/shard_map/all_to_all | solution.py:303
  67.6 0.9 %shard_map.34.weights_ref = f32[16,256]{1,0:T(8,128)S(1)} custom-call(s32[16,256]{1,0:T(8,128)S(1)} %get-tuple-element.9.next_words_ref.words_ref, f32[8,88,128]{2,1,0:T(8,128)S(1)} %all-to-all-done.2.part_ref), custom_call_target="tpu_custom_call" | custom-call | tf_op jit(solution)/shard_map/pallas_call | solution.py:279
  68.5 0.1 collective-permute-start.2
  68.6 0.6 shard_map.35.top_ref
  69.2 0.0 collective-permute-done.3.x_ref
  69.2 2.6 %collective-permute-done.2.weights_ref = f32[16,256]{1,0:T(8,128)S(1)} collective-permute-done((f32[16,256]{1,0:T(8,128)S(1)}, f32[16,256]{1,0:T(8,128)S(1)}, u32[]{:S(2)}, u32[]{:S(2)}) %collective-permute-start.2) | collective-permute-done | bytes 16416 | tf_op jit(solution)/shard_map/ppermute | solution.py:309
  71.7 0.6 shard_map.36
  72.3 13.7 %all_to_all.20.in_ref = f32[8,64,256]{2,1,0:T(8,128)S(1)} all-to-all(f32[8,64,256]{2,1,0:T(8,128)S(1)} %bitcast.7), channel_id=1, replica_groups=mesh['x'=4,'z'=8,'yh'=2,'cols'=4] {'x','yh'}, dimensions={0} | all-to-all | bytes 1048576 | tf_op jit(solution)/shard_map/all_to_all | solution.py:303
  86.0 0.9 shard_map.37
  (1 shorter events, 0.0 us)
Async XLA Ops:
  1.9 6.1 %copy-start = (s32[2,4,256]{2,1,0:T(4,128)S(1)}, s32[2,4,256]{2,1,0:T(4,128)}, u32[]{:S(2)}) copy-start(s32[2,4,256]{2,1,0:T(4,128)} %param.3) | copy-start | bytes 24580
  1.9 16.9 %all-to-all-start = ((f32[8,64,256]{2,1,0:T(8,128)}), f32[8,64,256]{2,1,0:T(8,128)S(1)}, u32[]{:S(2)}, u32[]{:S(2)}) async-start(f32[8,64,256]{2,1,0:T(8,128)} %shard_map.29), calls=%async_computation | async-start | bytes 1048576 | tf_op jit(solution)/shard_map/all_to_all | solution.py:303
  21.7 21.5 %all-to-all-start.1 = ((f32[8,88,128]{2,1,0:T(8,128)}), f32[8,88,128]{2,1,0:T(8,128)S(1)}, u32[]{:S(2)}, u32[]{:S(2)}) async-start(f32[8,88,128]{2,1,0:T(8,128)} %shard_map.30), calls=%async_computation.1 | async-start | bytes 720896 | tf_op jit(solution)/shard_map/all_to_all | solution.py:303
  30.2 14.6 %collective-permute-start.1 = (f32[512,256]{1,0:T(8,128)S(1)}, f32[512,256]{1,0:T(8,128)S(1)}, u32[]{:S(2)}, u32[]{:S(2)}) collective-permute-start(f32[512,256]{1,0:T(8,128)S(1)} %bitcast.5), channel_id=1, source_target_pairs={{3,0},{0,1},{1,2},{2,3},{7,4},{4,5},{5,6},{6,7},{11,8},{8,9},{9,10... | collective-permute-start | bytes 1572872 | tf_op jit(solution)/shard_map/ppermute | solution.py:309
  44.1 3.2 %collective-permute-start = (f32[16,256]{1,0:T(8,128)S(1)}, f32[16,256]{1,0:T(8,128)S(1)}, u32[]{:S(2)}, u32[]{:S(2)}) collective-permute-start(f32[16,256]{1,0:T(8,128)S(1)} %shard_map.31.weights_ref), channel_id=1, source_target_pairs={{3,0},{0,1},{1,2},{2,3},{7,4},{4,5},{5,6},{6,7},{11,8},{8,9},{9,10... | collective-permute-start | bytes 49160 | tf_op jit(solution)/shard_map/ppermute | solution.py:309
  50.6 17.0 %all-to-all-start.2 = ((f32[8,88,128]{2,1,0:T(8,128)}), f32[8,88,128]{2,1,0:T(8,128)S(1)}, u32[]{:S(2)}, u32[]{:S(2)}) async-start(f32[8,88,128]{2,1,0:T(8,128)} %get-tuple-element.11), calls=%async_computation.2 | async-start | bytes 720896 | tf_op jit(solution)/shard_map/all_to_all | solution.py:303
  54.1 15.1 %collective-permute-start.3 = (f32[512,256]{1,0:T(8,128)S(1)}, f32[512,256]{1,0:T(8,128)S(1)}, u32[]{:S(2)}, u32[]{:S(2)}) collective-permute-start(f32[512,256]{1,0:T(8,128)S(1)} %get-tuple-element.12.x_ref), channel_id=1, source_target_pairs={{3,0},{0,1},{1,2},{2,3},{7,4},{4,5},{5,6},{6,7},{11,8},{8,9},{9,10... | collective-permute-start | bytes 1572872 | tf_op jit(solution)/shard_map/ppermute | solution.py:309
  68.5 3.2 %collective-permute-start.2 = (f32[16,256]{1,0:T(8,128)S(1)}, f32[16,256]{1,0:T(8,128)S(1)}, u32[]{:S(2)}, u32[]{:S(2)}) collective-permute-start(f32[16,256]{1,0:T(8,128)S(1)} %shard_map.34.weights_ref), channel_id=1, source_target_pairs={{3,0},{0,1},{1,2},{2,3},{7,4},{4,5},{5,6},{6,7},{11,8},{8,9},{9,10... | collective-permute-start | bytes 49160 | tf_op jit(solution)/shard_map/ppermute | solution.py:309
